TPU v7x, 32 devices: a whole 2x2x4 slice. The times are simulated.
32 devices in a mesh: tm: 8 (over z, y), series: 4 (over x, core).
Axes of the slice: x: 2, y: 2, z: 4, core: 2. Of those that a mesh axis runs over, the one named last changes fastest.
Arguments:
- returns: float32 [2048, 8192], P('tm', 'series'), may hold values from -40 to 40
- sector: int32 [8192], P('series'), may hold values from 0 to 511, as said below
Outputs:
- shrunk_variance: float32 [2048, 8192], P('tm', 'series')
Inputs may be any that keep to these rules, and one draw needn't show every extreme that they name: `sector`: sectors differ widely in size; some sectors may hold no series.
All inputs are finite; a program needn't handle non-finite values.
Results may differ from a plain program's by a relative error of at most 0.0003.
Values sent between devices are 32-bit elements; how exact they have to be, the bound alone decides.
No kernel may reach another device: no remote copies, remote signals or barrier semaphores. Data moves between devices by JAX's collectives and lax.ppermute only.
A program may use at most 64 MiB of HBM per device.

v0:
```python
import jax
import jax.numpy as jnp
from jax import lax
from jax.sharding import PartitionSpec as P

W = 64
SECTORS = 512


ridge_rate = 0.05
shrink_weight = 0.3
highest = lax.Precision.HIGHEST


def shifted(value, axis, steps):
    count = lax.axis_size(axis)
    leading, last = (max(0, -steps), min(count, count - steps))
    return lax.ppermute(value, axis, [(source, source + steps) for source in range(leading, last)])


def sector_table(sector):
    labels = jnp.arange(SECTORS, dtype=jnp.int32)
    return (sector[:, None] == labels[None, :]).astype(jnp.float32)


def band_matrix(rows):
    row_pos = jnp.arange(rows, dtype=jnp.int32)[:, None]
    col_pos = jnp.arange(rows + W - 1, dtype=jnp.int32)[None, :]
    return ((col_pos >= row_pos) & (col_pos < row_pos + W)).astype(jnp.float32)


def window_variance(ext_returns, ext_factor, first_step):
    rows = ext_returns.shape[0] - (W - 1)
    series_width = ext_returns.shape[1]
    stacked = jnp.concatenate(
        [
            ext_returns,
            ext_factor,
            ext_returns * ext_returns,
            ext_factor * ext_factor,
            ext_returns * ext_factor,
        ],
        axis=1,
    )
    moments = jnp.dot(
        band_matrix(rows), stacked, precision=highest, preferred_element_type=jnp.float32
    )
    sum_ret = moments[:, :series_width]
    sum_fac = moments[:, series_width : 2 * series_width]
    sum_rr = moments[:, 2 * series_width : 3 * series_width]
    sum_ff = moments[:, 3 * series_width : 4 * series_width]
    sum_rf = moments[:, 4 * series_width :]
    steps_seen = jnp.minimum(first_step + jnp.arange(rows, dtype=jnp.int32) + 1, W).astype(
        jnp.float32
    )[:, None]
    centred_rr = sum_rr - sum_ret * sum_ret / steps_seen
    centred_ff = sum_ff - sum_fac * sum_fac / steps_seen
    centred_rf = sum_rf - sum_ret * sum_fac / steps_seen
    return (
        centred_rr - centred_rf * centred_rf / (centred_ff + ridge_rate * steps_seen)
    ) / steps_seen


def local(returns, sector):
    time_rows = returns.shape[0]
    table = sector_table(sector)
    part_sums = jnp.dot(returns, table, precision=highest, preferred_element_type=jnp.float32)
    part_counts = jnp.sum(table, axis=0)
    sums, counts = lax.psum((part_sums, part_counts), "series")
    means = sums / jnp.maximum(counts, 1.0)[None, :]
    factor = jnp.dot(means, table.T, precision=highest, preferred_element_type=jnp.float32)
    prior_ret, prior_fac = shifted(
        (returns[time_rows - (W - 1) :], factor[time_rows - (W - 1) :]), "tm", 1
    )
    ext_returns = jnp.concatenate([prior_ret, returns], axis=0)
    ext_factor = jnp.concatenate([prior_fac, factor], axis=0)
    first_step = lax.axis_index("tm") * time_rows
    variance = window_variance(ext_returns, ext_factor, first_step)
    part_totals = jnp.dot(
        jnp.sum(variance, axis=0)[None, :],
        table,
        precision=highest,
        preferred_element_type=jnp.float32,
    )[0]
    series_totals = lax.psum(part_totals, "series")
    totals = lax.psum(series_totals, "tm")
    all_steps = time_rows * lax.axis_size("tm")
    sector_mean = totals / (all_steps * jnp.maximum(counts, 1.0))
    pooled = jnp.dot(
        sector_mean[None, :], table.T, precision=highest, preferred_element_type=jnp.float32
    )
    return (1.0 - shrink_weight) * variance + shrink_weight * pooled


def solution(mesh):
    placed = (P("tm", "series"), P("series"))
    return jax.shard_map(
        local, mesh=mesh, in_specs=placed, out_specs=P("tm", "series"), check_vma=False
    )
```

profile of v0, /device:TPU:0, one launch (start us, length us, event | category | flops | bytes accessed | tf_op | source)
XLA Modules:
  0.0 131.1 jit_solution(16794404465955598857)
XLA Ops:
  6.5 0.0 copy-start.3
  6.5 0.0 copy-start
  6.5 0.0 all-reduce.2.cloned.1.call-start
  6.5 5.3 %fusion.17 = f32[256,512]{0,1:T(8,128)} fusion(f32[256,2048]{1,0:T(8,128)} %param.2, s32[2048]{0:T(1024)} %param.3), kind=kOutput, calls=%fused_computation.27 | convolution fusion | flops 3223322624 | bytes 2629632 | tf_op jit(solution)/shard_map/dot_general | solution.py:67
  11.9 0.0 all-reduce.2.cloned.1.call-update
  11.9 0.0 copy-done
  11.9 0.8 slice.21
  12.7 4.9 %collective-permute-start = (f32[63,2048]{1,0:T(8,128)}, f32[63,2048]{1,0:T(8,128)S(1)}, u32[]{:S(2)}, u32[]{:S(2)}) collective-permute-start(f32[63,2048]{1,0:T(8,128)} %slice.21), channel_id=1, source_target_pairs={{0,4},{4,8},{8,12},{12,16},{16,20},{20,24},{24,28},{1,5},{5,9},{9,... | collective-permute-start | bytes 1548296 | tf_op jit(solution)/shard_map/ppermute | solution.py:18
  17.7 0.0 copy-done.3
  17.7 0.6 convert_reduce_fusion
  18.3 6.8 %psum.29 = f32[512]{0:T(512)S(1)} all-reduce(f32[512]{0:T(512)S(1)} %convert_reduce_fusion), channel_id=1, replica_groups=mesh['tm'=8,'series'=4] {'series'}, use_global_device_ids=true, to_apply=%region_2.0 | all-reduce | flops 512 | bytes 4096 | tf_op jit(solution)/shard_map/psum | solution.py:69
  25.0 23.2 %all-reduce.2.cloned.1.call-done = f32[256,512]{0,1:T(8,128)} async-done(((f32[256,512]{0,1:T(8,128)}), f32[256,512]{0,1:T(8,128)}) %all-reduce.2.cloned.1.call-update) | async-done | bytes 524304 | tf_op jit(solution)/shard_map/psum | solution.py:69
  48.2 5.0 %fusion.2 = f32[256,2048]{1,0:T(8,128)S(1)} fusion(s32[2048]{0:T(1024)S(1)} %copy-done.3, f32[256,512]{0,1:T(8,128)} %all-reduce.2.cloned.1.call-done, f32[512]{0:T(512)S(1)} %broadcast_maximum_fusion), kind=kOutput, calls=%fused_computation.4 | convolution fusion | flops 3222405120 | bytes 2631680 | tf_op jit(solution)/shard_map/dot_general | solution.py:71
  53.2 0.0 copy-start.1
  53.2 1.3 copy-done.1
  54.5 0.9 slice.28
  55.4 3.6 %collective-permute-start.1 = (f32[63,2048]{1,0:T(8,128)}, f32[63,2048]{1,0:T(8,128)S(1)}, u32[]{:S(2)}, u32[]{:S(2)}) collective-permute-start(f32[63,2048]{1,0:T(8,128)} %slice.28), channel_id=1, source_target_pairs={{0,4},{4,8},{8,12},{12,16},{16,20},{20,24},{24,28},{1,5},{5,9},{9,... | collective-permute-start | bytes 1548296 | tf_op jit(solution)/shard_map/ppermute | solution.py:18
  59.0 0.0 copy-start.2
  59.1 0.0 collective-permute-done
  59.1 1.9 %fusion.15 = f32[319,10240]{1,0:T(8,128)} fusion(f32[256,2048]{1,0:T(8,128)S(1)} %copy-done, f32[63,2048]{1,0:T(8,128)S(1)} %collective-permute-done), kind=kLoop, calls=%fused_computation.25 | loop fusion | flops 653311 | bytes 5234688
  60.9 8.4 %collective-permute-done.1 = f32[63,2048]{1,0:T(8,128)S(1)} collective-permute-done((f32[63,2048]{1,0:T(8,128)}, f32[63,2048]{1,0:T(8,128)S(1)}, u32[]{:S(2)}, u32[]{:S(2)}) %collective-permute-start.1) | collective-permute-done | bytes 516128 | tf_op jit(solution)/shard_map/ppermute | solution.py:18
  69.3 0.0 copy-done.2
  69.3 1.9 %fusion.16 = f32[319,10240]{1,0:T(8,128)} fusion(f32[319,10240]{1,0:T(8,128)} %fusion.15, f32[256,2048]{1,0:T(8,128)S(1)} %copy-done.2, f32[63,2048]{1,0:T(8,128)S(1)} %collective-permute-done.1), kind=kLoop, calls=%fused_computation.26 | loop fusion | flops 653312 | bytes 5234688
  71.2 1.9 %multiply_dynamic-update-slice_fusion.2 = f32[319,10240]{1,0:T(8,128)} fusion(f32[319,10240]{1,0:T(8,128)} %fusion.16, f32[256,2048]{1,0:T(8,128)S(1)} %copy-done, f32[63,2048]{1,0:T(8,128)S(1)} %collective-permute-done), kind=kLoop, calls=%fused_computation.10 | loop fusion | flops 1306624 | bytes 5234688
  73.1 1.9 %multiply_dynamic-update-slice_fusion.1 = f32[319,10240]{1,0:T(8,128)} fusion(f32[319,10240]{1,0:T(8,128)} %multiply_dynamic-update-slice_fusion.2, f32[256,2048]{1,0:T(8,128)S(1)} %copy-done.2, f32[63,2048]{1,0:T(8,128)S(1)} %collective-permute-done.1), kind=kLoop, calls=%fused_computation.9 | loop fusion | flops 1306624 | bytes 5234688
  75.0 2.1 %multiply_dynamic-update-slice_fusion = f32[319,10240]{1,0:T(8,128)} fusion(f32[319,10240]{1,0:T(8,128)} %multiply_dynamic-update-slice_fusion.1, f32[256,2048]{1,0:T(8,128)S(1)} %copy-done, f32[63,2048]{1,0:T(8,128)S(1)} %collective-permute-done, f32[256,2048]{1,0:T(8,128)S(1)} %copy-done.2, f32[63,2048]{1,0:T(8,128)S(1)} %collective-permute-done.1), kind=kLoop, calls=%fused_computation.8 | loop fusion | flops 1959936 | bytes 7847936 | tf_op jit(solution)/shard_map/concatenate | solution.py:35
  77.1 12.4 %fusion.22 = f32[256,10240]{1,0:T(8,128)S(1)} fusion(f32[319,10240]{1,0:T(8,128)} %multiply_dynamic-update-slice_fusion, s32[256]{0:T(256)S(1)} %iota_add_fusion), kind=kOutput, calls=%fused_computation.32 | convolution fusion | flops 10035117056 | bytes 23553024 | tf_op jit(solution)/shard_map/dot_general | solution.py:45
  89.5 1.6 %fusion.26 = (f32[2048]{0:T(1024)S(1)}, f32[256,2048]{1,0:T(8,128)S(1)}) fusion(f32[256]{0:T(256)S(1)} %broadcast_multiply_fusion.1, f32[256,10240]{1,0:T(8,128)S(1)} %fusion.22, f32[256]{0:T(256)S(1)} %minimum_convert_fusion), kind=kLoop, calls=%fused_computation.41 | loop fusion | flops 7862272 | bytes 12593152 | tf_op jit(solution)/shard_map/reduce_sum | solution.py:80
  91.1 1.4 %fusion.1 = f32[1,512]{1,0:T(1,128)S(1)} fusion(f32[2048,1]{0,1:T(1,128)S(1)} %bitcast.10, s32[2048]{0:T(1024)S(1)} %copy-done.3), kind=kOutput, calls=%fused_computation.3 | convolution fusion | flops 13631488 | bytes 18432 | tf_op jit(solution)/shard_map/dot_general | solution.py:79
  92.5 5.6 %psum.30 = f32[512]{0:T(512)S(1)} all-reduce(f32[512]{0:T(512)S(1)} %bitcast.13), channel_id=1, replica_groups=mesh['tm'=8,'series'=4] {'series'}, use_global_device_ids=true, to_apply=%region_4.0 | all-reduce | flops 512 | bytes 4096 | tf_op jit(solution)/shard_map/psum | solution.py:85
  98.2 22.2 %psum.31 = f32[512]{0:T(512)S(1)} all-reduce(f32[512]{0:T(512)S(1)} %psum.30), channel_id=1, replica_groups=mesh['tm'=8,'series'=4] {'tm'}, use_global_device_ids=true, to_apply=%region_5.0 | all-reduce | flops 512 | bytes 4096 | tf_op jit(solution)/shard_map/psum | solution.py:86
  120.4 2.2 %fusion = f32[1,2048]{1,0:T(1,128)S(1)} fusion(f32[512,1]{0,1:T(1,128)S(1)} %bitcast.12, s32[2048]{0:T(1024)S(1)} %copy-done.3), kind=kOutput, calls=%fused_computation.2 | convolution fusion | flops 13631488 | bytes 18432 | tf_op jit(solution)/shard_map/dot_general | solution.py:89
  122.6 1.6 %multiply_add_fusion = f32[256,2048]{1,0:T(8,128)} fusion(f32[256,2048]{1,0:T(8,128)S(1)} %get-tuple-element.6, f32[2048]{0:T(1024)S(1)} %broadcast_multiply_fusion), kind=kLoop, calls=%fused_computation.20 | loop fusion | flops 1048576 | bytes 4202496 | tf_op jit(solution)/shard_map/add | solution.py:92
  (6 shorter events, 0.0 us)
Async XLA Ops:
  6.5 11.1 %copy-start.3 = (s32[2048]{0:T(1024)S(1)}, s32[2048]{0:T(1024)}, u32[]{:S(2)}) copy-start(s32[2048]{0:T(1024)} %param.3) | copy-start | bytes 24580
  6.5 5.4 %copy-start = (f32[256,2048]{1,0:T(8,128)S(1)}, f32[256,2048]{1,0:T(8,128)}, u32[]{:S(2)}) copy-start(f32[256,2048]{1,0:T(8,128)} %param.2) | copy-start | bytes 6291460
  6.5 41.7 %all-reduce.2.cloned.1.call-start = ((), (), s32[]{:S(2)}) async-start(), calls=%async_computation | async-start | bytes 1048576 | tf_op jit(solution)/shard_map/psum | solution.py:69
  12.7 46.3 %collective-permute-start = (f32[63,2048]{1,0:T(8,128)}, f32[63,2048]{1,0:T(8,128)S(1)}, u32[]{:S(2)}, u32[]{:S(2)}) collective-permute-start(f32[63,2048]{1,0:T(8,128)} %slice.21), channel_id=1, source_target_pairs={{0,4},{4,8},{8,12},{12,16},{16,20},{20,24},{24,28},{1,5},{5,9},{9,... | collective-permute-start | bytes 1548296 | tf_op jit(solution)/shard_map/ppermute | solution.py:18
  53.2 1.3 %copy-start.1 = (f32[256,2048]{1,0:T(8,128)}, f32[256,2048]{1,0:T(8,128)S(1)}, u32[]{:S(2)}) copy-start(f32[256,2048]{1,0:T(8,128)S(1)} %fusion.2) | copy-start | bytes 6291460
  55.4 13.9 %collective-permute-start.1 = (f32[63,2048]{1,0:T(8,128)}, f32[63,2048]{1,0:T(8,128)S(1)}, u32[]{:S(2)}, u32[]{:S(2)}) collective-permute-start(f32[63,2048]{1,0:T(8,128)} %slice.28), channel_id=1, source_target_pairs={{0,4},{4,8},{8,12},{12,16},{16,20},{20,24},{24,28},{1,5},{5,9},{9,... | collective-permute-start | bytes 1548296 | tf_op jit(solution)/shard_map/ppermute | solution.py:18
  59.0 10.3 %copy-start.2 = (f32[256,2048]{1,0:T(8,128)S(1)}, f32[256,2048]{1,0:T(8,128)}, u32[]{:S(2)}) copy-start(f32[256,2048]{1,0:T(8,128)} %copy-done.1) | copy-start | bytes 6291460
Sparse Core Ops, SparseCore 0:
  12.0 36.1 all-reduce.1
where the time goes:
time: 131 us
  blocking collectives  34.6 us (26%)
  waiting for transfers between devices  31.6 us (24%)
  matrix products  26.3 us (20%)
  other arithmetic  13.5 us (10%)
  between operations  13.5 us (10%)
  starting transfers between devices  8.5 us (6%)
  local copies, waits for them, and re-layouts  3.04 us (2%)
    psum x1, waiting for transfers between devices, local(): sums, counts = lax.psum((part_sums, part_counts), 'series')  23.2 us
    psum x1, blocking collectives, local(): totals = lax.psum(series_totals, 'tm')  22.2 us
    dot_general x1, matrix products, window_variance(): jnp.dot(band_matrix(rows), stacked, precision=highest, preferred_element_...  12.4 us
    ppermute x2, starting transfers between devices, shifted(): lax.ppermute(value, axis, [(source, source + steps) for source in range(l...  8.49 us
    ppermute x2, waiting for transfers between devices, shifted(): lax.ppermute(value, axis, [(source, source + steps) for source in range(l...  8.4 us
    unnamed x4, other arithmetic  7.57 us
    psum x1, blocking collectives, local(): sums, counts = lax.psum((part_sums, part_counts), 'series')  6.75 us
    psum x1, blocking collectives, local(): series_totals = lax.psum(part_totals, 'series')  5.64 us
  transfers between devices with their start and end apart: 3, of which 2 were waited for; matrix products, arithmetic and copies ran while one was open for 7% of the time, Pallas kernels for 0%

commit v1 on v0

v1 whole, which is shorter than its diff:
```python
import functools

import jax
import jax.numpy as jnp
from jax import lax
from jax.experimental import pallas as pl
from jax.experimental.pallas import tpu as pltpu
from jax.sharding import PartitionSpec as P

W = 64
SECTORS = 512
HALF = SECTORS // 2
LANES = 128

ridge_rate = 0.05
shrink_weight = 0.3

f32 = jnp.float32
bf16 = jnp.bfloat16
MIB = 1024 * 1024


def dot_nn(a, b):
    return lax.dot_general(a, b, (((1,), (0,)), ((), ())), preferred_element_type=f32)


def dot_nt(a, b):
    return lax.dot_general(a, b, (((1,), (1,)), ((), ())), preferred_element_type=f32)


def split2(x):
    hi = x.astype(bf16)
    return hi, (x - hi.astype(f32)).astype(bf16)


def split3_rows(x):
    hi = x.astype(bf16).astype(f32)
    rest = x - hi
    mid = rest.astype(bf16).astype(f32)
    low = rest - mid
    row = lax.broadcasted_iota(jnp.int32, (16, x.shape[1]), 0)
    return jnp.where(row == 0, hi, jnp.where(row == 1, mid, jnp.where(row == 2, low, 0.0))).astype(bf16)


def window(x):
    size = 1
    while size < W:
        x = x + pltpu.roll(x, size, 0)
        size *= 2
    return x[W:]


def sums_kernel(core_ref, ret_ref, sec_ref, keep_ref, send_ref, table_ref, tail_ref, hi_ref, lo_ref):
    rows = ret_ref.shape[0]
    core = core_ref[0]
    label = lax.broadcasted_iota(jnp.int32, table_ref.shape, 0)
    label = (label + core * HALF) & (SECTORS - 1)
    table_ref[...] = jnp.where(label == sec_ref[...], 1.0, 0.0).astype(bf16)
    value = ret_ref[...]
    hi, lo = split2(value)
    hi_ref[:rows] = hi
    lo_ref[:rows] = lo
    hi_ref[rows:] = jnp.ones_like(hi_ref[rows:])
    lo_ref[rows:] = jnp.zeros_like(lo_ref[rows:])
    tail_ref[...] = ret_ref[rows - W :]
    acc = dot_nt(hi_ref[...], table_ref[...]) + dot_nt(lo_ref[...], table_ref[...])
    keep_ref[...] = acc[: rows + 8, :HALF]
    send_ref[...] = acc[: rows + 8, HALF:]


def sector_sums(core, returns, sector):
    rows, width = returns.shape
    half = jax.ShapeDtypeStruct((rows + 8, HALF), f32)
    return pl.pallas_call(
        sums_kernel,
        out_shape=(
            half,
            half,
            jax.ShapeDtypeStruct((SECTORS, width), bf16),
            jax.ShapeDtypeStruct((W, width), f32),
        ),
        in_specs=[
            pl.BlockSpec(memory_space=pltpu.SMEM),
            pl.BlockSpec(memory_space=pltpu.VMEM),
            pl.BlockSpec(memory_space=pltpu.VMEM),
        ],
        out_specs=[pl.BlockSpec(memory_space=pltpu.VMEM)] * 4,
        scratch_shapes=[pltpu.VMEM((rows + 16, width), bf16)] * 2,
        compiler_params=pltpu.CompilerParams(vmem_limit_bytes=24 * MIB),
        cost_estimate=pl.CostEstimate(
            flops=4 * rows * width * SECTORS, bytes_accessed=8 * rows * width, transcendentals=0
        ),
        name="sector_sums",
    )(core, returns, sector)


def variance_kernel(
    info_ref, own_ref, other_ref, hown_ref, hother_ref, halo_ref, ret_ref, table_ref,
    var_ref, totals_ref, hi_ref, lo_ref, steps_ref, acc_ref,
):
    rows = ret_ref.shape[0]
    ext = rows + W
    step = pl.program_id(0)
    core, first_step = info_ref[0], info_ref[1]

    @pl.when(step == 0)
    def _():
        position = lax.broadcasted_iota(jnp.int32, (rows, LANES), 0) + (first_step + 1)
        inv = 1.0 / jnp.minimum(position, W).astype(f32)
        steps_ref[...] = inv
        for tile in range(SECTORS // LANES):
            here, prior = (own_ref, hown_ref) if tile < HALF // LANES else (other_ref, hother_ref)
            cols = pl.ds((tile * LANES) % HALF, LANES)
            count = jnp.maximum(here[rows : rows + 1, cols], 1.0)
            mean = jnp.concatenate([prior[:, cols], here[:rows, cols]], axis=0) / count
            mean_f = window(mean) * inv
            cff = window(mean * mean) * inv - mean_f * mean_f
            gain = 1.0 / (cff + ridge_rate)
            out = pl.ds(tile * LANES, LANES)
            for start, part in ((0, mean), (ext, mean_f), (ext + rows, gain)):
                hi, lo = split2(part)
                hi_ref[start : start + part.shape[0], out] = hi
                lo_ref[start : start + part.shape[0], out] = lo
        acc_ref[...] = jnp.zeros_like(acc_ref)

    inv = steps_ref[...]
    spread = dot_nn(hi_ref[...], table_ref[...]) + dot_nn(lo_ref[...], table_ref[...])
    column_sums = []
    for tile in range(ret_ref.shape[1] // LANES):
        cols = slice(tile * LANES, (tile + 1) * LANES)
        ret = jnp.concatenate([halo_ref[:, cols], ret_ref[:, cols]], axis=0)
        factor = spread[:ext, cols]
        mean_f = spread[ext : ext + rows, cols]
        gain = spread[ext + rows :, cols]
        mean_r = window(ret) * inv
        crr = window(ret * ret) * inv - mean_r * mean_r
        crf = window(ret * factor) * inv - mean_r * mean_f
        variance = crr - crf * crf * gain
        var_ref[:, cols] = (1.0 - shrink_weight) * variance
        column_sums.append(jnp.sum(variance, axis=0, keepdims=True))
    acc_ref[...] += dot_nt(split3_rows(jnp.concatenate(column_sums, axis=1)), table_ref[...])

    @pl.when(step == pl.num_programs(0) - 1)
    def _():
        total = jnp.sum(acc_ref[...], axis=0, keepdims=True)
        swapped = jnp.concatenate([total[:, HALF:], total[:, :HALF]], axis=1)
        total = jnp.where(core == 0, total, swapped)
        totals_ref[...] = jnp.broadcast_to(total, totals_ref.shape)


def window_variance(info, own, other, hown, hother, halo, returns, table, devices):
    rows, width = returns.shape
    block = 2 * LANES
    fixed = lambda a: pl.BlockSpec(a.shape, lambda i: (0, 0))
    return pl.pallas_call(
        variance_kernel,
        grid=(width // block,),
        out_shape=(
            jax.ShapeDtypeStruct((rows, width), f32),
            jax.ShapeDtypeStruct((devices, SECTORS), f32),
        ),
        in_specs=[
            pl.BlockSpec(memory_space=pltpu.SMEM),
            fixed(own), fixed(other), fixed(hown), fixed(hother),
            pl.BlockSpec((W, block), lambda i: (0, i)),
            pl.BlockSpec((rows, block), lambda i: (0, i)),
            pl.BlockSpec((SECTORS, block), lambda i: (0, i)),
        ],
        out_specs=[
            pl.BlockSpec((rows, block), lambda i: (0, i)),
            pl.BlockSpec((devices, SECTORS), lambda i: (0, 0)),
        ],
        scratch_shapes=[
            pltpu.VMEM((3 * rows + W, SECTORS), bf16),
            pltpu.VMEM((3 * rows + W, SECTORS), bf16),
            pltpu.VMEM((rows, LANES), f32),
            pltpu.VMEM((16, SECTORS), f32),
        ],
        compiler_params=pltpu.CompilerParams(vmem_limit_bytes=24 * MIB),
        cost_estimate=pl.CostEstimate(
            flops=12 * rows * width * SECTORS, bytes_accessed=12 * rows * width, transcendentals=0
        ),
        name="window_variance",
    )(info, own, other, hown, hother, halo, returns, table)


def shrink_kernel(all_steps, core_ref, parts_ref, cown_ref, cother_ref, table_ref, var_ref, out_ref, pooled_ref):
    @pl.when(pl.program_id(0) == 0)
    def _():
        total = jnp.sum(parts_ref[...], axis=0, keepdims=True)
        swapped = jnp.concatenate([total[:, HALF:], total[:, :HALF]], axis=1)
        total = jnp.where(core_ref[0] == 0, total, swapped)
        count = jnp.concatenate([cown_ref[0:1], cother_ref[0:1]], axis=1)
        mean = total / (all_steps * jnp.maximum(count, 1.0))
        spread = dot_nn(split3_rows(shrink_weight * mean), table_ref[...])
        pooled_ref[...] = jnp.broadcast_to(
            jnp.sum(spread, axis=0, keepdims=True), pooled_ref.shape
        )

    out_ref[...] = var_ref[...] + pooled_ref[0:1]


def shrink(all_steps, core, parts, own, other, table, variance):
    rows, width = variance.shape
    block = rows // 4
    tail = pl.BlockSpec((8, HALF), lambda i: (rows // 8, 0))
    return pl.pallas_call(
        functools.partial(shrink_kernel, float(all_steps)),
        grid=(rows // block,),
        out_shape=jax.ShapeDtypeStruct((rows, width), f32),
        in_specs=[
            pl.BlockSpec(memory_space=pltpu.SMEM),
            pl.BlockSpec(parts.shape, lambda i: (0, 0)),
            tail,
            tail,
            pl.BlockSpec(table.shape, lambda i: (0, 0)),
            pl.BlockSpec((block, width), lambda i: (i, 0)),
        ],
        out_specs=pl.BlockSpec((block, width), lambda i: (i, 0)),
        scratch_shapes=[pltpu.VMEM((8, width), f32)],
        compiler_params=pltpu.CompilerParams(vmem_limit_bytes=24 * MIB),
        cost_estimate=pl.CostEstimate(
            flops=2 * rows * width, bytes_accessed=8 * rows * width, transcendentals=0
        ),
        name="shrink",
    )(core, parts, own, other, table, variance)


def swap(value, axis, bit):
    return lax.ppermute(value, axis, [(i, i ^ bit) for i in range(lax.axis_size(axis))])


def ahead(value, axis):
    return lax.ppermute(value, axis, [(i, i + 1) for i in range(lax.axis_size(axis) - 1)])


def across(value, axis):
    bit = 2
    while bit < lax.axis_size(axis):
        value = value + swap(value, axis, bit)
        bit *= 2
    return value


def local(returns, sector):
    rows, width = returns.shape
    n_time, n_series = lax.axis_size("tm"), lax.axis_size("series")
    core = (lax.axis_index("series") % 2).astype(jnp.int32)
    first_step = (lax.axis_index("tm") * rows).astype(jnp.int32)
    info = jnp.stack([core, first_step])
    keep, send, table, tail = sector_sums(info, returns, sector[None, :])
    part = keep + swap(send, "series", 1)
    part_tail = ahead(part[rows - W : rows], "tm")
    halo = ahead(tail, "tm")
    own = across(part, "series")
    own_tail = across(part_tail, "series")
    other = swap(own, "series", 1)
    other_tail = swap(own_tail, "series", 1)
    variance, totals = window_variance(
        info, own, other, own_tail, other_tail, halo, returns, table, n_time * n_series
    )
    parts = lax.all_to_all(totals, ("tm", "series"), 0, 0)
    return shrink(n_time * rows, info, parts, own, other, table, variance)


def solution(mesh):
    placed = (P("tm", "series"), P("series"))
    return jax.shard_map(
        local, mesh=mesh, in_specs=placed, out_specs=P("tm", "series"), check_vma=False
    )
```

time: 131 us -> 58.9 us (0.45)
  matrix products: 26.3 us -> 0 us
  blocking collectives: 34.6 us -> 13.1 us
  Pallas kernels: 0 us -> 16.8 us
  waiting for transfers between devices: 31.6 us -> 14.9 us
  between operations: 13.5 us -> 0.08 us
  other arithmetic: 13.5 us -> 0.16 us
  starting transfers between devices: 8.5 us -> 11.3 us
    psum x3 -> x0, blocking collectives: 34.6 us -> none  [the longest x1 22.2 us: local(): totals = lax.psum(series_totals, 'tm')]
    dot_general x5 -> x0, matrix products: 26.3 us -> none  [the longest x1 12.4 us: window_variance(): jnp.dot(band_matrix(rows), stacked, precision=highest, preferred_element_...]
    psum x1 -> x0, waiting for transfers between devices: 23.2 us -> none  [local(): sums, counts = lax.psum((part_sums, part_counts), 'series')]
    pallas_call x0 -> x3, Pallas kernels: none -> 16.8 us  [the longest x1 11.8 us: window_variance(): pl.pallas_call(variance_kernel, grid=(width // block,), out_shape=(jax.Sh...]
    all_to_all x0 -> x1, blocking collectives: none -> 13.1 us  [local(): parts = lax.all_to_all(totals, ('tm', 'series'), 0, 0)]
    unnamed x4 -> x0, other arithmetic: 7.57 us -> none
    ppermute x2 -> x7, waiting for transfers between devices: 8.4 us -> 14.9 us  [the longest x5 9.48 us: swap(): lax.ppermute(value, axis, [(i, i ^ bit) for i in range(lax.axis_size(axis...]
    ppermute x2 -> x7, starting transfers between devices: 8.49 us -> 11.3 us  [the longest x2 7.12 us: ahead(): lax.ppermute(value, axis, [(i, i + 1) for i in range(lax.axis_size(axis)...]
  transfers between devices with their start and end apart: 3 -> 7, of which waited for: 2 -> 5; matrix products, arithmetic and copies ran while one was open for 7% -> 0% of each run, Pallas kernels for 0% -> 0%
where the time goes in v1:
time: 58.9 us; the launch traced here: 58.6 us
  Pallas kernels  16.8 us (29%)
  waiting for transfers between devices  14.9 us (25%)
  blocking collectives  13.1 us (22%)
  starting transfers between devices  11.3 us (19%)
  local copies, waits for them, and re-layouts  2.37 us (4%)
    all_to_all x1, blocking collectives, local(): parts = lax.all_to_all(totals, ('tm', 'series'), 0, 0)  13.1 us
    pallas_call x1, Pallas kernels, window_variance(): pl.pallas_call(variance_kernel, grid=(width // block,), out_shape=(jax.Sh...  11.8 us
    ppermute x5, waiting for transfers between devices, swap(): lax.ppermute(value, axis, [(i, i ^ bit) for i in range(lax.axis_size(axis...  9.48 us
    ppermute x2, starting transfers between devices, ahead(): lax.ppermute(value, axis, [(i, i + 1) for i in range(lax.axis_size(axis)...  7.12 us
    ppermute x2, waiting for transfers between devices, ahead(): lax.ppermute(value, axis, [(i, i + 1) for i in range(lax.axis_size(axis)...  5.42 us
    ppermute x5, starting transfers between devices, swap(): lax.ppermute(value, axis, [(i, i ^ bit) for i in range(lax.axis_size(axis...  4.15 us
    pallas_call x1, Pallas kernels, shrink(): pl.pallas_call(functools.partial(shrink_kernel, float(all_steps)), grid=(...  2.81 us
    unnamed x5, local copies, waits for them, and re-layouts  2.29 us
  transfers between devices with their start and end apart: 7, of which 5 were waited for; matrix products, arithmetic and copies ran while one was open for 0% of the time, Pallas kernels for 0%

profile of v1, /device:TPU:0, one launch (start us, length us, event | category | flops | bytes accessed | tf_op | source)
XLA Modules:
  0.0 58.6 jit_solution(7340752306812103176)
XLA Ops:
  0.0 0.1 pad_add_fusion.core_ref.info_ref
  0.1 0.0 copy-start
  0.1 1.6 %copy-done = f32[256,2048]{1,0:T(8,128)S(1)} copy-done((f32[256,2048]{1,0:T(8,128)S(1)}, f32[256,2048]{1,0:T(8,128)}, u32[]{:S(2)}) %copy-start) | copy-done | bytes 2097176
  1.7 0.0 copy-start.1
  1.7 0.7 %copy-done.1 = s32[2048]{0:T(1024)S(1)} copy-done((s32[2048]{0:T(1024)S(1)}, s32[2048]{0:T(1024)}, u32[]{:S(2)}) %copy-start.1) | copy-done | bytes 8216
  2.4 2.2 %sector_sums.1 = (f32[264,256]{1,0:T(8,128)S(1)}, f32[264,256]{1,0:T(8,128)S(1)}, bf16[512,2048]{1,0:T(8,128)(2,1)S(1)}, f32[64,2048]{1,0:T(8,128)S(1)}) custom-call(s32[2]{0:T(128)S(1)} %pad_add_fusion.core_ref.info_ref, f32[256,2048]{1,0:T(8,128)S(1)} %copy-done, s32[1,2048]{1,0:T(1,128)S(1)} %bitcast.9), custom_call_target="tpu_custom_call" | custom-call | flops 1073741824 | bytes 4194304 | tf_op jit(solution)/shard_map/sector_sums/pallas_call | solution.py:74
  4.5 0.6 collective-permute-start
  5.1 1.2 %collective-permute-done = f32[264,256]{1,0:T(8,128)S(1)} collective-permute-done((f32[264,256]{1,0:T(8,128)S(1)}, f32[264,256]{1,0:T(8,128)S(1)}, u32[]{:S(2)}, u32[]{:S(2)}) %collective-permute-start) | collective-permute-done | bytes 270368 | tf_op jit(solution)/shard_map/ppermute | solution.py:230
  6.3 2.9 %collective-permute-start.1 = (f32[264,256]{1,0:T(8,128)S(1)}, f32[264,256]{1,0:T(8,128)S(1)}, u32[]{:S(2)}, u32[]{:S(2)}) collective-permute-start(f32[264,256]{1,0:T(8,128)S(1)} %add.14), channel_id=1, source_target_pairs={{0,2},{1,3},{2,0},{3,1},{4,6},{5,7},{6,4},{7,5},{8,10},{9,11},{10,... | collective-permute-start | bytes 811016 | tf_op jit(solution)/shard_map/ppermute | solution.py:230
  9.2 3.4 %collective-permute-start.6 = (f32[64,2048]{1,0:T(8,128)S(1)}, f32[64,2048]{1,0:T(8,128)S(1)}, u32[]{:S(2)}, u32[]{:S(2)}) collective-permute-start(f32[64,2048]{1,0:T(8,128)S(1)} %get-tuple-element.13), channel_id=1, source_target_pairs={{0,4},{4,8},{8,12},{12,16},{16,20},{20,24},{24,28},{1,5},{5,9},{9,... | collective-permute-start | bytes 1572872 | tf_op jit(solution)/shard_map/ppermute | solution.py:234
  12.7 3.3 %collective-permute-done.1 = f32[264,256]{1,0:T(8,128)S(1)} collective-permute-done((f32[264,256]{1,0:T(8,128)S(1)}, f32[264,256]{1,0:T(8,128)S(1)}, u32[]{:S(2)}, u32[]{:S(2)}) %collective-permute-start.1) | collective-permute-done | bytes 270368 | tf_op jit(solution)/shard_map/ppermute | solution.py:230
  16.1 0.1 collective-permute-start.2
  16.1 3.7 %collective-permute-start.3 = (f32[64,256]{1,0:T(8,128)S(1)}, f32[64,256]{1,0:T(8,128)S(1)}, u32[]{:S(2)}, u32[]{:S(2)}) collective-permute-start(f32[64,256]{1,0:T(8,128)S(1)} %slice.4), channel_id=1, source_target_pairs={{0,4},{4,8},{8,12},{12,16},{16,20},{20,24},{24,28},{1,5},{5,9},{9,... | collective-permute-start | bytes 196616 | tf_op jit(solution)/shard_map/ppermute | solution.py:234
  19.8 5.4 %collective-permute-done.3 = f32[64,256]{1,0:T(8,128)S(1)} collective-permute-done((f32[64,256]{1,0:T(8,128)S(1)}, f32[64,256]{1,0:T(8,128)S(1)}, u32[]{:S(2)}, u32[]{:S(2)}) %collective-permute-start.3) | collective-permute-done | bytes 65568 | tf_op jit(solution)/shard_map/ppermute | solution.py:234
  25.3 0.5 collective-permute-start.4
  25.8 3.7 %collective-permute-done.4 = f32[64,256]{1,0:T(8,128)S(1)} collective-permute-done((f32[64,256]{1,0:T(8,128)S(1)}, f32[64,256]{1,0:T(8,128)S(1)}, u32[]{:S(2)}, u32[]{:S(2)}) %collective-permute-start.4) | collective-permute-done | bytes 65568 | tf_op jit(solution)/shard_map/ppermute | solution.py:230
  29.5 0.1 collective-permute-start.5
  29.6 1.2 %collective-permute-done.5.hother_ref = f32[64,256]{1,0:T(8,128)S(1)} collective-permute-done((f32[64,256]{1,0:T(8,128)S(1)}, f32[64,256]{1,0:T(8,128)S(1)}, u32[]{:S(2)}, u32[]{:S(2)}) %collective-permute-start.5) | collective-permute-done | bytes 65568 | tf_op jit(solution)/shard_map/ppermute | solution.py:230
  30.9 0.0 collective-permute-done.6.halo_ref
  30.9 0.0 collective-permute-done.2.other_ref.cother_ref
  30.9 11.8 %window_variance.1 = (f32[256,2048]{1,0:T(8,128)S(1)}, f32[32,512]{1,0:T(8,128)S(1)}) custom-call(s32[2]{0:T(128)S(1)} %pad_add_fusion.core_ref.info_ref, f32[264,256]{1,0:T(8,128)S(1)} %add.15.own_ref.cown_ref, f32[264,256]{1,0:T(8,128)S(1)} %collective-permute-done.2.other_ref.cother_ref, f32[64,256]{1,0:T(8,128)S(1)} %add.16.hown_ref, ...), custom_call_target="tpu_custom_call" | custom-call | flops 3221225472 | bytes 6291456 | tf_op jit(solution)/shard_map/window_variance/pallas_call | solution.py:155
  42.7 0.1 copy.3
  42.7 13.1 %all_to_all.11 = f32[32,1,512]{2,1,0:T(1,128)S(1)} all-to-all(f32[32,1,512]{2,1,0:T(1,128)S(1)} %copy.3), channel_id=1, replica_groups=mesh['tm'=8,'series'=4] {'tm','series'}, dimensions={0} | all-to-all | bytes 131072 | tf_op jit(solution)/shard_map/all_to_all | solution.py:262
  55.8 2.8 %shrink.1 = f32[256,2048]{1,0:T(8,128)} custom-call(s32[2]{0:T(128)S(1)} %pad_add_fusion.core_ref.info_ref, f32[32,512]{1,0:T(8,128)S(1)} %bitcast.7, f32[264,256]{1,0:T(8,128)S(1)} %add.15.own_ref.cown_ref, f32[264,256]{1,0:T(8,128)S(1)} %collective-permute-done.2.other_ref.cother_ref, bf16[512,2048]{1,0:T(8,128)(2,1)S(1)} %get-tuple-element.14.table_ref, ...), custom_call_target="tpu_custom_call" | custom-call | flops 1048576 | bytes 4194304 | tf_op jit(solution)/shard_map/shrink/pallas_call | solution.py:207
  (5 shorter events, 0.1 us)
Async XLA Ops:
  0.1 1.6 %copy-start = (f32[256,2048]{1,0:T(8,128)S(1)}, f32[256,2048]{1,0:T(8,128)}, u32[]{:S(2)}) copy-start(f32[256,2048]{1,0:T(8,128)} %ret_ref.3) | copy-start | bytes 6291460
  1.7 0.7 %copy-start.1 = (s32[2048]{0:T(1024)S(1)}, s32[2048]{0:T(1024)}, u32[]{:S(2)}) copy-start(s32[2048]{0:T(1024)} %param.3) | copy-start | bytes 24580
  4.5 1.7 %collective-permute-start = (f32[264,256]{1,0:T(8,128)S(1)}, f32[264,256]{1,0:T(8,128)S(1)}, u32[]{:S(2)}, u32[]{:S(2)}) collective-permute-start(f32[264,256]{1,0:T(8,128)S(1)} %get-tuple-element.12), channel_id=1, source_target_pairs={{0,1},{1,0},{2,3},{3,2},{4,5},{5,4},{6,7},{7,6},{8,9},{9,8},{10,11... | collective-permute-start | bytes 811016 | tf_op jit(solution)/shard_map/ppermute | solution.py:230
  6.3 9.7 %collective-permute-start.1 = (f32[264,256]{1,0:T(8,128)S(1)}, f32[264,256]{1,0:T(8,128)S(1)}, u32[]{:S(2)}, u32[]{:S(2)}) collective-permute-start(f32[264,256]{1,0:T(8,128)S(1)} %add.14), channel_id=1, source_target_pairs={{0,2},{1,3},{2,0},{3,1},{4,6},{5,7},{6,4},{7,5},{8,10},{9,11},{10,... | collective-permute-start | bytes 811016 | tf_op jit(solution)/shard_map/ppermute | solution.py:230
  9.2 21.6 %collective-permute-start.6 = (f32[64,2048]{1,0:T(8,128)S(1)}, f32[64,2048]{1,0:T(8,128)S(1)}, u32[]{:S(2)}, u32[]{:S(2)}) collective-permute-start(f32[64,2048]{1,0:T(8,128)S(1)} %get-tuple-element.13), channel_id=1, source_target_pairs={{0,4},{4,8},{8,12},{12,16},{16,20},{20,24},{24,28},{1,5},{5,9},{9,... | collective-permute-start | bytes 1572872 | tf_op jit(solution)/shard_map/ppermute | solution.py:234
  16.1 14.8 %collective-permute-start.2 = (f32[264,256]{1,0:T(8,128)S(1)}, f32[264,256]{1,0:T(8,128)S(1)}, u32[]{:S(2)}, u32[]{:S(2)}) collective-permute-start(f32[264,256]{1,0:T(8,128)S(1)} %add.15.own_ref.cown_ref), channel_id=1, source_target_pairs={{0,1},{1,0},{2,3},{3,2},{4,5},{5,4},{6,7},{7,6},{8,9},{9,8},{10,11... | collective-permute-start | bytes 811016 | tf_op jit(solution)/shard_map/ppermute | solution.py:230
  16.1 9.1 %collective-permute-start.3 = (f32[64,256]{1,0:T(8,128)S(1)}, f32[64,256]{1,0:T(8,128)S(1)}, u32[]{:S(2)}, u32[]{:S(2)}) collective-permute-start(f32[64,256]{1,0:T(8,128)S(1)} %slice.4), channel_id=1, source_target_pairs={{0,4},{4,8},{8,12},{12,16},{16,20},{20,24},{24,28},{1,5},{5,9},{9,... | collective-permute-start | bytes 196616 | tf_op jit(solution)/shard_map/ppermute | solution.py:234
  25.3 4.3 %collective-permute-start.4 = (f32[64,256]{1,0:T(8,128)S(1)}, f32[64,256]{1,0:T(8,128)S(1)}, u32[]{:S(2)}, u32[]{:S(2)}) collective-permute-start(f32[64,256]{1,0:T(8,128)S(1)} %collective-permute-done.3), channel_id=1, source_target_pairs={{0,2},{1,3},{2,0},{3,1},{4,6},{5,7},{6,4},{7,5},{8,10},{9,11},{10,... | collective-permute-start | bytes 196616 | tf_op jit(solution)/shard_map/ppermute | solution.py:230
  29.5 1.3 %collective-permute-start.5 = (f32[64,256]{1,0:T(8,128)S(1)}, f32[64,256]{1,0:T(8,128)S(1)}, u32[]{:S(2)}, u32[]{:S(2)}) collective-permute-start(f32[64,256]{1,0:T(8,128)S(1)} %add.16.hown_ref), channel_id=1, source_target_pairs={{0,1},{1,0},{2,3},{3,2},{4,5},{5,4},{6,7},{7,6},{8,9},{9,8},{10,11... | collective-permute-start | bytes 196616 | tf_op jit(solution)/shard_map/ppermute | solution.py:230

commit v2 on v1

v2 whole, which is shorter than its diff:
```python
import functools

import jax
import jax.numpy as jnp
from jax import lax
from jax.experimental import pallas as pl
from jax.experimental.pallas import tpu as pltpu
from jax.sharding import PartitionSpec as P


W = 64
SECTORS = 512
HALF = SECTORS // 2
LANES = 128

ridge_rate = 0.05
shrink_weight = 0.3

f32 = jnp.float32
bf16 = jnp.bfloat16
MIB = 1024 * 1024


def dot_nn(a, b):
    return lax.dot_general(a, b, (((1,), (0,)), ((), ())), preferred_element_type=f32)


def dot_nt(a, b):
    return lax.dot_general(a, b, (((1,), (1,)), ((), ())), preferred_element_type=f32)


def split2(x):
    hi = x.astype(bf16)
    return hi, (x - hi.astype(f32)).astype(bf16)


def split3_rows(x):
    hi = x.astype(bf16).astype(f32)
    rest = x - hi
    mid = rest.astype(bf16).astype(f32)
    low = rest - mid
    row = lax.broadcasted_iota(jnp.int32, (16, x.shape[1]), 0)
    return jnp.where(row == 0, hi, jnp.where(row == 1, mid, jnp.where(row == 2, low, 0.0))).astype(bf16)


def sums_kernel(core_ref, ret_ref, sec_ref, keep_ref, send_ref, table_ref, tail_ref, hi_ref, lo_ref):
    rows = ret_ref.shape[0]
    core = core_ref[0]
    label = lax.broadcasted_iota(jnp.int32, table_ref.shape, 0)
    label = (label + core * HALF) & (SECTORS - 1)
    table_ref[...] = jnp.where(label == sec_ref[...], 1.0, 0.0).astype(bf16)
    value = ret_ref[...]
    hi, lo = split2(value)
    hi_ref[:rows] = hi
    lo_ref[:rows] = lo
    hi_ref[rows:] = jnp.ones_like(hi_ref[rows:])
    lo_ref[rows:] = jnp.zeros_like(lo_ref[rows:])
    tail_ref[...] = ret_ref[rows - W :]
    acc = dot_nt(hi_ref[...], table_ref[...]) + dot_nt(lo_ref[...], table_ref[...])
    keep_ref[...] = acc[: rows + 8, :HALF]
    send_ref[...] = acc[: rows + 8, HALF:]


def sector_sums(core, returns, sector):
    rows, width = returns.shape
    half = jax.ShapeDtypeStruct((rows + 8, HALF), f32)
    return pl.pallas_call(
        sums_kernel,
        out_shape=(
            half,
            half,
            jax.ShapeDtypeStruct((SECTORS, width), bf16),
            jax.ShapeDtypeStruct((W, width), f32),
        ),
        in_specs=[
            pl.BlockSpec(memory_space=pltpu.SMEM),
            pl.BlockSpec(memory_space=pltpu.VMEM),
            pl.BlockSpec(memory_space=pltpu.VMEM),
        ],
        out_specs=[pl.BlockSpec(memory_space=pltpu.VMEM)] * 4,
        scratch_shapes=[pltpu.VMEM((rows + 16, width), bf16)] * 2,
        compiler_params=pltpu.CompilerParams(vmem_limit_bytes=24 * MIB),
        cost_estimate=pl.CostEstimate(
            flops=4 * rows * width * SECTORS, bytes_accessed=8 * rows * width, transcendentals=0
        ),
        name="sector_sums",
    )(core, returns, sector)


class Window:
    def __init__(self):
        self.rolled = {}
        self.sums = {8: [], 16: [], 32: []}

    def push(self, x, row):
        size = 1
        while size < 8:
            turned = pltpu.roll(x, size, 0)
            before = self.rolled.get(size, turned)
            self.rolled[size] = turned
            x = x + jnp.where(row < size, before, turned)
            size *= 2
        while size < W:
            seen = self.sums[size]
            seen.append(x)
            back = size // 8
            if len(seen) <= back:
                return None
            x = x + seen[-1 - back]
            size *= 2
        return x


def tile_at(index):
    return pl.ds(pl.multiple_of(index * LANES, LANES), LANES)


def rows_of(group):
    return slice(group * 8, group * 8 + 8)


def inverse_counts(first_step, inv_ref):
    position = lax.broadcasted_iota(jnp.int32, inv_ref.shape, 0) + (first_step + 1)
    inv_ref[...] = 1.0 / jnp.minimum(position, W).astype(f32)


def moments_body(load, inv, groups, mean_ref, crr_ref):
    row = lax.broadcasted_iota(jnp.int32, (8, LANES), 0)

    def tile(index, _):
        cols = tile_at(index)
        first, second = Window(), Window()
        for group in range(groups):
            ret = load(group, cols)
            total, squares = first.push(ret, row), second.push(ret * ret, row)
            if group >= W // 8:
                here = rows_of(group - W // 8)
                scale = inv(group - W // 8)
                mean = total * scale
                mean_ref[here, cols] = mean
                crr_ref[here, cols] = squares * scale - mean * mean
        return 0

    lax.fori_loop(0, mean_ref.shape[1] // LANES, tile, 0)


def moments_main_kernel(ret_ref, mean_ref, crr_ref):
    moments_body(
        lambda group, cols: ret_ref[rows_of(group), cols],
        lambda group: 1.0 / W,
        ret_ref.shape[0] // 8,
        mean_ref,
        crr_ref,
    )


def moments_head_kernel(info_ref, halo_ref, ret_ref, mean_ref, crr_ref, inv_ref):
    inverse_counts(info_ref[1], inv_ref)
    blocks = W // 8
    moments_body(
        lambda group, cols: halo_ref[rows_of(group), cols]
        if group < blocks
        else ret_ref[rows_of(group - blocks), cols],
        lambda group: inv_ref[rows_of(group)],
        2 * blocks,
        mean_ref,
        crr_ref,
    )


def sector_rows(means, inv, groups, starts, hi_ref, lo_ref, out):
    row = lax.broadcasted_iota(jnp.int32, (8, LANES), 0)
    first, second = Window(), Window()
    mean_parts, gain_parts = [], []
    for group in range(groups):
        mean = means[group]
        total, squares = first.push(mean, row), second.push(mean * mean, row)
        if group >= W // 8:
            scale = inv(group - W // 8)
            mean_f = total * scale
            mean_parts.append(mean_f)
            gain_parts.append(1.0 / (squares * scale - mean_f * mean_f + ridge_rate))
    for start, parts in zip(starts, (means, mean_parts, gain_parts)):
        if start is None:
            continue
        for pair in range(0, len(parts), 2):
            hi, lo = split2(jnp.concatenate(parts[pair : pair + 2], axis=0))
            here = slice(start + pair * 8, start + pair * 8 + 16)
            hi_ref[here, out] = hi
            lo_ref[here, out] = lo


def main_kernel(
    own_ref, other_ref, own_tail_ref, other_tail_ref, ret_ref, mean_ref, crr_ref, table_ref,
    var_ref, factor_ref, colsum_ref, hi_ref, lo_ref, spread_ref,
):
    rows = ret_ref.shape[0]
    main = rows - W
    blocks = W // 8
    for tile in range(SECTORS // LANES):
        here, tail = (own_ref, own_tail_ref) if tile < HALF // LANES else (other_ref, other_tail_ref)
        cols = pl.ds((tile * LANES) % HALF, LANES)
        scale = 1.0 / jnp.maximum(tail[W : W + 8, cols], 1.0)
        means = [
            (here[rows_of(g), cols] if g < main // 8 else tail[rows_of(g - main // 8), cols]) * scale
            for g in range(rows // 8)
        ]
        sector_rows(
            means, lambda g: 1.0 / W, rows // 8, (0, rows, rows + main), hi_ref, lo_ref,
            slice(tile * LANES, (tile + 1) * LANES),
        )
    row = lax.broadcasted_iota(jnp.int32, (8, LANES), 0)
    wide = spread_ref.shape[1]

    def chunk(index, _):
        outer = pl.ds(pl.multiple_of(index * wide, wide), wide)
        spread_ref[...] = dot_nn(hi_ref[...], table_ref[:, outer]) + dot_nn(
            lo_ref[...], table_ref[:, outer]
        )
        for tile in range(wide // LANES):
            inner = slice(tile * LANES, (tile + 1) * LANES)
            cols = pl.ds(pl.multiple_of(index * wide + tile * LANES, LANES), LANES)
            cross = Window()
            total = jnp.zeros((8, LANES), f32)
            for group in range(rows // 8):
                factor = spread_ref[rows_of(group), inner]
                if group < blocks:
                    factor_ref[rows_of(group), cols] = factor
                product = cross.push(ret_ref[rows_of(group), cols] * factor, row)
                if group >= blocks:
                    g = group - blocks
                    mean_f = spread_ref[rows_of(rows // 8 + g), inner]
                    gain = spread_ref[rows_of((rows + main) // 8 + g), inner]
                    crf = product * (1.0 / W) - mean_ref[rows_of(g), cols] * mean_f
                    variance = crr_ref[rows_of(g), cols] - crf * crf * gain
                    var_ref[rows_of(g), cols] = (1.0 - shrink_weight) * variance
                    total = total + variance
            colsum_ref[:, cols] = total
        return 0

    lax.fori_loop(0, ret_ref.shape[1] // wide, chunk, 0)


def head_kernel(
    info_ref, own_ref, other_ref, counts_own_ref, counts_other_ref, prior_own_ref, prior_other_ref,
    halo_ref, ret_ref, factor_ref, mean_ref, crr_ref, colsum_ref, table_ref,
    var_ref, totals_ref, hi_ref, lo_ref, spread_ref, inv_ref, parts_ref,
):
    blocks = W // 8
    inverse_counts(info_ref[1], inv_ref)
    for tile in range(SECTORS // LANES):
        mine = tile < HALF // LANES
        here, prior, counts = (
            (own_ref, prior_own_ref, counts_own_ref)
            if mine
            else (other_ref, prior_other_ref, counts_other_ref)
        )
        cols = pl.ds((tile * LANES) % HALF, LANES)
        scale = 1.0 / jnp.maximum(counts[W : W + 8, cols], 1.0)
        means = [
            (prior[rows_of(g), cols] if g < blocks else here[rows_of(g - blocks), cols]) * scale
            for g in range(2 * blocks)
        ]
        sector_rows(
            means, lambda g: inv_ref[rows_of(g)], 2 * blocks, (0, 2 * W, 3 * W), hi_ref, lo_ref,
            slice(tile * LANES, (tile + 1) * LANES),
        )
    row = lax.broadcasted_iota(jnp.int32, (8, LANES), 0)
    wide = spread_ref.shape[1]

    def chunk(index, _):
        outer = pl.ds(pl.multiple_of(index * wide, wide), wide)
        spread_ref[...] = dot_nn(hi_ref[...], table_ref[:, outer]) + dot_nn(
            lo_ref[...], table_ref[:, outer]
        )
        for tile in range(wide // LANES):
            inner = slice(tile * LANES, (tile + 1) * LANES)
            cols = pl.ds(pl.multiple_of(index * wide + tile * LANES, LANES), LANES)
            cross = Window()
            total = colsum_ref[:, cols]
            for group in range(2 * blocks):
                g = group - blocks
                if g < 0:
                    product = halo_ref[rows_of(group), cols] * spread_ref[rows_of(group), inner]
                else:
                    product = ret_ref[rows_of(g), cols] * factor_ref[rows_of(g), cols]
                product = cross.push(product, row)
                if g >= 0:
                    mean_f = spread_ref[rows_of(2 * blocks + g), inner]
                    gain = spread_ref[rows_of(3 * blocks + g), inner]
                    crf = product * inv_ref[rows_of(g)] - mean_ref[rows_of(g), cols] * mean_f
                    variance = crr_ref[rows_of(g), cols] - crf * crf * gain
                    var_ref[rows_of(g), cols] = (1.0 - shrink_weight) * variance
                    total = total + variance
            hi = total.astype(bf16).astype(f32)
            mid = (total - hi).astype(bf16).astype(f32)
            parts_ref[:, cols] = jnp.concatenate(
                [hi, mid, total - hi - mid, jnp.zeros_like(hi)], axis=0
            ).astype(bf16)
        return 0

    lax.fori_loop(0, ret_ref.shape[1] // wide, chunk, 0)
    total = jnp.sum(dot_nt(parts_ref[...], table_ref[...]), axis=0, keepdims=True)
    swapped = jnp.concatenate([total[:, HALF:], total[:, :HALF]], axis=1)
    total = jnp.where(info_ref[0] == 0, total, swapped)
    totals_ref[...] = jnp.broadcast_to(total, totals_ref.shape)


SMEM = pl.BlockSpec(memory_space=pltpu.SMEM)
VMEM = pl.BlockSpec(memory_space=pltpu.VMEM)


def kernel_call(body, outs, scalars, arrays, scratch=(), flops=0, moved=0):
    return kernel_of(body, outs, scalars, arrays, scratch, flops, moved)


def kernel_of(body, outs, scalars, arrays, scratch, flops, moved):
    return pl.pallas_call(
        body,
        out_shape=tuple(jax.ShapeDtypeStruct(shape, f32) for shape in outs),
        in_specs=[SMEM] * len(scalars) + [VMEM] * len(arrays),
        out_specs=[VMEM] * len(outs),
        scratch_shapes=list(scratch),
        compiler_params=pltpu.CompilerParams(vmem_limit_bytes=24 * MIB),
        cost_estimate=pl.CostEstimate(flops=flops, bytes_accessed=moved, transcendentals=0),
    )(*scalars, *arrays)


def shrink_kernel(
    all_steps, core_ref, parts_ref, cown_ref, cother_ref, table_ref, head_ref, main_ref, out_ref, pooled_ref
):
    step = pl.program_id(0)

    @pl.when(step == 0)
    def _():
        total = jnp.sum(parts_ref[...], axis=0, keepdims=True)
        swapped = jnp.concatenate([total[:, HALF:], total[:, :HALF]], axis=1)
        total = jnp.where(core_ref[0] == 0, total, swapped)
        count = jnp.concatenate([cown_ref[W : W + 1], cother_ref[W : W + 1]], axis=1)
        mean = total / (all_steps * jnp.maximum(count, 1.0))
        spread = dot_nn(split3_rows(shrink_weight * mean), table_ref[...])
        pooled_ref[...] = jnp.broadcast_to(
            jnp.sum(spread, axis=0, keepdims=True), pooled_ref.shape
        )
        out_ref[...] = head_ref[...] + pooled_ref[0:1]

    @pl.when(step > 0)
    def _():
        out_ref[...] = main_ref[...] + pooled_ref[0:1]


def shrink(all_steps, core, parts, own, other, table, head, main):
    width = head.shape[1]
    rows = head.shape[0] + main.shape[0]
    fixed = lambda a: pl.BlockSpec(a.shape, lambda i: (0, 0))
    return pl.pallas_call(
        functools.partial(shrink_kernel, float(all_steps)),
        grid=(rows // W,),
        out_shape=jax.ShapeDtypeStruct((rows, width), f32),
        in_specs=[
            SMEM,
            fixed(parts),
            fixed(own),
            fixed(other),
            fixed(table),
            fixed(head),
            pl.BlockSpec((W, width), lambda i: (jnp.maximum(i - 1, 0), 0)),
        ],
        out_specs=pl.BlockSpec((W, width), lambda i: (i, 0)),
        scratch_shapes=[pltpu.VMEM((8, width), f32)],
        compiler_params=pltpu.CompilerParams(vmem_limit_bytes=24 * MIB),
        cost_estimate=pl.CostEstimate(
            flops=2 * rows * width, bytes_accessed=8 * rows * width, transcendentals=0
        ),
        name="shrink",
    )(core, parts, own, other, table, head, main)


def swap(value, axis, bit):
    return lax.ppermute(value, axis, [(i, i ^ bit) for i in range(lax.axis_size(axis))])


def ahead(value, axis):
    return lax.ppermute(value, axis, [(i, i + 1) for i in range(lax.axis_size(axis) - 1)])


def across(value, axis):
    bit = 2
    while bit < lax.axis_size(axis):
        value = value + swap(value, axis, bit)
        bit *= 2
    return value


def step(returns, sector):
    rows, width = returns.shape
    main = rows - W
    n_time, n_series = lax.axis_size("tm"), lax.axis_size("series")
    core = (lax.axis_index("series") % 2).astype(jnp.int32)
    first_step = (lax.axis_index("tm") * rows).astype(jnp.int32)
    info = jnp.stack([core, first_step])
    keep, send, table, tail = sector_sums(info, returns, sector[None, :])
    halo = ahead(tail, "tm")
    swapped = swap(send, "series", 1)
    own_tail = across(keep[main:] + swapped[main:], "series")
    own = across(keep[:main] + swapped[:main], "series")
    prior_own = ahead(own_tail, "tm")
    other_tail = swap(own_tail, "series", 1)
    other = swap(own, "series", 1)
    prior_other = swap(prior_own, "series", 1)
    wide = 2 * LANES
    lhs = 3 * rows - 2 * W
    mean, crr = kernel_call(
        moments_main_kernel, [(main, width)] * 2, [], [returns],
        flops=40 * main * width, moved=12 * main * width,
    )
    mean_head, crr_head = kernel_call(
        moments_head_kernel, [(W, width)] * 2, [info], [halo, returns],
        scratch=[pltpu.VMEM((W, LANES), f32)], flops=40 * W * width, moved=12 * W * width,
    )
    var, factor, colsum = kernel_call(
        main_kernel, [(main, width), (W, width), (8, width)], [],
        [own, other, own_tail, other_tail, returns, mean, crr, table],
        scratch=[pltpu.VMEM((lhs, SECTORS), bf16)] * 2 + [pltpu.VMEM((lhs, wide), f32)],
        flops=4 * lhs * width * SECTORS, moved=12 * rows * width,
    )
    var_head, totals = kernel_call(
        head_kernel, [(W, width), (n_time * n_series, SECTORS)], [info],
        [own, other, own_tail, other_tail, prior_own, prior_other, halo, returns, factor,
         mean_head, crr_head, colsum, table],
        scratch=[pltpu.VMEM((4 * W, SECTORS), bf16)] * 2
        + [pltpu.VMEM((4 * W, wide), f32), pltpu.VMEM((W, LANES), f32), pltpu.VMEM((32, width), bf16)],
        flops=16 * W * width * SECTORS, moved=12 * W * width,
    )
    parts = lax.all_to_all(totals, ("tm", "series"), 0, 0)
    return shrink(n_time * rows, info, parts, own_tail, other_tail, table, var_head, var)


def solution(mesh):
    placed = (P("tm", "series"), P("series"))
    return jax.shard_map(
        step, mesh=mesh, in_specs=placed, out_specs=P("tm", "series"), check_vma=False
    )
```

time: 58.9 us -> 53 us (0.90)
  waiting for transfers between devices: 14.9 us -> 6.22 us
  starting transfers between devices: 11.3 us -> 12.7 us
  Pallas kernels: 16.8 us -> 17.7 us
    ppermute x2, waiting for transfers between devices: 5.42 us -> 0.37 us  [ahead(): lax.ppermute(value, axis, [(i, i + 1) for i in range(lax.axis_size(axis)...]
    ppermute x5 -> x6, waiting for transfers between devices: 9.48 us -> 5.85 us  [swap(): lax.ppermute(value, axis, [(i, i ^ bit) for i in range(lax.axis_size(axis...]
    ppermute x5 -> x6, starting transfers between devices: 4.15 us -> 5.61 us  [swap(): lax.ppermute(value, axis, [(i, i ^ bit) for i in range(lax.axis_size(axis...]
    pallas_call x1 -> x4, Pallas kernels: 11.8 us -> 12.7 us  [kernel_of(): pl.pallas_call(body, out_shape=tuple((jax.ShapeDtypeStruct(shape, f32) fo...]
    unnamed x5 -> x7, local copies, waits for them, and re-layouts: 2.29 us -> 2.3 us
  transfers between devices with their start and end apart: 7 -> 8, of which waited for: 5 -> 4; matrix products, arithmetic and copies ran while one was open for 0% -> 0% of each run, Pallas kernels for 0% -> 16%
where the time goes in v2:
time: 53 us; the launch traced here: 52.7 us
  Pallas kernels  17.7 us (33%)
  blocking collectives  13.4 us (25%)
  starting transfers between devices  12.7 us (24%)
  waiting for transfers between devices  6.22 us (12%)
  local copies, waits for them, and re-layouts  2.36 us (4%)
    all_to_all x1, blocking collectives, step(): parts = lax.all_to_all(totals, ('tm', 'series'), 0, 0)  13.4 us
    pallas_call x4, Pallas kernels, kernel_of(): pl.pallas_call(body, out_shape=tuple((jax.ShapeDtypeStruct(shape, f32) fo...  12.7 us
    ppermute x2, starting transfers between devices, ahead(): lax.ppermute(value, axis, [(i, i + 1) for i in range(lax.axis_size(axis)...  7.12 us
    ppermute x6, waiting for transfers between devices, swap(): lax.ppermute(value, axis, [(i, i ^ bit) for i in range(lax.axis_size(axis...  5.85 us
    ppermute x6, starting transfers between devices, swap(): lax.ppermute(value, axis, [(i, i ^ bit) for i in range(lax.axis_size(axis...  5.61 us
    pallas_call x1, Pallas kernels, shrink(): pl.pallas_call(functools.partial(shrink_kernel, float(all_steps)), grid=(...  2.81 us
    unnamed x7, local copies, waits for them, and re-layouts  2.3 us
    pallas_call x1, Pallas kernels, sector_sums(): pl.pallas_call(sums_kernel, out_shape=(half, half, jax.ShapeDtypeStruct((...  2.18 us
  transfers between devices with their start and end apart: 8, of which 4 were waited for; matrix products, arithmetic and copies ran while one was open for 0% of the time, Pallas kernels for 16%

profile of v2, /device:TPU:0, one launch (start us, length us, event | category | flops | bytes accessed | tf_op | source)
XLA Modules:
  0.0 52.7 jit_solution(10772313303174666224)
XLA Ops:
  0.0 0.1 pad_add_fusion.core_ref.info_ref
  0.1 0.0 copy-start
  0.1 1.6 %copy-done = f32[256,2048]{1,0:T(8,128)S(1)} copy-done((f32[256,2048]{1,0:T(8,128)S(1)}, f32[256,2048]{1,0:T(8,128)}, u32[]{:S(2)}) %copy-start) | copy-done | bytes 2097176
  1.7 0.0 copy-start.2
  1.7 0.7 %copy-done.2 = s32[2048]{0:T(1024)S(1)} copy-done((s32[2048]{0:T(1024)S(1)}, s32[2048]{0:T(1024)}, u32[]{:S(2)}) %copy-start.2) | copy-done | bytes 8216
  2.4 0.0 copy-start.1
  2.4 2.2 %sector_sums.1 = (f32[264,256]{1,0:T(8,128)S(1)}, f32[264,256]{1,0:T(8,128)S(1)}, bf16[512,2048]{1,0:T(8,128)(2,1)S(1)}, f32[64,2048]{1,0:T(8,128)S(1)}) custom-call(s32[2]{0:T(128)S(1)} %pad_add_fusion.core_ref.info_ref, f32[256,2048]{1,0:T(8,128)S(1)} %copy-done, s32[1,2048]{1,0:T(1,128)S(1)} %bitcast.9), custom_call_target="tpu_custom_call" | custom-call | flops 1073741824 | bytes 4194304 | tf_op jit(solution)/shard_map/sector_sums/pallas_call | solution.py:67
  4.6 0.6 %collective-permute-start = (f32[264,256]{1,0:T(8,128)S(1)}, f32[264,256]{1,0:T(8,128)S(1)}, u32[]{:S(2)}, u32[]{:S(2)}) collective-permute-start(f32[264,256]{1,0:T(8,128)S(1)} %get-tuple-element.19), channel_id=1, source_target_pairs={{0,1},{1,0},{2,3},{3,2},{4,5},{5,4},{6,7},{7,6},{8,9},{9,8},{10,11... | collective-permute-start | bytes 811016 | tf_op jit(solution)/shard_map/ppermute | solution.py:380
  5.1 1.2 %collective-permute-done = f32[264,256]{1,0:T(8,128)S(1)} collective-permute-done((f32[264,256]{1,0:T(8,128)S(1)}, f32[264,256]{1,0:T(8,128)S(1)}, u32[]{:S(2)}, u32[]{:S(2)}) %collective-permute-start) | collective-permute-done | bytes 270368 | tf_op jit(solution)/shard_map/ppermute | solution.py:380
  6.3 2.9 %collective-permute-start.1 = (f32[192,256]{1,0:T(8,128)S(1)}, f32[192,256]{1,0:T(8,128)S(1)}, u32[]{:S(2)}, u32[]{:S(2)}) collective-permute-start(f32[192,256]{1,0:T(8,128)S(1)} %slice_add_fusion), channel_id=1, source_target_pairs={{0,2},{1,3},{2,0},{3,1},{4,6},{5,7},{6,4},{7,5},{8,10},{9,11},{10,... | collective-permute-start | bytes 589832 | tf_op jit(solution)/shard_map/ppermute | solution.py:380
  9.2 3.4 %collective-permute-start.7 = (f32[64,2048]{1,0:T(8,128)S(1)}, f32[64,2048]{1,0:T(8,128)S(1)}, u32[]{:S(2)}, u32[]{:S(2)}) collective-permute-start(f32[64,2048]{1,0:T(8,128)S(1)} %get-tuple-element.20), channel_id=1, source_target_pairs={{0,4},{4,8},{8,12},{12,16},{16,20},{20,24},{24,28},{1,5},{5,9},{9,... | collective-permute-start | bytes 1572872 | tf_op jit(solution)/shard_map/ppermute | solution.py:384
  12.7 1.7 %collective-permute-done.1 = f32[192,256]{1,0:T(8,128)S(1)} collective-permute-done((f32[192,256]{1,0:T(8,128)S(1)}, f32[192,256]{1,0:T(8,128)S(1)}, u32[]{:S(2)}, u32[]{:S(2)}) %collective-permute-start.1) | collective-permute-done | bytes 196640 | tf_op jit(solution)/shard_map/ppermute | solution.py:380
  14.5 0.1 collective-permute-start.2
  14.6 1.8 %collective-permute-start.3 = (f32[72,256]{1,0:T(8,128)S(1)}, f32[72,256]{1,0:T(8,128)S(1)}, u32[]{:S(2)}, u32[]{:S(2)}) collective-permute-start(f32[72,256]{1,0:T(8,128)S(1)} %slice_add_fusion.1), channel_id=1, source_target_pairs={{0,2},{1,3},{2,0},{3,1},{4,6},{5,7},{6,4},{7,5},{8,10},{9,11},{10,... | collective-permute-start | bytes 221192 | tf_op jit(solution)/shard_map/ppermute | solution.py:380
  16.4 2.9 %collective-permute-done.3 = f32[72,256]{1,0:T(8,128)S(1)} collective-permute-done((f32[72,256]{1,0:T(8,128)S(1)}, f32[72,256]{1,0:T(8,128)S(1)}, u32[]{:S(2)}, u32[]{:S(2)}) %collective-permute-start.3) | collective-permute-done | bytes 73760 | tf_op jit(solution)/shard_map/ppermute | solution.py:380
  19.3 3.7 %collective-permute-start.5 = (f32[72,256]{1,0:T(8,128)S(1)}, f32[72,256]{1,0:T(8,128)S(1)}, u32[]{:S(2)}, u32[]{:S(2)}) collective-permute-start(f32[72,256]{1,0:T(8,128)S(1)} %add.20.own_tail_ref.counts_own_ref.cown_ref), channel_id=1, source_target_pairs={{0,4},{4,8},{8,12},{12,16},{16,20},{20,24},{24,28},{1,5},{5,9},{9,... | collective-permute-start | bytes 221192 | tf_op jit(solution)/shard_map/ppermute | solution.py:384
  23.0 0.1 collective-permute-start.4
  23.1 0.0 copy-done.1
  23.1 2.0 %shard_map.28 = (f32[192,2048]{1,0:T(8,128)S(1)}, f32[192,2048]{1,0:T(8,128)S(1)}) custom-call(f32[256,2048]{1,0:T(8,128)S(1)} %copy-done.1), custom_call_target="tpu_custom_call" | custom-call | flops 15728640 | bytes 4718592 | tf_op jit(solution)/shard_map/pallas_call | solution.py:318
  25.1 0.4 collective-permute-done.5.prior_own_ref
  25.4 0.2 collective-permute-start.6
  25.6 0.0 collective-permute-done.7.halo_ref
  25.6 1.6 %shard_map.30 = (f32[64,2048]{1,0:T(8,128)S(1)}, f32[64,2048]{1,0:T(8,128)S(1)}) custom-call(s32[2]{0:T(128)S(1)} %pad_add_fusion.core_ref.info_ref, f32[64,2048]{1,0:T(8,128)S(1)} %collective-permute-done.7.halo_ref, f32[256,2048]{1,0:T(8,128)S(1)} %copy-done.1), custom_call_target="tpu_custom_call" | custom-call | flops 5242880 | bytes 1572864 | tf_op jit(solution)/shard_map/pallas_call | solution.py:318
  27.2 0.0 collective-permute-done.4.other_tail_ref.counts_other_ref.cother_ref
  27.2 0.0 collective-permute-done.2.other_ref
  27.2 5.1 %shard_map.29 = (f32[192,2048]{1,0:T(8,128)S(1)}, f32[64,2048]{1,0:T(8,128)S(1)}, f32[8,2048]{1,0:T(8,128)S(1)}) custom-call(f32[192,256]{1,0:T(8,128)S(1)} %add.18.own_ref, f32[192,256]{1,0:T(8,128)S(1)} %collective-permute-done.2.other_ref, f32[72,256]{1,0:T(8,128)S(1)} %add.20.own_tail_ref.counts_own_ref.cown_ref, ...), custom_call_target="tpu_custom_call" | custom-call | flops 2684354560 | bytes 6291456 | tf_op jit(solution)/shard_map/pallas_call | solution.py:318
  32.3 0.0 collective-permute-done.6.prior_other_ref
  32.4 4.1 %shard_map.31 = (f32[64,2048]{1,0:T(8,128)S(1)}, f32[32,512]{1,0:T(8,128)S(1)}) custom-call(s32[2]{0:T(128)S(1)} %pad_add_fusion.core_ref.info_ref, f32[192,256]{1,0:T(8,128)S(1)} %add.18.own_ref, f32[192,256]{1,0:T(8,128)S(1)} %collective-permute-done.2.other_ref, f32[72,256]{1,0:T(8,128)S(1)} %add.20.own_tail_ref.counts_own_ref.cown_ref, ...), custom_call_target="tpu_custom_call" | custom-call | flops 1073741824 | bytes 1572864 | tf_op jit(solution)/shard_map/pallas_call | solution.py:318
  36.4 0.1 copy.3
  36.5 13.4 %all_to_all.11 = f32[32,1,512]{2,1,0:T(1,128)S(1)} all-to-all(f32[32,1,512]{2,1,0:T(1,128)S(1)} %copy.3), channel_id=1, replica_groups=mesh['tm'=8,'series'=4] {'tm','series'}, dimensions={0} | all-to-all | bytes 131072 | tf_op jit(solution)/shard_map/all_to_all | solution.py:435
  49.9 2.8 %shrink.1 = f32[256,2048]{1,0:T(8,128)} custom-call(s32[2]{0:T(128)S(1)} %pad_add_fusion.core_ref.info_ref, f32[32,512]{1,0:T(8,128)S(1)} %bitcast.7, f32[72,256]{1,0:T(8,128)S(1)} %add.20.own_tail_ref.counts_own_ref.cown_ref, f32[72,256]{1,0:T(8,128)S(1)} %collective-permute-done.4.other_tail_ref.counts_other_ref.cother_ref, ...), custom_call_target="tpu_custom_call" | custom-call | flops 1048576 | bytes 4194304 | tf_op jit(solution)/shard_map/shrink/pallas_call | solution.py:356
  (5 shorter events, 0.1 us)
Async XLA Ops:
  0.1 1.6 %copy-start = (f32[256,2048]{1,0:T(8,128)S(1)}, f32[256,2048]{1,0:T(8,128)}, u32[]{:S(2)}) copy-start(f32[256,2048]{1,0:T(8,128)} %ret_ref.9) | copy-start | bytes 6291460
  1.7 0.7 %copy-start.2 = (s32[2048]{0:T(1024)S(1)}, s32[2048]{0:T(1024)}, u32[]{:S(2)}) copy-start(s32[2048]{0:T(1024)} %param.3) | copy-start | bytes 24580
  2.4 20.7 %copy-start.1 = (f32[256,2048]{1,0:T(8,128)S(1)}, f32[256,2048]{1,0:T(8,128)}, u32[]{:S(2)}) copy-start(f32[256,2048]{1,0:T(8,128)} %ret_ref.9) | copy-start | bytes 6291460
  4.6 1.7 %collective-permute-start = (f32[264,256]{1,0:T(8,128)S(1)}, f32[264,256]{1,0:T(8,128)S(1)}, u32[]{:S(2)}, u32[]{:S(2)}) collective-permute-start(f32[264,256]{1,0:T(8,128)S(1)} %get-tuple-element.19), channel_id=1, source_target_pairs={{0,1},{1,0},{2,3},{3,2},{4,5},{5,4},{6,7},{7,6},{8,9},{9,8},{10,11... | collective-permute-start | bytes 811016 | tf_op jit(solution)/shard_map/ppermute | solution.py:380
  6.3 8.1 %collective-permute-start.1 = (f32[192,256]{1,0:T(8,128)S(1)}, f32[192,256]{1,0:T(8,128)S(1)}, u32[]{:S(2)}, u32[]{:S(2)}) collective-permute-start(f32[192,256]{1,0:T(8,128)S(1)} %slice_add_fusion), channel_id=1, source_target_pairs={{0,2},{1,3},{2,0},{3,1},{4,6},{5,7},{6,4},{7,5},{8,10},{9,11},{10,... | collective-permute-start | bytes 589832 | tf_op jit(solution)/shard_map/ppermute | solution.py:380
  9.2 16.4 %collective-permute-start.7 = (f32[64,2048]{1,0:T(8,128)S(1)}, f32[64,2048]{1,0:T(8,128)S(1)}, u32[]{:S(2)}, u32[]{:S(2)}) collective-permute-start(f32[64,2048]{1,0:T(8,128)S(1)} %get-tuple-element.20), channel_id=1, source_target_pairs={{0,4},{4,8},{8,12},{12,16},{16,20},{20,24},{24,28},{1,5},{5,9},{9,... | collective-permute-start | bytes 1572872 | tf_op jit(solution)/shard_map/ppermute | solution.py:384
  14.5 12.7 %collective-permute-start.2 = (f32[192,256]{1,0:T(8,128)S(1)}, f32[192,256]{1,0:T(8,128)S(1)}, u32[]{:S(2)}, u32[]{:S(2)}) collective-permute-start(f32[192,256]{1,0:T(8,128)S(1)} %add.18.own_ref), channel_id=1, source_target_pairs={{0,1},{1,0},{2,3},{3,2},{4,5},{5,4},{6,7},{7,6},{8,9},{9,8},{10,11... | collective-permute-start | bytes 589832 | tf_op jit(solution)/shard_map/ppermute | solution.py:380
  14.6 4.7 %collective-permute-start.3 = (f32[72,256]{1,0:T(8,128)S(1)}, f32[72,256]{1,0:T(8,128)S(1)}, u32[]{:S(2)}, u32[]{:S(2)}) collective-permute-start(f32[72,256]{1,0:T(8,128)S(1)} %slice_add_fusion.1), channel_id=1, source_target_pairs={{0,2},{1,3},{2,0},{3,1},{4,6},{5,7},{6,4},{7,5},{8,10},{9,11},{10,... | collective-permute-start | bytes 221192 | tf_op jit(solution)/shard_map/ppermute | solution.py:380
  19.3 6.1 %collective-permute-start.5 = (f32[72,256]{1,0:T(8,128)S(1)}, f32[72,256]{1,0:T(8,128)S(1)}, u32[]{:S(2)}, u32[]{:S(2)}) collective-permute-start(f32[72,256]{1,0:T(8,128)S(1)} %add.20.own_tail_ref.counts_own_ref.cown_ref), channel_id=1, source_target_pairs={{0,4},{4,8},{8,12},{12,16},{16,20},{20,24},{24,28},{1,5},{5,9},{9,... | collective-permute-start | bytes 221192 | tf_op jit(solution)/shard_map/ppermute | solution.py:384
  23.0 4.2 %collective-permute-start.4 = (f32[72,256]{1,0:T(8,128)S(1)}, f32[72,256]{1,0:T(8,128)S(1)}, u32[]{:S(2)}, u32[]{:S(2)}) collective-permute-start(f32[72,256]{1,0:T(8,128)S(1)} %add.20.own_tail_ref.counts_own_ref.cown_ref), channel_id=1, source_target_pairs={{0,1},{1,0},{2,3},{3,2},{4,5},{5,4},{6,7},{7,6},{8,9},{9,8},{10,11... | collective-permute-start | bytes 221192 | tf_op jit(solution)/shard_map/ppermute | solution.py:380
  25.4 6.9 %collective-permute-start.6 = (f32[72,256]{1,0:T(8,128)S(1)}, f32[72,256]{1,0:T(8,128)S(1)}, u32[]{:S(2)}, u32[]{:S(2)}) collective-permute-start(f32[72,256]{1,0:T(8,128)S(1)} %collective-permute-done.5.prior_own_ref), channel_id=1, source_target_pairs={{0,1},{1,0},{2,3},{3,2},{4,5},{5,4},{6,7},{7,6},{8,9},{9,8},{10,11... | collective-permute-start | bytes 221192 | tf_op jit(solution)/shard_map/ppermute | solution.py:380

commit v3 on v2

--- a/solution.py
+++ b/solution.py
@@ -43,27 +43,57 @@
     return jnp.where(row == 0, hi, jnp.where(row == 1, mid, jnp.where(row == 2, low, 0.0))).astype(bf16)
 
 
-def sums_kernel(core_ref, ret_ref, sec_ref, keep_ref, send_ref, table_ref, tail_ref, hi_ref, lo_ref):
-    rows = ret_ref.shape[0]
+def sums_kernel(
+    core_ref, ret_hbm, sec_hbm, keep_ref, send_ref, table_ref, tail_ref,
+    sec_ref, ret_ref, left_ref, acc_ref, sec_sem, tail_sem, ret_sems,
+):
+    rows, _ = ret_hbm.shape
+    chunks, wide = ret_ref.shape[0], ret_ref.shape[2]
+    height = rows + 16
+    sec_copy = pltpu.make_async_copy(sec_hbm, sec_ref, sec_sem)
+    sec_copy.start()
+    copies = []
+    for c in range(chunks):
+        copy = pltpu.make_async_copy(
+            ret_hbm.at[:, pl.ds(c * wide, wide)], ret_ref.at[c], ret_sems.at[c]
+        )
+        copy.start()
+        copies.append(copy)
+    tail_copy = pltpu.make_async_copy(ret_hbm.at[pl.ds(rows - W, W)], tail_ref, tail_sem)
+    tail_copy.start()
     core = core_ref[0]
-    label = lax.broadcasted_iota(jnp.int32, table_ref.shape, 0)
-    label = (label + core * HALF) & (SECTORS - 1)
-    table_ref[...] = jnp.where(label == sec_ref[...], 1.0, 0.0).astype(bf16)
-    value = ret_ref[...]
-    hi, lo = split2(value)
-    hi_ref[:rows] = hi
-    lo_ref[:rows] = lo
-    hi_ref[rows:] = jnp.ones_like(hi_ref[rows:])
-    lo_ref[rows:] = jnp.zeros_like(lo_ref[rows:])
-    tail_ref[...] = ret_ref[rows - W :]
-    acc = dot_nt(hi_ref[...], table_ref[...]) + dot_nt(lo_ref[...], table_ref[...])
-    keep_ref[...] = acc[: rows + 8, :HALF]
-    send_ref[...] = acc[: rows + 8, HALF:]
+    left_ref[rows:height] = jnp.ones((16, wide), bf16)
+    left_ref[height + rows :] = jnp.zeros((16, wide), bf16)
+    sec_copy.wait()
+    for c in range(chunks):
+        cols = slice(c * wide, (c + 1) * wide)
+        label = lax.broadcasted_iota(jnp.int32, (SECTORS, wide), 0)
+        label = (label + core * HALF) & (SECTORS - 1)
+        table_ref[:, cols] = jnp.where(label == sec_ref[:, cols], 1.0, 0.0).astype(bf16)
+    for c in range(chunks):
+        copies[c].wait()
+        hi, lo = split2(ret_ref[c])
+        left_ref[:rows] = hi
+        left_ref[height : height + rows] = lo
+        part = dot_nt(left_ref[...], table_ref[:, c * wide : (c + 1) * wide])
+        part = part[: rows + 8] + part[height : height + rows + 8]
+        if c == 0:
+            acc_ref[...] = part
+        elif c < chunks - 1:
+            acc_ref[...] += part
+        else:
+            part = acc_ref[...] + part
+            keep_ref[...] = part[:, :HALF]
+            send_ref[...] = part[:, HALF:]
+    tail_copy.wait()
 
 
 def sector_sums(core, returns, sector):
     rows, width = returns.shape
+    chunks = 4
+    wide = width // chunks
     half = jax.ShapeDtypeStruct((rows + 8, HALF), f32)
+    hbm = pl.BlockSpec(memory_space=pltpu.HBM)
     return pl.pallas_call(
         sums_kernel,
         out_shape=(
@@ -72,13 +102,17 @@
             jax.ShapeDtypeStruct((SECTORS, width), bf16),
             jax.ShapeDtypeStruct((W, width), f32),
         ),
-        in_specs=[
-            pl.BlockSpec(memory_space=pltpu.SMEM),
-            pl.BlockSpec(memory_space=pltpu.VMEM),
-            pl.BlockSpec(memory_space=pltpu.VMEM),
+        in_specs=[pl.BlockSpec(memory_space=pltpu.SMEM), hbm, hbm],
+        out_specs=[pl.BlockSpec(memory_space=pltpu.VMEM)] * 4,
+        scratch_shapes=[
+            pltpu.VMEM((1, width), jnp.int32),
+            pltpu.VMEM((chunks, rows, wide), f32),
+            pltpu.VMEM((2 * rows + 32, wide), bf16),
+            pltpu.VMEM((rows + 8, SECTORS), f32),
+            pltpu.SemaphoreType.DMA,
+            pltpu.SemaphoreType.DMA,
+            pltpu.SemaphoreType.DMA((chunks,)),
         ],
-        out_specs=[pl.BlockSpec(memory_space=pltpu.VMEM)] * 4,
-        scratch_shapes=[pltpu.VMEM((rows + 16, width), bf16)] * 2,
         compiler_params=pltpu.CompilerParams(vmem_limit_bytes=24 * MIB),
         cost_estimate=pl.CostEstimate(
             flops=4 * rows * width * SECTORS, bytes_accessed=8 * rows * width, transcendentals=0
@@ -168,7 +202,7 @@
     )
 
 
-def sector_rows(means, inv, groups, starts, hi_ref, lo_ref, out):
+def sector_rows(means, inv, groups, starts, hi_ref, lo_ref, out, kept=None):
     row = lax.broadcasted_iota(jnp.int32, (8, LANES), 0)
     first, second = Window(), Window()
     mean_parts, gain_parts = [], []
@@ -180,9 +214,7 @@
             mean_f = total * scale
             mean_parts.append(mean_f)
             gain_parts.append(1.0 / (squares * scale - mean_f * mean_f + ridge_rate))
-    for start, parts in zip(starts, (means, mean_parts, gain_parts)):
-        if start is None:
-            continue
+    for start, parts in zip(starts, (means[:kept], mean_parts, gain_parts)):
         for pair in range(0, len(parts), 2):
             hi, lo = split2(jnp.concatenate(parts[pair : pair + 2], axis=0))
             here = slice(start + pair * 8, start + pair * 8 + 16)
@@ -190,9 +222,35 @@
             lo_ref[here, out] = lo
 
 
+def pipelined(left_hi, left_lo, table_ref, buffers, work):
+    even, odd = buffers
+    wide = even.shape[1]
+    chunks = table_ref.shape[1] // wide
+
+    def fill(buffer, index):
+        cols = pl.ds(pl.multiple_of(index * wide, wide), wide)
+        buffer[...] = dot_nn(left_hi[...], table_ref[:, cols]) + dot_nn(
+            left_lo[...], table_ref[:, cols]
+        )
+
+    fill(even, 0)
+
+    def pair(j, _):
+        fill(odd, 2 * j + 1)
+        work(even, 2 * j)
+        fill(even, 2 * j + 2)
+        work(odd, 2 * j + 1)
+        return 0
+
+    lax.fori_loop(0, chunks // 2 - 1, pair, 0)
+    fill(odd, chunks - 1)
+    work(even, chunks - 2)
+    work(odd, chunks - 1)
+
+
 def main_kernel(
     own_ref, other_ref, own_tail_ref, other_tail_ref, ret_ref, mean_ref, crr_ref, table_ref,
-    var_ref, factor_ref, colsum_ref, hi_ref, lo_ref, spread_ref,
+    var_ref, factor_ref, colsum_ref, hi_ref, lo_ref, even_ref, odd_ref,
 ):
     rows = ret_ref.shape[0]
     main = rows - W
@@ -210,13 +268,9 @@
             slice(tile * LANES, (tile + 1) * LANES),
         )
     row = lax.broadcasted_iota(jnp.int32, (8, LANES), 0)
-    wide = spread_ref.shape[1]
-
-    def chunk(index, _):
-        outer = pl.ds(pl.multiple_of(index * wide, wide), wide)
-        spread_ref[...] = dot_nn(hi_ref[...], table_ref[:, outer]) + dot_nn(
-            lo_ref[...], table_ref[:, outer]
-        )
+    wide = even_ref.shape[1]
+
+    def chunk(spread_ref, index):
         for tile in range(wide // LANES):
             inner = slice(tile * LANES, (tile + 1) * LANES)
             cols = pl.ds(pl.multiple_of(index * wide + tile * LANES, LANES), LANES)
@@ -236,15 +290,14 @@
                     var_ref[rows_of(g), cols] = (1.0 - shrink_weight) * variance
                     total = total + variance
             colsum_ref[:, cols] = total
-        return 0
-
-    lax.fori_loop(0, ret_ref.shape[1] // wide, chunk, 0)
+
+    pipelined(hi_ref, lo_ref, table_ref, (even_ref, odd_ref), chunk)
 
 
 def head_kernel(
     info_ref, own_ref, other_ref, counts_own_ref, counts_other_ref, prior_own_ref, prior_other_ref,
     halo_ref, ret_ref, factor_ref, mean_ref, crr_ref, colsum_ref, table_ref,
-    var_ref, totals_ref, hi_ref, lo_ref, spread_ref, inv_ref, parts_ref,
+    var_ref, totals_ref, hi_ref, lo_ref, even_ref, odd_ref, inv_ref, parts_ref,
 ):
     blocks = W // 8
     inverse_counts(info_ref[1], inv_ref)
@@ -262,17 +315,13 @@
             for g in range(2 * blocks)
         ]
         sector_rows(
-            means, lambda g: inv_ref[rows_of(g)], 2 * blocks, (0, 2 * W, 3 * W), hi_ref, lo_ref,
-            slice(tile * LANES, (tile + 1) * LANES),
+            means, lambda g: inv_ref[rows_of(g)], 2 * blocks, (0, W, 2 * W), hi_ref, lo_ref,
+            slice(tile * LANES, (tile + 1) * LANES), blocks,
         )
     row = lax.broadcasted_iota(jnp.int32, (8, LANES), 0)
-    wide = spread_ref.shape[1]
-
-    def chunk(index, _):
-        outer = pl.ds(pl.multiple_of(index * wide, wide), wide)
-        spread_ref[...] = dot_nn(hi_ref[...], table_ref[:, outer]) + dot_nn(
-            lo_ref[...], table_ref[:, outer]
-        )
+    wide = even_ref.shape[1]
+
+    def chunk(spread_ref, index):
         for tile in range(wide // LANES):
             inner = slice(tile * LANES, (tile + 1) * LANES)
             cols = pl.ds(pl.multiple_of(index * wide + tile * LANES, LANES), LANES)
@@ -286,8 +335,8 @@
                     product = ret_ref[rows_of(g), cols] * factor_ref[rows_of(g), cols]
                 product = cross.push(product, row)
                 if g >= 0:
-                    mean_f = spread_ref[rows_of(2 * blocks + g), inner]
-                    gain = spread_ref[rows_of(3 * blocks + g), inner]
+                    mean_f = spread_ref[rows_of(blocks + g), inner]
+                    gain = spread_ref[rows_of(2 * blocks + g), inner]
                     crf = product * inv_ref[rows_of(g)] - mean_ref[rows_of(g), cols] * mean_f
                     variance = crr_ref[rows_of(g), cols] - crf * crf * gain
                     var_ref[rows_of(g), cols] = (1.0 - shrink_weight) * variance
@@ -297,9 +346,8 @@
             parts_ref[:, cols] = jnp.concatenate(
                 [hi, mid, total - hi - mid, jnp.zeros_like(hi)], axis=0
             ).astype(bf16)
-        return 0
-
-    lax.fori_loop(0, ret_ref.shape[1] // wide, chunk, 0)
+
+    pipelined(hi_ref, lo_ref, table_ref, (even_ref, odd_ref), chunk)
     total = jnp.sum(dot_nt(parts_ref[...], table_ref[...]), axis=0, keepdims=True)
     swapped = jnp.concatenate([total[:, HALF:], total[:, :HALF]], axis=1)
     total = jnp.where(info_ref[0] == 0, total, swapped)
@@ -327,47 +375,41 @@
 
 
 def shrink_kernel(
-    all_steps, core_ref, parts_ref, cown_ref, cother_ref, table_ref, head_ref, main_ref, out_ref, pooled_ref
+    all_steps, core_ref, parts_ref, cown_ref, cother_ref, table_ref, head_ref, main_ref, out_hbm, out_ref, sems
 ):
-    step = pl.program_id(0)
-
-    @pl.when(step == 0)
-    def _():
-        total = jnp.sum(parts_ref[...], axis=0, keepdims=True)
-        swapped = jnp.concatenate([total[:, HALF:], total[:, :HALF]], axis=1)
-        total = jnp.where(core_ref[0] == 0, total, swapped)
-        count = jnp.concatenate([cown_ref[W : W + 1], cother_ref[W : W + 1]], axis=1)
-        mean = total / (all_steps * jnp.maximum(count, 1.0))
-        spread = dot_nn(split3_rows(shrink_weight * mean), table_ref[...])
-        pooled_ref[...] = jnp.broadcast_to(
-            jnp.sum(spread, axis=0, keepdims=True), pooled_ref.shape
-        )
-        out_ref[...] = head_ref[...] + pooled_ref[0:1]
-
-    @pl.when(step > 0)
-    def _():
-        out_ref[...] = main_ref[...] + pooled_ref[0:1]
+    total = jnp.sum(parts_ref[...], axis=0, keepdims=True)
+    swapped = jnp.concatenate([total[:, HALF:], total[:, :HALF]], axis=1)
+    total = jnp.where(core_ref[0] == 0, total, swapped)
+    count = jnp.concatenate([cown_ref[W : W + 1], cother_ref[W : W + 1]], axis=1)
+    mean = total / (all_steps * jnp.maximum(count, 1.0))
+    left = split3_rows(shrink_weight * mean)
+    chunks, _, wide = out_ref.shape
+    copies = []
+    for c in range(chunks):
+        cols = slice(c * wide, (c + 1) * wide)
+        pooled = jnp.sum(dot_nn(left, table_ref[:, cols]), axis=0, keepdims=True)
+        out_ref[c, :W] = head_ref[:, cols] + pooled
+        out_ref[c, W:] = main_ref[:, cols] + pooled
+        copy = pltpu.make_async_copy(out_ref.at[c], out_hbm.at[:, pl.ds(c * wide, wide)], sems.at[c])
+        copy.start()
+        copies.append(copy)
+    for copy in copies:
+        copy.wait()
 
 
 def shrink(all_steps, core, parts, own, other, table, head, main):
     width = head.shape[1]
     rows = head.shape[0] + main.shape[0]
-    fixed = lambda a: pl.BlockSpec(a.shape, lambda i: (0, 0))
+    chunks = 4
     return pl.pallas_call(
         functools.partial(shrink_kernel, float(all_steps)),
-        grid=(rows // W,),
         out_shape=jax.ShapeDtypeStruct((rows, width), f32),
-        in_specs=[
-            SMEM,
-            fixed(parts),
-            fixed(own),
-            fixed(other),
-            fixed(table),
-            fixed(head),
-            pl.BlockSpec((W, width), lambda i: (jnp.maximum(i - 1, 0), 0)),
+        in_specs=[SMEM] + [VMEM] * 6,
+        out_specs=pl.BlockSpec(memory_space=pltpu.HBM),
+        scratch_shapes=[
+            pltpu.VMEM((chunks, rows, width // chunks), f32),
+            pltpu.SemaphoreType.DMA((chunks,)),
         ],
-        out_specs=pl.BlockSpec((W, width), lambda i: (i, 0)),
-        scratch_shapes=[pltpu.VMEM((8, width), f32)],
         compiler_params=pltpu.CompilerParams(vmem_limit_bytes=24 * MIB),
         cost_estimate=pl.CostEstimate(
             flops=2 * rows * width, bytes_accessed=8 * rows * width, transcendentals=0
@@ -421,15 +463,16 @@
     var, factor, colsum = kernel_call(
         main_kernel, [(main, width), (W, width), (8, width)], [],
         [own, other, own_tail, other_tail, returns, mean, crr, table],
-        scratch=[pltpu.VMEM((lhs, SECTORS), bf16)] * 2 + [pltpu.VMEM((lhs, wide), f32)],
+        scratch=[pltpu.VMEM((lhs, SECTORS), bf16)] * 2 + [pltpu.VMEM((lhs, wide), f32)] * 2,
         flops=4 * lhs * width * SECTORS, moved=12 * rows * width,
     )
     var_head, totals = kernel_call(
         head_kernel, [(W, width), (n_time * n_series, SECTORS)], [info],
         [own, other, own_tail, other_tail, prior_own, prior_other, halo, returns, factor,
          mean_head, crr_head, colsum, table],
-        scratch=[pltpu.VMEM((4 * W, SECTORS), bf16)] * 2
-        + [pltpu.VMEM((4 * W, wide), f32), pltpu.VMEM((W, LANES), f32), pltpu.VMEM((32, width), bf16)],
+        scratch=[pltpu.VMEM((3 * W, SECTORS), bf16)] * 2
+        + [pltpu.VMEM((3 * W, wide), f32)] * 2
+        + [pltpu.VMEM((W, LANES), f32), pltpu.VMEM((32, width), bf16)],
         flops=16 * W * width * SECTORS, moved=12 * W * width,
     )
     parts = lax.all_to_all(totals, ("tm", "series"), 0, 0)

time: 53 us -> 51.8 us (0.977)
  Pallas kernels: 17.7 us -> 16.6 us
    pallas_call x4, Pallas kernels: 12.7 us -> 11.7 us  [kernel_of(): pl.pallas_call(body, out_shape=tuple((jax.ShapeDtypeStruct(shape, f32) fo...]
    pallas_call x1, Pallas kernels: 2.81 us -> 2.11 us  [shrink(): pl.pallas_call(functools.partial(shrink_kernel, float(all_steps)), out_sh...]
    pallas_call x1, Pallas kernels: 2.18 us -> 2.8 us  [sector_sums(): pl.pallas_call(sums_kernel, out_shape=(half, half, jax.ShapeDtypeStruct((...]
where the time goes in v3:
time: 51.8 us; the launch traced here: 51.6 us
  Pallas kernels  16.6 us (32%)
  blocking collectives  13.4 us (26%)
  starting transfers between devices  12.7 us (25%)
  waiting for transfers between devices  6.22 us (12%)
  local copies, waits for them, and re-layouts  2.36 us (5%)
    all_to_all x1, blocking collectives, step(): parts = lax.all_to_all(totals, ('tm', 'series'), 0, 0)  13.4 us
    pallas_call x4, Pallas kernels, kernel_of(): pl.pallas_call(body, out_shape=tuple((jax.ShapeDtypeStruct(shape, f32) fo...  11.7 us
    ppermute x2, starting transfers between devices, ahead(): lax.ppermute(value, axis, [(i, i + 1) for i in range(lax.axis_size(axis)...  7.13 us
    ppermute x6, waiting for transfers between devices, swap(): lax.ppermute(value, axis, [(i, i ^ bit) for i in range(lax.axis_size(axis...  5.85 us
    ppermute x6, starting transfers between devices, swap(): lax.ppermute(value, axis, [(i, i ^ bit) for i in range(lax.axis_size(axis...  5.6 us
    pallas_call x1, Pallas kernels, sector_sums(): pl.pallas_call(sums_kernel, out_shape=(half, half, jax.ShapeDtypeStruct((...  2.8 us
    unnamed x7, local copies, waits for them, and re-layouts  2.3 us
    pallas_call x1, Pallas kernels, shrink(): pl.pallas_call(functools.partial(shrink_kernel, float(all_steps)), out_sh...  2.11 us
  transfers between devices with their start and end apart: 8, of which 4 were waited for; matrix products, arithmetic and copies ran while one was open for 0% of the time, Pallas kernels for 16%

profile of v3, /device:TPU:0, one launch (start us, length us, event | category | flops | bytes accessed | tf_op | source)
XLA Modules:
  0.0 51.6 jit_solution(13513047341176532127)
XLA Ops:
  0.0 0.1 pad_add_fusion.core_ref.info_ref
  0.1 0.0 copy-start
  0.1 1.6 %copy-done = f32[256,2048]{1,0:T(8,128)S(1)} copy-done((f32[256,2048]{1,0:T(8,128)S(1)}, f32[256,2048]{1,0:T(8,128)}, u32[]{:S(2)}) %copy-start) | copy-done | bytes 2097176
  1.7 0.0 copy-start.2
  1.7 0.7 %copy-done.2 = s32[2048]{0:T(1024)S(1)} copy-done((s32[2048]{0:T(1024)S(1)}, s32[2048]{0:T(1024)}, u32[]{:S(2)}) %copy-start.2) | copy-done | bytes 8216
  2.4 0.0 copy-start.1
  2.4 2.8 %sector_sums.1 = (f32[264,256]{1,0:T(8,128)S(1)}, f32[264,256]{1,0:T(8,128)S(1)}, bf16[512,2048]{1,0:T(8,128)(2,1)S(1)}, f32[64,2048]{1,0:T(8,128)S(1)}) custom-call(s32[2]{0:T(128)S(1)} %pad_add_fusion.core_ref.info_ref, f32[256,2048]{1,0:T(8,128)S(1)} %copy-done, s32[1,2048]{1,0:T(1,128)S(1)} %bitcast.9), custom_call_target="tpu_custom_call" | custom-call | flops 1073741824 | bytes 4194304 | tf_op jit(solution)/shard_map/sector_sums/pallas_call | solution.py:97
  5.2 0.6 %collective-permute-start = (f32[264,256]{1,0:T(8,128)S(1)}, f32[264,256]{1,0:T(8,128)S(1)}, u32[]{:S(2)}, u32[]{:S(2)}) collective-permute-start(f32[264,256]{1,0:T(8,128)S(1)} %get-tuple-element.19), channel_id=1, source_target_pairs={{0,1},{1,0},{2,3},{3,2},{4,5},{5,4},{6,7},{7,6},{8,9},{9,8},{10,11... | collective-permute-start | bytes 811016 | tf_op jit(solution)/shard_map/ppermute | solution.py:422
  5.7 1.2 %collective-permute-done = f32[264,256]{1,0:T(8,128)S(1)} collective-permute-done((f32[264,256]{1,0:T(8,128)S(1)}, f32[264,256]{1,0:T(8,128)S(1)}, u32[]{:S(2)}, u32[]{:S(2)}) %collective-permute-start) | collective-permute-done | bytes 270368 | tf_op jit(solution)/shard_map/ppermute | solution.py:422
  6.9 2.9 %collective-permute-start.1 = (f32[192,256]{1,0:T(8,128)S(1)}, f32[192,256]{1,0:T(8,128)S(1)}, u32[]{:S(2)}, u32[]{:S(2)}) collective-permute-start(f32[192,256]{1,0:T(8,128)S(1)} %slice_add_fusion), channel_id=1, source_target_pairs={{0,2},{1,3},{2,0},{3,1},{4,6},{5,7},{6,4},{7,5},{8,10},{9,11},{10,... | collective-permute-start | bytes 589832 | tf_op jit(solution)/shard_map/ppermute | solution.py:422
  9.9 3.5 %collective-permute-start.7 = (f32[64,2048]{1,0:T(8,128)S(1)}, f32[64,2048]{1,0:T(8,128)S(1)}, u32[]{:S(2)}, u32[]{:S(2)}) collective-permute-start(f32[64,2048]{1,0:T(8,128)S(1)} %get-tuple-element.20), channel_id=1, source_target_pairs={{0,4},{4,8},{8,12},{12,16},{16,20},{20,24},{24,28},{1,5},{5,9},{9,... | collective-permute-start | bytes 1572872 | tf_op jit(solution)/shard_map/ppermute | solution.py:426
  13.3 1.7 %collective-permute-done.1 = f32[192,256]{1,0:T(8,128)S(1)} collective-permute-done((f32[192,256]{1,0:T(8,128)S(1)}, f32[192,256]{1,0:T(8,128)S(1)}, u32[]{:S(2)}, u32[]{:S(2)}) %collective-permute-start.1) | collective-permute-done | bytes 196640 | tf_op jit(solution)/shard_map/ppermute | solution.py:422
  15.1 0.1 collective-permute-start.2
  15.2 1.8 %collective-permute-start.3 = (f32[72,256]{1,0:T(8,128)S(1)}, f32[72,256]{1,0:T(8,128)S(1)}, u32[]{:S(2)}, u32[]{:S(2)}) collective-permute-start(f32[72,256]{1,0:T(8,128)S(1)} %slice_add_fusion.1), channel_id=1, source_target_pairs={{0,2},{1,3},{2,0},{3,1},{4,6},{5,7},{6,4},{7,5},{8,10},{9,11},{10,... | collective-permute-start | bytes 221192 | tf_op jit(solution)/shard_map/ppermute | solution.py:422
  17.0 2.9 %collective-permute-done.3 = f32[72,256]{1,0:T(8,128)S(1)} collective-permute-done((f32[72,256]{1,0:T(8,128)S(1)}, f32[72,256]{1,0:T(8,128)S(1)}, u32[]{:S(2)}, u32[]{:S(2)}) %collective-permute-start.3) | collective-permute-done | bytes 73760 | tf_op jit(solution)/shard_map/ppermute | solution.py:422
  19.9 3.7 %collective-permute-start.5 = (f32[72,256]{1,0:T(8,128)S(1)}, f32[72,256]{1,0:T(8,128)S(1)}, u32[]{:S(2)}, u32[]{:S(2)}) collective-permute-start(f32[72,256]{1,0:T(8,128)S(1)} %add.20.own_tail_ref.counts_own_ref.cown_ref), channel_id=1, source_target_pairs={{0,4},{4,8},{8,12},{12,16},{16,20},{20,24},{24,28},{1,5},{5,9},{9,... | collective-permute-start | bytes 221192 | tf_op jit(solution)/shard_map/ppermute | solution.py:426
  23.6 0.1 collective-permute-start.4
  23.7 0.0 copy-done.1
  23.7 2.0 %shard_map.28 = (f32[192,2048]{1,0:T(8,128)S(1)}, f32[192,2048]{1,0:T(8,128)S(1)}) custom-call(f32[256,2048]{1,0:T(8,128)S(1)} %copy-done.1), custom_call_target="tpu_custom_call" | custom-call | flops 15728640 | bytes 4718592 | tf_op jit(solution)/shard_map/pallas_call | solution.py:366
  25.7 0.4 collective-permute-done.5.prior_own_ref
  26.0 0.2 collective-permute-start.6
  26.2 0.0 collective-permute-done.7.halo_ref
  26.2 1.6 %shard_map.30 = (f32[64,2048]{1,0:T(8,128)S(1)}, f32[64,2048]{1,0:T(8,128)S(1)}) custom-call(s32[2]{0:T(128)S(1)} %pad_add_fusion.core_ref.info_ref, f32[64,2048]{1,0:T(8,128)S(1)} %collective-permute-done.7.halo_ref, f32[256,2048]{1,0:T(8,128)S(1)} %copy-done.1), custom_call_target="tpu_custom_call" | custom-call | flops 5242880 | bytes 1572864 | tf_op jit(solution)/shard_map/pallas_call | solution.py:366
  27.8 0.0 collective-permute-done.4.other_tail_ref.counts_other_ref.cother_ref
  27.8 0.0 collective-permute-done.2.other_ref
  27.8 4.9 %shard_map.29 = (f32[192,2048]{1,0:T(8,128)S(1)}, f32[64,2048]{1,0:T(8,128)S(1)}, f32[8,2048]{1,0:T(8,128)S(1)}) custom-call(f32[192,256]{1,0:T(8,128)S(1)} %add.18.own_ref, f32[192,256]{1,0:T(8,128)S(1)} %collective-permute-done.2.other_ref, f32[72,256]{1,0:T(8,128)S(1)} %add.20.own_tail_ref.counts_own_ref.cown_ref, ...), custom_call_target="tpu_custom_call" | custom-call | flops 2684354560 | bytes 6291456 | tf_op jit(solution)/shard_map/pallas_call | solution.py:366
  32.7 0.0 collective-permute-done.6.prior_other_ref
  32.7 3.3 %shard_map.31 = (f32[64,2048]{1,0:T(8,128)S(1)}, f32[32,512]{1,0:T(8,128)S(1)}) custom-call(s32[2]{0:T(128)S(1)} %pad_add_fusion.core_ref.info_ref, f32[192,256]{1,0:T(8,128)S(1)} %add.18.own_ref, f32[192,256]{1,0:T(8,128)S(1)} %collective-permute-done.2.other_ref, f32[72,256]{1,0:T(8,128)S(1)} %add.20.own_tail_ref.counts_own_ref.cown_ref, ...), custom_call_target="tpu_custom_call" | custom-call | flops 1073741824 | bytes 1572864 | tf_op jit(solution)/shard_map/pallas_call | solution.py:366
  36.0 0.1 copy.3
  36.1 13.4 %all_to_all.11 = f32[32,1,512]{2,1,0:T(1,128)S(1)} all-to-all(f32[32,1,512]{2,1,0:T(1,128)S(1)} %copy.3), channel_id=1, replica_groups=mesh['tm'=8,'series'=4] {'tm','series'}, dimensions={0} | all-to-all | bytes 131072 | tf_op jit(solution)/shard_map/all_to_all | solution.py:478
  49.5 2.1 %shrink.1 = f32[256,2048]{1,0:T(8,128)} custom-call(s32[2]{0:T(128)S(1)} %pad_add_fusion.core_ref.info_ref, f32[32,512]{1,0:T(8,128)S(1)} %bitcast.7, f32[72,256]{1,0:T(8,128)S(1)} %add.20.own_tail_ref.counts_own_ref.cown_ref, f32[72,256]{1,0:T(8,128)S(1)} %collective-permute-done.4.other_tail_ref.counts_other_ref.cother_ref, ...), custom_call_target="tpu_custom_call" | custom-call | flops 1048576 | bytes 4194304 | tf_op jit(solution)/shard_map/shrink/pallas_call | solution.py:404
  (5 shorter events, 0.1 us)
Async XLA Ops:
  0.1 1.6 %copy-start = (f32[256,2048]{1,0:T(8,128)S(1)}, f32[256,2048]{1,0:T(8,128)}, u32[]{:S(2)}) copy-start(f32[256,2048]{1,0:T(8,128)} %ret_ref.7) | copy-start | bytes 6291460
  1.7 0.7 %copy-start.2 = (s32[2048]{0:T(1024)S(1)}, s32[2048]{0:T(1024)}, u32[]{:S(2)}) copy-start(s32[2048]{0:T(1024)} %param.3) | copy-start | bytes 24580
  2.4 21.3 %copy-start.1 = (f32[256,2048]{1,0:T(8,128)S(1)}, f32[256,2048]{1,0:T(8,128)}, u32[]{:S(2)}) copy-start(f32[256,2048]{1,0:T(8,128)} %ret_ref.7) | copy-start | bytes 6291460
  5.2 1.7 %collective-permute-start = (f32[264,256]{1,0:T(8,128)S(1)}, f32[264,256]{1,0:T(8,128)S(1)}, u32[]{:S(2)}, u32[]{:S(2)}) collective-permute-start(f32[264,256]{1,0:T(8,128)S(1)} %get-tuple-element.19), channel_id=1, source_target_pairs={{0,1},{1,0},{2,3},{3,2},{4,5},{5,4},{6,7},{7,6},{8,9},{9,8},{10,11... | collective-permute-start | bytes 811016 | tf_op jit(solution)/shard_map/ppermute | solution.py:422
  6.9 8.1 %collective-permute-start.1 = (f32[192,256]{1,0:T(8,128)S(1)}, f32[192,256]{1,0:T(8,128)S(1)}, u32[]{:S(2)}, u32[]{:S(2)}) collective-permute-start(f32[192,256]{1,0:T(8,128)S(1)} %slice_add_fusion), channel_id=1, source_target_pairs={{0,2},{1,3},{2,0},{3,1},{4,6},{5,7},{6,4},{7,5},{8,10},{9,11},{10,... | collective-permute-start | bytes 589832 | tf_op jit(solution)/shard_map/ppermute | solution.py:422
  9.9 16.4 %collective-permute-start.7 = (f32[64,2048]{1,0:T(8,128)S(1)}, f32[64,2048]{1,0:T(8,128)S(1)}, u32[]{:S(2)}, u32[]{:S(2)}) collective-permute-start(f32[64,2048]{1,0:T(8,128)S(1)} %get-tuple-element.20), channel_id=1, source_target_pairs={{0,4},{4,8},{8,12},{12,16},{16,20},{20,24},{24,28},{1,5},{5,9},{9,... | collective-permute-start | bytes 1572872 | tf_op jit(solution)/shard_map/ppermute | solution.py:426
  15.1 12.7 %collective-permute-start.2 = (f32[192,256]{1,0:T(8,128)S(1)}, f32[192,256]{1,0:T(8,128)S(1)}, u32[]{:S(2)}, u32[]{:S(2)}) collective-permute-start(f32[192,256]{1,0:T(8,128)S(1)} %add.18.own_ref), channel_id=1, source_target_pairs={{0,1},{1,0},{2,3},{3,2},{4,5},{5,4},{6,7},{7,6},{8,9},{9,8},{10,11... | collective-permute-start | bytes 589832 | tf_op jit(solution)/shard_map/ppermute | solution.py:422
  15.2 4.7 %collective-permute-start.3 = (f32[72,256]{1,0:T(8,128)S(1)}, f32[72,256]{1,0:T(8,128)S(1)}, u32[]{:S(2)}, u32[]{:S(2)}) collective-permute-start(f32[72,256]{1,0:T(8,128)S(1)} %slice_add_fusion.1), channel_id=1, source_target_pairs={{0,2},{1,3},{2,0},{3,1},{4,6},{5,7},{6,4},{7,5},{8,10},{9,11},{10,... | collective-permute-start | bytes 221192 | tf_op jit(solution)/shard_map/ppermute | solution.py:422
  19.9 6.1 %collective-permute-start.5 = (f32[72,256]{1,0:T(8,128)S(1)}, f32[72,256]{1,0:T(8,128)S(1)}, u32[]{:S(2)}, u32[]{:S(2)}) collective-permute-start(f32[72,256]{1,0:T(8,128)S(1)} %add.20.own_tail_ref.counts_own_ref.cown_ref), channel_id=1, source_target_pairs={{0,4},{4,8},{8,12},{12,16},{16,20},{20,24},{24,28},{1,5},{5,9},{9,... | collective-permute-start | bytes 221192 | tf_op jit(solution)/shard_map/ppermute | solution.py:426
  23.6 4.2 %collective-permute-start.4 = (f32[72,256]{1,0:T(8,128)S(1)}, f32[72,256]{1,0:T(8,128)S(1)}, u32[]{:S(2)}, u32[]{:S(2)}) collective-permute-start(f32[72,256]{1,0:T(8,128)S(1)} %add.20.own_tail_ref.counts_own_ref.cown_ref), channel_id=1, source_target_pairs={{0,1},{1,0},{2,3},{3,2},{4,5},{5,4},{6,7},{7,6},{8,9},{9,8},{10,11... | collective-permute-start | bytes 221192 | tf_op jit(solution)/shard_map/ppermute | solution.py:422
  26.0 6.7 %collective-permute-start.6 = (f32[72,256]{1,0:T(8,128)S(1)}, f32[72,256]{1,0:T(8,128)S(1)}, u32[]{:S(2)}, u32[]{:S(2)}) collective-permute-start(f32[72,256]{1,0:T(8,128)S(1)} %collective-permute-done.5.prior_own_ref), channel_id=1, source_target_pairs={{0,1},{1,0},{2,3},{3,2},{4,5},{5,4},{6,7},{7,6},{8,9},{9,8},{10,11... | collective-permute-start | bytes 221192 | tf_op jit(solution)/shard_map/ppermute | solution.py:422

commit v4 on v3

v4 whole, which is shorter than its diff:
```python
import functools

import jax
import jax.numpy as jnp
from jax import lax
from jax.experimental import pallas as pl
from jax.experimental.pallas import tpu as pltpu
from jax.sharding import PartitionSpec as P


W = 64
SECTORS = 512
HALF = SECTORS // 2
LANES = 128

ridge_rate = 0.05
shrink_weight = 0.3

f32 = jnp.float32
bf16 = jnp.bfloat16
MIB = 1024 * 1024


def dot_nn(a, b):
    return lax.dot_general(a, b, (((1,), (0,)), ((), ())), preferred_element_type=f32)


def dot_nt(a, b):
    return lax.dot_general(a, b, (((1,), (1,)), ((), ())), preferred_element_type=f32)


def split2(x):
    hi = x.astype(bf16)
    return hi, (x - hi.astype(f32)).astype(bf16)


def split3_rows(x):
    hi = x.astype(bf16).astype(f32)
    rest = x - hi
    mid = rest.astype(bf16).astype(f32)
    low = rest - mid
    row = lax.broadcasted_iota(jnp.int32, (16, x.shape[1]), 0)
    return jnp.where(row == 0, hi, jnp.where(row == 1, mid, jnp.where(row == 2, low, 0.0))).astype(bf16)


def table_kernel(ret_hbm, sec_ref, core_ref, first_ref, table_ref, ret_ref, flip_ref, inv_ref, sem):
    copy = pltpu.make_async_copy(ret_hbm, ret_ref, sem)
    copy.start()
    wide = 4 * LANES
    flip_ref[...] = jnp.concatenate([core_ref[...]] * (SECTORS // LANES), axis=1)
    position = lax.broadcasted_iota(jnp.int32, inv_ref.shape, 0) + (first_ref[0:1] + 1)
    inv_ref[...] = 1.0 / jnp.minimum(position, W).astype(f32)
    for c in range(table_ref.shape[1] // wide):
        cols = slice(c * wide, (c + 1) * wide)
        label = lax.broadcasted_iota(jnp.int32, (SECTORS, wide), 0)
        table_ref[:, cols] = jnp.where(label == sec_ref[:, cols], 1.0, 0.0).astype(bf16)
    copy.wait()


def sums_kernel(ret_ref, table_ref, keep_ref, send_ref, tail_ref, left_ref):
    rows, width = ret_ref.shape
    height = rows + 16
    hi, lo = split2(ret_ref[...])
    left_ref[:rows] = hi
    left_ref[rows:height] = jnp.ones((16, width), bf16)
    left_ref[height : height + rows] = lo
    left_ref[height + rows :] = jnp.zeros((16, width), bf16)
    tail_ref[...] = ret_ref[rows - W :]
    part = dot_nt(left_ref[...], table_ref[...])
    part = part[: rows + 8] + part[height : height + rows + 8]
    keep_ref[...] = part[:, :HALF]
    send_ref[...] = part[:, HALF:]


class Window:
    def __init__(self):
        self.rolled = {}
        self.sums = {8: [], 16: [], 32: []}

    def push(self, x, row):
        size = 1
        while size < 8:
            turned = pltpu.roll(x, size, 0)
            before = self.rolled.get(size, turned)
            self.rolled[size] = turned
            x = x + jnp.where(row < size, before, turned)
            size *= 2
        while size < W:
            seen = self.sums[size]
            seen.append(x)
            back = size // 8
            if len(seen) <= back:
                return None
            x = x + seen[-1 - back]
            size *= 2
        return x


def tile_at(index):
    return pl.ds(pl.multiple_of(index * LANES, LANES), LANES)


def rows_of(group):
    return slice(group * 8, group * 8 + 8)


def moments_body(load, inv, groups, mean_ref, crr_ref):
    row = lax.broadcasted_iota(jnp.int32, (8, LANES), 0)

    def tile(index, _):
        cols = tile_at(index)
        first, second = Window(), Window()
        for group in range(groups):
            ret = load(group, cols)
            total, squares = first.push(ret, row), second.push(ret * ret, row)
            if group >= W // 8:
                here = rows_of(group - W // 8)
                scale = inv(group - W // 8)
                mean = total * scale
                mean_ref[here, cols] = mean
                crr_ref[here, cols] = squares * scale - mean * mean
        return 0

    lax.fori_loop(0, mean_ref.shape[1] // LANES, tile, 0)


def moments_main_kernel(ret_ref, mean_ref, crr_ref):
    moments_body(
        lambda group, cols: ret_ref[rows_of(group), cols],
        lambda group: 1.0 / W,
        ret_ref.shape[0] // 8,
        mean_ref,
        crr_ref,
    )


def moments_head_kernel(inv_ref, halo_ref, ret_ref, mean_ref, crr_ref):
    blocks = W // 8
    moments_body(
        lambda group, cols: halo_ref[rows_of(group), cols]
        if group < blocks
        else ret_ref[rows_of(group - blocks), cols],
        lambda group: inv_ref[rows_of(group)],
        2 * blocks,
        mean_ref,
        crr_ref,
    )


def sector_rows(means, inv, groups, starts, hi_ref, lo_ref, out, kept=None):
    row = lax.broadcasted_iota(jnp.int32, (8, LANES), 0)
    first, second = Window(), Window()
    mean_parts, gain_parts = [], []
    for group in range(groups):
        mean = means[group]
        total, squares = first.push(mean, row), second.push(mean * mean, row)
        if group >= W // 8:
            scale = inv(group - W // 8)
            mean_f = total * scale
            mean_parts.append(mean_f)
            gain_parts.append(1.0 / (squares * scale - mean_f * mean_f + ridge_rate))
    for start, parts in zip(starts, (means[:kept], mean_parts, gain_parts)):
        for pair in range(0, len(parts), 2):
            hi, lo = split2(jnp.concatenate(parts[pair : pair + 2], axis=0))
            here = slice(start + pair * 8, start + pair * 8 + 16)
            hi_ref[here, out] = hi
            lo_ref[here, out] = lo


def pipelined(fill, work, buffers, chunks):
    even, odd = buffers
    fill(even, 0)

    def pair(j, _):
        fill(odd, 2 * j + 1)
        work(even, 2 * j)
        fill(even, 2 * j + 2)
        work(odd, 2 * j + 1)
        return 0

    lax.fori_loop(0, chunks // 2 - 1, pair, 0)
    fill(odd, chunks - 1)
    work(even, chunks - 2)
    work(odd, chunks - 1)


def chunk_at(index, wide):
    return pl.ds(pl.multiple_of(index * wide, wide), wide)


def main_rows(sums_ref, tail_ref, hi_ref, lo_ref):
    main = sums_ref.shape[0]
    rows = main + W
    for tile in range(HALF // LANES):
        cols = slice(tile * LANES, (tile + 1) * LANES)
        scale = 1.0 / jnp.maximum(tail_ref[W : W + 8, cols], 1.0)
        means = [
            (sums_ref[rows_of(g), cols] if g < main // 8 else tail_ref[rows_of(g - main // 8), cols])
            * scale
            for g in range(rows // 8)
        ]
        sector_rows(
            means, lambda g: 1.0 / W, rows // 8, (0, rows, rows + main), hi_ref, lo_ref, cols
        )


def own_kernel(own_ref, own_tail_ref, table_ref, spread_ref, hi_ref, lo_ref):
    main_rows(own_ref, own_tail_ref, hi_ref, lo_ref)
    wide = 2 * LANES

    def chunk(index, _):
        cols = chunk_at(index, wide)
        table = table_ref[:HALF, cols]
        spread_ref[:, cols] = dot_nn(hi_ref[...], table) + dot_nn(lo_ref[...], table)
        return 0

    lax.fori_loop(0, table_ref.shape[1] // wide, chunk, 0)


def main_kernel(
    other_ref, other_tail_ref, spread_ref, ret_ref, mean_ref, crr_ref, table_ref,
    var_ref, factor_ref, colsum_ref, hi_ref, lo_ref, even_ref, odd_ref,
):
    rows = ret_ref.shape[0]
    main = rows - W
    blocks = W // 8
    main_rows(other_ref, other_tail_ref, hi_ref, lo_ref)
    row = lax.broadcasted_iota(jnp.int32, (8, LANES), 0)
    wide = even_ref.shape[1]

    def fill(buffer, index):
        cols = chunk_at(index, wide)
        table = table_ref[HALF:, cols]
        buffer[...] = spread_ref[:, cols] + dot_nn(hi_ref[...], table) + dot_nn(lo_ref[...], table)

    def work(spread_ref, index):
        for tile in range(wide // LANES):
            inner = slice(tile * LANES, (tile + 1) * LANES)
            cols = pl.ds(pl.multiple_of(index * wide + tile * LANES, LANES), LANES)
            cross = Window()
            total = jnp.zeros((8, LANES), f32)
            for group in range(rows // 8):
                factor = spread_ref[rows_of(group), inner]
                if group < blocks:
                    factor_ref[rows_of(group), cols] = factor
                product = cross.push(ret_ref[rows_of(group), cols] * factor, row)
                if group >= blocks:
                    g = group - blocks
                    mean_f = spread_ref[rows_of(rows // 8 + g), inner]
                    gain = spread_ref[rows_of((rows + main) // 8 + g), inner]
                    crf = product * (1.0 / W) - mean_ref[rows_of(g), cols] * mean_f
                    variance = crr_ref[rows_of(g), cols] - crf * crf * gain
                    var_ref[rows_of(g), cols] = (1.0 - shrink_weight) * variance
                    total = total + variance
            colsum_ref[:, cols] = total

    pipelined(fill, work, (even_ref, odd_ref), ret_ref.shape[1] // wide)


def head_kernel(
    inv_ref, flip_ref, own_ref, other_ref, counts_own_ref, counts_other_ref, prior_own_ref, prior_other_ref,
    halo_ref, ret_ref, factor_ref, mean_ref, crr_ref, colsum_ref, table_ref,
    var_ref, totals_ref, hi_ref, lo_ref, even_ref, odd_ref, acc_ref,
):
    blocks = W // 8
    acc_ref[...] = jnp.zeros_like(acc_ref)
    for tile in range(SECTORS // LANES):
        mine = tile < HALF // LANES
        here, prior, counts = (
            (own_ref, prior_own_ref, counts_own_ref)
            if mine
            else (other_ref, prior_other_ref, counts_other_ref)
        )
        cols = pl.ds((tile * LANES) % HALF, LANES)
        scale = 1.0 / jnp.maximum(counts[W : W + 8, cols], 1.0)
        means = [
            (prior[rows_of(g), cols] if g < blocks else here[rows_of(g - blocks), cols]) * scale
            for g in range(2 * blocks)
        ]
        sector_rows(
            means, lambda g: inv_ref[rows_of(g)], 2 * blocks, (0, W, 2 * W), hi_ref, lo_ref,
            slice(tile * LANES, (tile + 1) * LANES), blocks,
        )
    row = lax.broadcasted_iota(jnp.int32, (8, LANES), 0)
    wide = even_ref.shape[1]

    def fill(buffer, index):
        cols = chunk_at(index, wide)
        table = table_ref[:, cols]
        buffer[...] = dot_nn(hi_ref[...], table) + dot_nn(lo_ref[...], table)

    def work(spread_ref, index):
        parts = []
        for tile in range(wide // LANES):
            inner = slice(tile * LANES, (tile + 1) * LANES)
            cols = pl.ds(pl.multiple_of(index * wide + tile * LANES, LANES), LANES)
            cross = Window()
            total = colsum_ref[:, cols]
            for group in range(2 * blocks):
                g = group - blocks
                if g < 0:
                    product = halo_ref[rows_of(group), cols] * spread_ref[rows_of(group), inner]
                else:
                    product = ret_ref[rows_of(g), cols] * factor_ref[rows_of(g), cols]
                product = cross.push(product, row)
                if g >= 0:
                    mean_f = spread_ref[rows_of(blocks + g), inner]
                    gain = spread_ref[rows_of(2 * blocks + g), inner]
                    crf = product * inv_ref[rows_of(g)] - mean_ref[rows_of(g), cols] * mean_f
                    variance = crr_ref[rows_of(g), cols] - crf * crf * gain
                    var_ref[rows_of(g), cols] = (1.0 - shrink_weight) * variance
                    total = total + variance
            hi = total.astype(bf16).astype(f32)
            mid = (total - hi).astype(bf16).astype(f32)
            parts.append(
                jnp.concatenate([hi, mid, total - hi - mid, jnp.zeros_like(hi)], axis=0).astype(bf16)
            )
        acc_ref[...] += dot_nt(
            jnp.concatenate(parts, axis=1), table_ref[:, chunk_at(index, wide)]
        )

    pipelined(fill, work, (even_ref, odd_ref), ret_ref.shape[1] // wide)
    total = jnp.sum(acc_ref[...], axis=0, keepdims=True)
    swapped = jnp.concatenate([total[:, HALF:], total[:, :HALF]], axis=1)
    total = jnp.where(flip_ref[0:1] == 0, total, swapped)
    totals_ref[...] = jnp.broadcast_to(total, totals_ref.shape)


VMEM = pl.BlockSpec(memory_space=pltpu.VMEM)


def kernel_call(body, outs, arrays, scratch=(), flops=0, moved=0):
    return kernel_of(body, outs, arrays, scratch, flops, moved)


def kernel_of(body, outs, arrays, scratch, flops, moved):
    return pl.pallas_call(
        body,
        out_shape=tuple(o if hasattr(o, "dtype") else jax.ShapeDtypeStruct(o, f32) for o in outs),
        in_specs=[VMEM] * len(arrays),
        out_specs=[VMEM] * len(outs),
        scratch_shapes=list(scratch),
        compiler_params=pltpu.CompilerParams(vmem_limit_bytes=10 * MIB),
        cost_estimate=pl.CostEstimate(flops=flops, bytes_accessed=moved, transcendentals=0),
    )(*arrays)


def shrink_kernel(
    all_steps, flip_ref, parts_ref, cown_ref, cother_ref, table_ref, head_ref, main_ref, out_hbm, out_ref, sems
):
    total = jnp.sum(parts_ref[...], axis=0, keepdims=True)
    swapped = jnp.concatenate([total[:, HALF:], total[:, :HALF]], axis=1)
    total = jnp.where(flip_ref[0:1] == 0, total, swapped)
    count = jnp.concatenate([cown_ref[W : W + 1], cother_ref[W : W + 1]], axis=1)
    mean = total / (all_steps * jnp.maximum(count, 1.0))
    left = split3_rows(shrink_weight * mean)
    chunks, _, wide = out_ref.shape
    copies = []
    for c in range(chunks):
        cols = slice(c * wide, (c + 1) * wide)
        pooled = jnp.sum(dot_nn(left, table_ref[:, cols]), axis=0, keepdims=True)
        out_ref[c, :W] = head_ref[:, cols] + pooled
        out_ref[c, W:] = main_ref[:, cols] + pooled
        copy = pltpu.make_async_copy(out_ref.at[c], out_hbm.at[:, pl.ds(c * wide, wide)], sems.at[c])
        copy.start()
        copies.append(copy)
    for copy in copies:
        copy.wait()


def shrink(all_steps, flip, parts, own, other, table, head, main):
    width = head.shape[1]
    rows = head.shape[0] + main.shape[0]
    chunks = 4
    return pl.pallas_call(
        functools.partial(shrink_kernel, float(all_steps)),
        out_shape=jax.ShapeDtypeStruct((rows, width), f32),
        in_specs=[VMEM] * 7,
        out_specs=pl.BlockSpec(memory_space=pltpu.HBM),
        scratch_shapes=[
            pltpu.VMEM((chunks, rows, width // chunks), f32),
            pltpu.SemaphoreType.DMA((chunks,)),
        ],
        compiler_params=pltpu.CompilerParams(vmem_limit_bytes=10 * MIB),
        cost_estimate=pl.CostEstimate(
            flops=2 * rows * width, bytes_accessed=8 * rows * width, transcendentals=0
        ),
        name="shrink",
    )(flip, parts, own, other, table, head, main)


def swap(value, axis, bit):
    return lax.ppermute(value, axis, [(i, i ^ bit) for i in range(lax.axis_size(axis))])


def ahead(value, axis):
    return lax.ppermute(value, axis, [(i, i + 1) for i in range(lax.axis_size(axis) - 1)])


def across(value, axis):
    bit = 2
    while bit < lax.axis_size(axis):
        value = value + swap(value, axis, bit)
        bit *= 2
    return value


def step(returns, sector):
    rows, width = returns.shape
    main = rows - W
    n_time, n_series = lax.axis_size("tm"), lax.axis_size("series")
    core = (lax.axis_index("series") % 2).astype(jnp.int32)
    first_step = (lax.axis_index("tm") * rows).astype(jnp.int32)
    table, returns, flip, inv = pl.pallas_call(
        table_kernel,
        out_shape=(
            jax.ShapeDtypeStruct((SECTORS, width), bf16),
            jax.ShapeDtypeStruct((rows, width), f32),
            jax.ShapeDtypeStruct((8, SECTORS), jnp.int32),
            jax.ShapeDtypeStruct((W, LANES), f32),
        ),
        in_specs=[pl.BlockSpec(memory_space=pltpu.HBM)] + [VMEM] * 3,
        out_specs=[VMEM] * 4,
        scratch_shapes=[pltpu.SemaphoreType.DMA],
        compiler_params=pltpu.CompilerParams(vmem_limit_bytes=48 * MIB),
        name="table",
    )(
        returns,
        (sector ^ (core * HALF))[None, :],
        jnp.broadcast_to(core, (8, LANES)),
        jnp.broadcast_to(first_step, (8, LANES)),
    )
    keep, send, tail = kernel_call(
        sums_kernel, [(rows + 8, HALF), (rows + 8, HALF), (W, width)], [returns, table],
        scratch=[pltpu.VMEM((2 * rows + 32, width), bf16)],
        flops=4 * rows * width * SECTORS, moved=8 * rows * width,
    )
    halo = ahead(tail, "tm")
    swapped = swap(send, "series", 1)
    own_tail = across(keep[main:] + swapped[main:], "series")
    own = across(keep[:main] + swapped[:main], "series")
    prior_own = ahead(own_tail, "tm")
    other_tail = swap(own_tail, "series", 1)
    other = swap(own, "series", 1)
    prior_other = swap(prior_own, "series", 1)
    wide = 2 * LANES
    lhs = 3 * rows - 2 * W
    mean, crr = kernel_call(
        moments_main_kernel, [(main, width)] * 2, [returns],
        flops=40 * main * width, moved=12 * main * width,
    )
    mean_head, crr_head = kernel_call(
        moments_head_kernel, [(W, width)] * 2, [inv, halo, returns],
        flops=40 * W * width, moved=12 * W * width,
    )
    left = [pltpu.VMEM((lhs, HALF), bf16)] * 2
    (spread,) = kernel_call(
        own_kernel, [(lhs, width)], [own, own_tail, table], scratch=left,
        flops=2 * lhs * width * SECTORS, moved=4 * lhs * width,
    )
    var, factor, colsum = kernel_call(
        main_kernel, [(main, width), (W, width), (8, width)],
        [other, other_tail, spread, returns, mean, crr, table],
        scratch=left + [pltpu.VMEM((lhs, wide), f32)] * 2,
        flops=4 * lhs * width * SECTORS, moved=12 * rows * width,
    )
    var_head, totals = kernel_call(
        head_kernel, [(W, width), (n_time * n_series, SECTORS)],
        [inv, flip, own, other, own_tail, other_tail, prior_own, prior_other, halo, returns, factor,
         mean_head, crr_head, colsum, table],
        scratch=[pltpu.VMEM((3 * W, SECTORS), bf16)] * 2
        + [pltpu.VMEM((3 * W, wide), f32)] * 2
        + [pltpu.VMEM((32, SECTORS), f32)],
        flops=16 * W * width * SECTORS, moved=12 * W * width,
    )
    parts = lax.all_to_all(totals, ("tm", "series"), 0, 0)
    return shrink(n_time * rows, flip, parts, own_tail, other_tail, table, var_head, var)


def solution(mesh):
    placed = (P("tm", "series"), P("series"))
    return jax.shard_map(step, mesh=mesh, in_specs=placed, out_specs=P("tm", "series"), check_vma=False)
```

time: 51.8 us -> 49.5 us (0.956)
  local copies, waits for them, and re-layouts: 2.36 us -> 0.08 us
  starting transfers between devices: 12.7 us -> 11.3 us
  other arithmetic: 0.15 us -> 0.78 us
  Pallas kernels: 16.6 us -> 17.2 us
    unnamed x7 -> x1, local copies, waits for them, and re-layouts: 2.3 us -> 0.01 us
    ppermute x6, starting transfers between devices: 5.6 us -> 3.43 us  [swap(): lax.ppermute(value, axis, [(i, i ^ bit) for i in range(lax.axis_size(axis...]
    pallas_call x5 -> x7, Pallas kernels: 14.5 us -> 15.7 us  [the longest x6 14.1 us: kernel_of(): pl.pallas_call(body, out_shape=tuple((o if hasattr(o, 'dtype') else jax.S...]
    ppermute x2, starting transfers between devices: 7.13 us -> 7.85 us  [ahead(): lax.ppermute(value, axis, [(i, i + 1) for i in range(lax.axis_size(axis)...]
    xor x0 -> x1, other arithmetic: none -> 0.7 us  [step(): sector ^ core * HALF]
    ppermute x6, waiting for transfers between devices: 5.85 us -> 6.5 us  [swap(): lax.ppermute(value, axis, [(i, i ^ bit) for i in range(lax.axis_size(axis...]
    pallas_call x1, Pallas kernels: 2.11 us -> 1.59 us  [shrink(): pl.pallas_call(functools.partial(shrink_kernel, float(all_steps)), out_sh...]
  transfers between devices with their start and end apart: 8 -> 8, of which waited for: 4 -> 1; matrix products, arithmetic and copies ran while one was open for 0% -> 0% of each run, Pallas kernels for 16% -> 20%
where the time goes in v4:
time: 49.5 us; the launch traced here: 49.2 us
  Pallas kernels  17.2 us (35%)
  blocking collectives  13.2 us (27%)
  starting transfers between devices  11.3 us (23%)
  waiting for transfers between devices  6.5 us (13%)
  other arithmetic  0.78 us (2%)
    pallas_call x6, Pallas kernels, kernel_of(): pl.pallas_call(body, out_shape=tuple((o if hasattr(o, 'dtype') else jax.S...  14.1 us
    all_to_all x1, blocking collectives, step(): parts = lax.all_to_all(totals, ('tm', 'series'), 0, 0)  13.2 us
    ppermute x2, starting transfers between devices, ahead(): lax.ppermute(value, axis, [(i, i + 1) for i in range(lax.axis_size(axis)...  7.85 us
    ppermute x6, waiting for transfers between devices, swap(): lax.ppermute(value, axis, [(i, i ^ bit) for i in range(lax.axis_size(axis...  6.5 us
    ppermute x6, starting transfers between devices, swap(): lax.ppermute(value, axis, [(i, i ^ bit) for i in range(lax.axis_size(axis...  3.43 us
    pallas_call x1, Pallas kernels, step(): pl.pallas_call(table_kernel, out_shape=(jax.ShapeDtypeStruct((SECTORS, wi...  1.6 us
    pallas_call x1, Pallas kernels, shrink(): pl.pallas_call(functools.partial(shrink_kernel, float(all_steps)), out_sh...  1.59 us
  transfers between devices with their start and end apart: 8, of which 1 were waited for; matrix products, arithmetic and copies ran while one was open for 0% of the time, Pallas kernels for 20%

profile of v4, /device:TPU:0, one launch (start us, length us, event | category | flops | bytes accessed | tf_op | source)
XLA Modules:
  0.0 49.2 jit_solution(12033872571746995813)
XLA Ops:
  0.0 0.7 %broadcast_xor_fusion = s32[2048]{0:T(1024)S(1)} fusion(s32[2048]{0:T(1024)} %param.3, s32[]{:T(128)S(6)} %mul.6), kind=kLoop, calls=%fused_computation.3 | loop fusion | flops 2048 | bytes 16388 | tf_op jit(solution)/shard_map/xor | solution.py:429
  0.7 1.6 %table.1 = (bf16[512,2048]{1,0:T(8,128)(2,1)S(1)}, f32[256,2048]{1,0:T(8,128)S(1)}, s32[8,512]{1,0:T(8,128)S(1)}, f32[64,128]{1,0:T(8,128)S(1)}) custom-call(f32[256,2048]{1,0:T(8,128)} %ret_hbm.1, s32[1,2048]{1,0:T(1,128)S(1)} %bitcast.7, s32[8,128]{1,0:T(8,128)S(1)} %broadcast_in_dim.10.core_ref, s32[8,128]{1,0:T(8,128)S(1)} %broadcast_in_dim.11.first_ref), custom_call_target="tpu_custom_call" | custom-call | tf_op jit(solution)/shard_map/table/pallas_call | solution.py:414
  2.3 1.3 %shard_map.28 = (f32[264,256]{1,0:T(8,128)S(1)}, f32[264,256]{1,0:T(8,128)S(1)}, f32[64,2048]{1,0:T(8,128)S(1)}) custom-call(f32[256,2048]{1,0:T(8,128)S(1)} %get-tuple-element.23.ret_ref, bf16[512,2048]{1,0:T(8,128)(2,1)S(1)} %get-tuple-element.24.table_ref), custom_call_target="tpu_custom_call" | custom-call | flops 1073741824 | bytes 4194304 | tf_op jit(solution)/shard_map/pallas_call | solution.py:337
  3.7 0.6 %collective-permute-start = (f32[264,256]{1,0:T(8,128)S(1)}, f32[264,256]{1,0:T(8,128)S(1)}, u32[]{:S(2)}, u32[]{:S(2)}) collective-permute-start(f32[264,256]{1,0:T(8,128)S(1)} %get-tuple-element.26), channel_id=1, source_target_pairs={{0,1},{1,0},{2,3},{3,2},{4,5},{5,4},{6,7},{7,6},{8,9},{9,8},{10,11... | collective-permute-start | bytes 811016 | tf_op jit(solution)/shard_map/ppermute | solution.py:393
  4.2 4.5 %collective-permute-start.7 = (f32[64,2048]{1,0:T(8,128)S(1)}, f32[64,2048]{1,0:T(8,128)S(1)}, u32[]{:S(2)}, u32[]{:S(2)}) collective-permute-start(f32[64,2048]{1,0:T(8,128)S(1)} %get-tuple-element.27), channel_id=1, source_target_pairs={{0,4},{4,8},{8,12},{12,16},{16,20},{20,24},{24,28},{1,5},{5,9},{9,... | collective-permute-start | bytes 1572872 | tf_op jit(solution)/shard_map/ppermute | solution.py:397
  8.7 0.0 collective-permute-done
  8.7 1.6 %collective-permute-start.1 = (f32[192,256]{1,0:T(8,128)S(1)}, f32[192,256]{1,0:T(8,128)S(1)}, u32[]{:S(2)}, u32[]{:S(2)}) collective-permute-start(f32[192,256]{1,0:T(8,128)S(1)} %slice_add_fusion), channel_id=1, source_target_pairs={{0,2},{1,3},{2,0},{3,1},{4,6},{5,7},{6,4},{7,5},{8,10},{9,11},{10,... | collective-permute-start | bytes 589832 | tf_op jit(solution)/shard_map/ppermute | solution.py:393
  10.3 0.6 %collective-permute-start.3 = (f32[72,256]{1,0:T(8,128)S(1)}, f32[72,256]{1,0:T(8,128)S(1)}, u32[]{:S(2)}, u32[]{:S(2)}) collective-permute-start(f32[72,256]{1,0:T(8,128)S(1)} %slice_add_fusion.1), channel_id=1, source_target_pairs={{0,2},{1,3},{2,0},{3,1},{4,6},{5,7},{6,4},{7,5},{8,10},{9,11},{10,... | collective-permute-start | bytes 221192 | tf_op jit(solution)/shard_map/ppermute | solution.py:393
  10.9 6.5 %collective-permute-done.3 = f32[72,256]{1,0:T(8,128)S(1)} collective-permute-done((f32[72,256]{1,0:T(8,128)S(1)}, f32[72,256]{1,0:T(8,128)S(1)}, u32[]{:S(2)}, u32[]{:S(2)}) %collective-permute-start.3) | collective-permute-done | bytes 73760 | tf_op jit(solution)/shard_map/ppermute | solution.py:393
  17.4 3.4 %collective-permute-start.5 = (f32[72,256]{1,0:T(8,128)S(1)}, f32[72,256]{1,0:T(8,128)S(1)}, u32[]{:S(2)}, u32[]{:S(2)}) collective-permute-start(f32[72,256]{1,0:T(8,128)S(1)} %add.20.own_tail_ref.counts_own_ref.cown_ref), channel_id=1, source_target_pairs={{0,4},{4,8},{8,12},{12,16},{16,20},{20,24},{24,28},{1,5},{5,9},{9,... | collective-permute-start | bytes 221192 | tf_op jit(solution)/shard_map/ppermute | solution.py:397
  20.8 0.0 collective-permute-done.1
  20.9 0.1 collective-permute-start.2
  20.9 2.0 %shard_map.30 = (f32[192,2048]{1,0:T(8,128)S(1)}, f32[192,2048]{1,0:T(8,128)S(1)}) custom-call(f32[256,2048]{1,0:T(8,128)S(1)} %get-tuple-element.23.ret_ref), custom_call_target="tpu_custom_call" | custom-call | flops 15728640 | bytes 4718592 | tf_op jit(solution)/shard_map/pallas_call | solution.py:337
  22.9 0.6 %collective-permute-start.4 = (f32[72,256]{1,0:T(8,128)S(1)}, f32[72,256]{1,0:T(8,128)S(1)}, u32[]{:S(2)}, u32[]{:S(2)}) collective-permute-start(f32[72,256]{1,0:T(8,128)S(1)} %add.20.own_tail_ref.counts_own_ref.cown_ref), channel_id=1, source_target_pairs={{0,1},{1,0},{2,3},{3,2},{4,5},{5,4},{6,7},{7,6},{8,9},{9,8},{10,11... | collective-permute-start | bytes 221192 | tf_op jit(solution)/shard_map/ppermute | solution.py:393
  23.5 0.0 collective-permute-done.5.prior_own_ref
  23.5 0.1 collective-permute-start.6
  23.6 3.1 %shard_map.29.spread_ref = f32[640,2048]{1,0:T(8,128)S(1)} custom-call(f32[192,256]{1,0:T(8,128)S(1)} %add.18.own_ref, f32[72,256]{1,0:T(8,128)S(1)} %add.20.own_tail_ref.counts_own_ref.cown_ref, bf16[512,2048]{1,0:T(8,128)(2,1)S(1)} %get-tuple-element.24.table_ref), custom_call_target="tpu_custom_call" | custom-call | flops 1342177280 | bytes 5242880 | tf_op jit(solution)/shard_map/pallas_call | solution.py:337
  26.6 0.0 collective-permute-done.7.halo_ref
  26.6 1.0 %shard_map.32 = (f32[64,2048]{1,0:T(8,128)S(1)}, f32[64,2048]{1,0:T(8,128)S(1)}) custom-call(f32[64,128]{1,0:T(8,128)S(1)} %get-tuple-element.22.inv_ref, f32[64,2048]{1,0:T(8,128)S(1)} %collective-permute-done.7.halo_ref, f32[256,2048]{1,0:T(8,128)S(1)} %get-tuple-element.23.ret_ref), custom_call_target="tpu_custom_call" | custom-call | flops 5242880 | bytes 1572864 | tf_op jit(solution)/shard_map/pallas_call | solution.py:337
  27.6 0.0 collective-permute-done.4.other_tail_ref.counts_other_ref.cother_ref
  27.7 0.0 collective-permute-done.2.other_ref
  27.7 3.7 %shard_map.31 = (f32[192,2048]{1,0:T(8,128)S(1)}, f32[64,2048]{1,0:T(8,128)S(1)}, f32[8,2048]{1,0:T(8,128)S(1)}) custom-call(f32[192,256]{1,0:T(8,128)S(1)} %collective-permute-done.2.other_ref, f32[72,256]{1,0:T(8,128)S(1)} %collective-permute-done.4.other_tail_ref.counts_other_ref.cother_ref, f32[640,2048]{1,0:T(8,128)S(1)} %shard_map.29.spread_ref, ...), custom_call_target="tpu_custom_call" | custom-call | flops 2684354560 | bytes 6291456 | tf_op jit(solution)/shard_map/pallas_call | solution.py:337
  31.4 0.0 collective-permute-done.6.prior_other_ref
  31.4 3.0 %shard_map.33 = (f32[64,2048]{1,0:T(8,128)S(1)}, f32[32,512]{1,0:T(8,128)S(1)}) custom-call(f32[64,128]{1,0:T(8,128)S(1)} %get-tuple-element.22.inv_ref, s32[8,512]{1,0:T(8,128)S(1)} %get-tuple-element.21.flip_ref, f32[192,256]{1,0:T(8,128)S(1)} %add.18.own_ref, f32[192,256]{1,0:T(8,128)S(1)} %collective-permute-done.2.other_ref, ...), custom_call_target="tpu_custom_call" | custom-call | flops 1073741824 | bytes 1572864 | tf_op jit(solution)/shard_map/pallas_call | solution.py:337
  34.4 0.1 copy.3
  34.4 13.2 %all_to_all.11 = f32[32,1,512]{2,1,0:T(1,128)S(1)} all-to-all(f32[32,1,512]{2,1,0:T(1,128)S(1)} %copy.3), channel_id=1, replica_groups=mesh['tm'=8,'series'=4] {'tm','series'}, dimensions={0} | all-to-all | bytes 131072 | tf_op jit(solution)/shard_map/all_to_all | solution.py:476
  47.7 1.6 %shrink.1 = f32[256,2048]{1,0:T(8,128)} custom-call(s32[8,512]{1,0:T(8,128)S(1)} %get-tuple-element.21.flip_ref, f32[32,512]{1,0:T(8,128)S(1)} %bitcast.5, f32[72,256]{1,0:T(8,128)S(1)} %add.20.own_tail_ref.counts_own_ref.cown_ref, f32[72,256]{1,0:T(8,128)S(1)} %collective-permute-done.4.other_tail_ref.counts_other_ref.cother_ref, ...), custom_call_target="tpu_custom_call" | custom-call | flops 1048576 | bytes 4194304 | tf_op jit(solution)/shard_map/shrink/pallas_call | solution.py:375
  (7 shorter events, 0.1 us)
Async XLA Ops:
  3.7 5.0 %collective-permute-start = (f32[264,256]{1,0:T(8,128)S(1)}, f32[264,256]{1,0:T(8,128)S(1)}, u32[]{:S(2)}, u32[]{:S(2)}) collective-permute-start(f32[264,256]{1,0:T(8,128)S(1)} %get-tuple-element.26), channel_id=1, source_target_pairs={{0,1},{1,0},{2,3},{3,2},{4,5},{5,4},{6,7},{7,6},{8,9},{9,8},{10,11... | collective-permute-start | bytes 811016 | tf_op jit(solution)/shard_map/ppermute | solution.py:393
  4.2 22.4 %collective-permute-start.7 = (f32[64,2048]{1,0:T(8,128)S(1)}, f32[64,2048]{1,0:T(8,128)S(1)}, u32[]{:S(2)}, u32[]{:S(2)}) collective-permute-start(f32[64,2048]{1,0:T(8,128)S(1)} %get-tuple-element.27), channel_id=1, source_target_pairs={{0,4},{4,8},{8,12},{12,16},{16,20},{20,24},{24,28},{1,5},{5,9},{9,... | collective-permute-start | bytes 1572872 | tf_op jit(solution)/shard_map/ppermute | solution.py:397
  8.7 12.1 %collective-permute-start.1 = (f32[192,256]{1,0:T(8,128)S(1)}, f32[192,256]{1,0:T(8,128)S(1)}, u32[]{:S(2)}, u32[]{:S(2)}) collective-permute-start(f32[192,256]{1,0:T(8,128)S(1)} %slice_add_fusion), channel_id=1, source_target_pairs={{0,2},{1,3},{2,0},{3,1},{4,6},{5,7},{6,4},{7,5},{8,10},{9,11},{10,... | collective-permute-start | bytes 589832 | tf_op jit(solution)/shard_map/ppermute | solution.py:393
  10.3 7.1 %collective-permute-start.3 = (f32[72,256]{1,0:T(8,128)S(1)}, f32[72,256]{1,0:T(8,128)S(1)}, u32[]{:S(2)}, u32[]{:S(2)}) collective-permute-start(f32[72,256]{1,0:T(8,128)S(1)} %slice_add_fusion.1), channel_id=1, source_target_pairs={{0,2},{1,3},{2,0},{3,1},{4,6},{5,7},{6,4},{7,5},{8,10},{9,11},{10,... | collective-permute-start | bytes 221192 | tf_op jit(solution)/shard_map/ppermute | solution.py:393
  17.4 6.1 %collective-permute-start.5 = (f32[72,256]{1,0:T(8,128)S(1)}, f32[72,256]{1,0:T(8,128)S(1)}, u32[]{:S(2)}, u32[]{:S(2)}) collective-permute-start(f32[72,256]{1,0:T(8,128)S(1)} %add.20.own_tail_ref.counts_own_ref.cown_ref), channel_id=1, source_target_pairs={{0,4},{4,8},{8,12},{12,16},{16,20},{20,24},{24,28},{1,5},{5,9},{9,... | collective-permute-start | bytes 221192 | tf_op jit(solution)/shard_map/ppermute | solution.py:397
  20.9 6.8 %collective-permute-start.2 = (f32[192,256]{1,0:T(8,128)S(1)}, f32[192,256]{1,0:T(8,128)S(1)}, u32[]{:S(2)}, u32[]{:S(2)}) collective-permute-start(f32[192,256]{1,0:T(8,128)S(1)} %add.18.own_ref), channel_id=1, source_target_pairs={{0,1},{1,0},{2,3},{3,2},{4,5},{5,4},{6,7},{7,6},{8,9},{9,8},{10,11... | collective-permute-start | bytes 589832 | tf_op jit(solution)/shard_map/ppermute | solution.py:393
  22.9 4.7 %collective-permute-start.4 = (f32[72,256]{1,0:T(8,128)S(1)}, f32[72,256]{1,0:T(8,128)S(1)}, u32[]{:S(2)}, u32[]{:S(2)}) collective-permute-start(f32[72,256]{1,0:T(8,128)S(1)} %add.20.own_tail_ref.counts_own_ref.cown_ref), channel_id=1, source_target_pairs={{0,1},{1,0},{2,3},{3,2},{4,5},{5,4},{6,7},{7,6},{8,9},{9,8},{10,11... | collective-permute-start | bytes 221192 | tf_op jit(solution)/shard_map/ppermute | solution.py:393
  23.5 7.9 %collective-permute-start.6 = (f32[72,256]{1,0:T(8,128)S(1)}, f32[72,256]{1,0:T(8,128)S(1)}, u32[]{:S(2)}, u32[]{:S(2)}) collective-permute-start(f32[72,256]{1,0:T(8,128)S(1)} %collective-permute-done.5.prior_own_ref), channel_id=1, source_target_pairs={{0,1},{1,0},{2,3},{3,2},{4,5},{5,4},{6,7},{7,6},{8,9},{9,8},{10,11... | collective-permute-start | bytes 221192 | tf_op jit(solution)/shard_map/ppermute | solution.py:393

commit v5 on v4

--- a/solution.py
+++ b/solution.py
@@ -43,33 +43,51 @@
     return jnp.where(row == 0, hi, jnp.where(row == 1, mid, jnp.where(row == 2, low, 0.0))).astype(bf16)
 
 
-def table_kernel(ret_hbm, sec_ref, core_ref, first_ref, table_ref, ret_ref, flip_ref, inv_ref, sem):
-    copy = pltpu.make_async_copy(ret_hbm, ret_ref, sem)
-    copy.start()
-    wide = 4 * LANES
+def load_kernel(
+    ret_hbm, sec_hbm, core_ref, first_ref,
+    keep_ref, send_ref, table_ref, ret_ref, tail_ref, flip_ref, inv_ref,
+    sec_ref, left_ref, acc_ref, sec_sem, tail_sem, ret_sems,
+):
+    rows, width = ret_ref.shape
+    wide = left_ref.shape[1]
+    height = rows + 16
+    chunks = width // wide
+    sec_copy = pltpu.make_async_copy(sec_hbm, sec_ref, sec_sem)
+    sec_copy.start()
+    copies = []
+    for c in range(chunks):
+        cols = pl.ds(c * wide, wide)
+        copy = pltpu.make_async_copy(ret_hbm.at[:, cols], ret_ref.at[:, cols], ret_sems.at[c])
+        copy.start()
+        copies.append(copy)
+    tail_copy = pltpu.make_async_copy(ret_hbm.at[pl.ds(rows - W, W)], tail_ref, tail_sem)
+    tail_copy.start()
     flip_ref[...] = jnp.concatenate([core_ref[...]] * (SECTORS // LANES), axis=1)
     position = lax.broadcasted_iota(jnp.int32, inv_ref.shape, 0) + (first_ref[0:1] + 1)
     inv_ref[...] = 1.0 / jnp.minimum(position, W).astype(f32)
-    for c in range(table_ref.shape[1] // wide):
+    left_ref[rows:height] = jnp.ones((16, wide), bf16)
+    left_ref[height + rows :] = jnp.zeros((16, wide), bf16)
+    turn = jnp.concatenate([core_ref[0:1] * HALF] * (wide // LANES), axis=1)
+    sec_copy.wait()
+    for c in range(chunks):
         cols = slice(c * wide, (c + 1) * wide)
         label = lax.broadcasted_iota(jnp.int32, (SECTORS, wide), 0)
-        table_ref[:, cols] = jnp.where(label == sec_ref[:, cols], 1.0, 0.0).astype(bf16)
-    copy.wait()
-
-
-def sums_kernel(ret_ref, table_ref, keep_ref, send_ref, tail_ref, left_ref):
-    rows, width = ret_ref.shape
-    height = rows + 16
-    hi, lo = split2(ret_ref[...])
-    left_ref[:rows] = hi
-    left_ref[rows:height] = jnp.ones((16, width), bf16)
-    left_ref[height : height + rows] = lo
-    left_ref[height + rows :] = jnp.zeros((16, width), bf16)
-    tail_ref[...] = ret_ref[rows - W :]
-    part = dot_nt(left_ref[...], table_ref[...])
-    part = part[: rows + 8] + part[height : height + rows + 8]
+        table_ref[:, cols] = jnp.where(label == (sec_ref[:, cols] ^ turn), 1.0, 0.0).astype(bf16)
+    for c in range(chunks):
+        cols = slice(c * wide, (c + 1) * wide)
+        copies[c].wait()
+        hi, lo = split2(ret_ref[:, cols])
+        left_ref[:rows] = hi
+        left_ref[height : height + rows] = lo
+        part = dot_nt(left_ref[...], table_ref[:, cols])
+        part = part[: rows + 8] + part[height : height + rows + 8]
+        if c > 0:
+            part = acc_ref[...] + part
+        if c < chunks - 1:
+            acc_ref[...] = part
     keep_ref[...] = part[:, :HALF]
     send_ref[...] = part[:, HALF:]
+    tail_copy.wait()
 
 
 class Window:
@@ -104,7 +122,7 @@
     return slice(group * 8, group * 8 + 8)
 
 
-def moments_body(load, inv, groups, mean_ref, crr_ref):
+def moments_body(load, inv, groups, total_ref, crr_ref):
     row = lax.broadcasted_iota(jnp.int32, (8, LANES), 0)
 
     def tile(index, _):
@@ -117,11 +135,11 @@
                 here = rows_of(group - W // 8)
                 scale = inv(group - W // 8)
                 mean = total * scale
-                mean_ref[here, cols] = mean
-                crr_ref[here, cols] = squares * scale - mean * mean
+                total_ref[here, cols] = total
+                crr_ref[here, cols] = (1.0 - shrink_weight) * (squares * scale - mean * mean)
         return 0
 
-    lax.fori_loop(0, mean_ref.shape[1] // LANES, tile, 0)
+    lax.fori_loop(0, total_ref.shape[1] // LANES, tile, 0)
 
 
 def moments_main_kernel(ret_ref, mean_ref, crr_ref):
@@ -147,7 +165,7 @@
     )
 
 
-def sector_rows(means, inv, groups, starts, hi_ref, lo_ref, out, kept=None):
+def sector_rows(means, inv, groups, starts, left_ref, out, low, kept=None):
     row = lax.broadcasted_iota(jnp.int32, (8, LANES), 0)
     first, second = Window(), Window()
     mean_parts, gain_parts = [], []
@@ -157,14 +175,15 @@
         if group >= W // 8:
             scale = inv(group - W // 8)
             mean_f = total * scale
+            spread = squares * scale - mean_f * mean_f + ridge_rate
             mean_parts.append(mean_f)
-            gain_parts.append(1.0 / (squares * scale - mean_f * mean_f + ridge_rate))
+            gain_parts.append((1.0 - shrink_weight) * scale * scale / spread)
     for start, parts in zip(starts, (means[:kept], mean_parts, gain_parts)):
         for pair in range(0, len(parts), 2):
             hi, lo = split2(jnp.concatenate(parts[pair : pair + 2], axis=0))
             here = slice(start + pair * 8, start + pair * 8 + 16)
-            hi_ref[here, out] = hi
-            lo_ref[here, out] = lo
+            left_ref[here, out : out + LANES] = hi
+            left_ref[here, out + low : out + low + LANES] = lo
 
 
 def pipelined(fill, work, buffers, chunks):
@@ -188,7 +207,7 @@
     return pl.ds(pl.multiple_of(index * wide, wide), wide)
 
 
-def main_rows(sums_ref, tail_ref, hi_ref, lo_ref):
+def main_rows(sums_ref, tail_ref, left_ref):
     main = sums_ref.shape[0]
     rows = main + W
     for tile in range(HALF // LANES):
@@ -200,38 +219,36 @@
             for g in range(rows // 8)
         ]
         sector_rows(
-            means, lambda g: 1.0 / W, rows // 8, (0, rows, rows + main), hi_ref, lo_ref, cols
+            means, lambda g: 1.0 / W, rows // 8, (0, rows, rows + main), left_ref, tile * LANES, HALF
         )
 
 
-def own_kernel(own_ref, own_tail_ref, table_ref, spread_ref, hi_ref, lo_ref):
-    main_rows(own_ref, own_tail_ref, hi_ref, lo_ref)
-    wide = 2 * LANES
-
-    def chunk(index, _):
-        cols = chunk_at(index, wide)
-        table = table_ref[:HALF, cols]
-        spread_ref[:, cols] = dot_nn(hi_ref[...], table) + dot_nn(lo_ref[...], table)
-        return 0
-
-    lax.fori_loop(0, table_ref.shape[1] // wide, chunk, 0)
+def twice(table):
+    return jnp.concatenate([table, table], axis=0)
+
+
+def own_kernel(own_ref, own_tail_ref, table_ref, spread_ref, left_ref):
+    main_rows(own_ref, own_tail_ref, left_ref)
+    wide = 4 * LANES
+    for index in range(table_ref.shape[1] // wide):
+        cols = slice(index * wide, (index + 1) * wide)
+        spread_ref[:, cols] = dot_nn(left_ref[...], twice(table_ref[:HALF, cols]))
 
 
 def main_kernel(
-    other_ref, other_tail_ref, spread_ref, ret_ref, mean_ref, crr_ref, table_ref,
-    var_ref, factor_ref, colsum_ref, hi_ref, lo_ref, even_ref, odd_ref,
+    other_ref, other_tail_ref, spread_ref, ret_ref, total_ref, crr_ref, table_ref,
+    var_ref, factor_ref, colsum_ref, left_ref, even_ref, odd_ref,
 ):
     rows = ret_ref.shape[0]
     main = rows - W
     blocks = W // 8
-    main_rows(other_ref, other_tail_ref, hi_ref, lo_ref)
+    main_rows(other_ref, other_tail_ref, left_ref)
     row = lax.broadcasted_iota(jnp.int32, (8, LANES), 0)
     wide = even_ref.shape[1]
 
     def fill(buffer, index):
         cols = chunk_at(index, wide)
-        table = table_ref[HALF:, cols]
-        buffer[...] = spread_ref[:, cols] + dot_nn(hi_ref[...], table) + dot_nn(lo_ref[...], table)
+        buffer[...] = spread_ref[:, cols] + dot_nn(left_ref[...], twice(table_ref[HALF:, cols]))
 
     def work(spread_ref, index):
         for tile in range(wide // LANES):
@@ -248,9 +265,9 @@
                     g = group - blocks
                     mean_f = spread_ref[rows_of(rows // 8 + g), inner]
                     gain = spread_ref[rows_of((rows + main) // 8 + g), inner]
-                    crf = product * (1.0 / W) - mean_ref[rows_of(g), cols] * mean_f
+                    crf = product - total_ref[rows_of(g), cols] * mean_f
                     variance = crr_ref[rows_of(g), cols] - crf * crf * gain
-                    var_ref[rows_of(g), cols] = (1.0 - shrink_weight) * variance
+                    var_ref[rows_of(g), cols] = variance
                     total = total + variance
             colsum_ref[:, cols] = total
 
@@ -259,8 +276,8 @@
 
 def head_kernel(
     inv_ref, flip_ref, own_ref, other_ref, counts_own_ref, counts_other_ref, prior_own_ref, prior_other_ref,
-    halo_ref, ret_ref, factor_ref, mean_ref, crr_ref, colsum_ref, table_ref,
-    var_ref, totals_ref, hi_ref, lo_ref, even_ref, odd_ref, acc_ref,
+    halo_ref, ret_ref, factor_ref, total_ref, crr_ref, colsum_ref, table_ref,
+    var_ref, totals_ref, left_ref, even_ref, odd_ref, acc_ref,
 ):
     blocks = W // 8
     acc_ref[...] = jnp.zeros_like(acc_ref)
@@ -278,16 +295,15 @@
             for g in range(2 * blocks)
         ]
         sector_rows(
-            means, lambda g: inv_ref[rows_of(g)], 2 * blocks, (0, W, 2 * W), hi_ref, lo_ref,
-            slice(tile * LANES, (tile + 1) * LANES), blocks,
+            means, lambda g: inv_ref[rows_of(g)], 2 * blocks, (0, W, 2 * W), left_ref,
+            tile * LANES, SECTORS, blocks,
         )
     row = lax.broadcasted_iota(jnp.int32, (8, LANES), 0)
     wide = even_ref.shape[1]
 
     def fill(buffer, index):
         cols = chunk_at(index, wide)
-        table = table_ref[:, cols]
-        buffer[...] = dot_nn(hi_ref[...], table) + dot_nn(lo_ref[...], table)
+        buffer[...] = dot_nn(left_ref[...], twice(table_ref[:, cols]))
 
     def work(spread_ref, index):
         parts = []
@@ -306,9 +322,9 @@
                 if g >= 0:
                     mean_f = spread_ref[rows_of(blocks + g), inner]
                     gain = spread_ref[rows_of(2 * blocks + g), inner]
-                    crf = product * inv_ref[rows_of(g)] - mean_ref[rows_of(g), cols] * mean_f
+                    crf = product - total_ref[rows_of(g), cols] * mean_f
                     variance = crr_ref[rows_of(g), cols] - crf * crf * gain
-                    var_ref[rows_of(g), cols] = (1.0 - shrink_weight) * variance
+                    var_ref[rows_of(g), cols] = variance
                     total = total + variance
             hi = total.astype(bf16).astype(f32)
             mid = (total - hi).astype(bf16).astype(f32)
@@ -353,7 +369,7 @@
     total = jnp.where(flip_ref[0:1] == 0, total, swapped)
     count = jnp.concatenate([cown_ref[W : W + 1], cother_ref[W : W + 1]], axis=1)
     mean = total / (all_steps * jnp.maximum(count, 1.0))
-    left = split3_rows(shrink_weight * mean)
+    left = split3_rows(shrink_weight / (1.0 - shrink_weight) * mean)
     chunks, _, wide = out_ref.shape
     copies = []
     for c in range(chunks):
@@ -411,29 +427,36 @@
     n_time, n_series = lax.axis_size("tm"), lax.axis_size("series")
     core = (lax.axis_index("series") % 2).astype(jnp.int32)
     first_step = (lax.axis_index("tm") * rows).astype(jnp.int32)
-    table, returns, flip, inv = pl.pallas_call(
-        table_kernel,
+    wide = 4 * LANES
+    hbm = pl.BlockSpec(memory_space=pltpu.HBM)
+    keep, send, table, returns, tail, flip, inv = pl.pallas_call(
+        load_kernel,
         out_shape=(
+            jax.ShapeDtypeStruct((rows + 8, HALF), f32),
+            jax.ShapeDtypeStruct((rows + 8, HALF), f32),
             jax.ShapeDtypeStruct((SECTORS, width), bf16),
             jax.ShapeDtypeStruct((rows, width), f32),
+            jax.ShapeDtypeStruct((W, width), f32),
             jax.ShapeDtypeStruct((8, SECTORS), jnp.int32),
             jax.ShapeDtypeStruct((W, LANES), f32),
         ),
-        in_specs=[pl.BlockSpec(memory_space=pltpu.HBM)] + [VMEM] * 3,
-        out_specs=[VMEM] * 4,
-        scratch_shapes=[pltpu.SemaphoreType.DMA],
+        in_specs=[hbm, hbm, VMEM, VMEM],
+        out_specs=[VMEM] * 7,
+        scratch_shapes=[
+            pltpu.VMEM((1, width), jnp.int32),
+            pltpu.VMEM((2 * rows + 32, wide), bf16),
+            pltpu.VMEM((rows + 8, SECTORS), f32),
+            pltpu.SemaphoreType.DMA,
+            pltpu.SemaphoreType.DMA,
+            pltpu.SemaphoreType.DMA((width // wide,)),
+        ],
         compiler_params=pltpu.CompilerParams(vmem_limit_bytes=48 * MIB),
-        name="table",
+        name="load",
     )(
         returns,
-        (sector ^ (core * HALF))[None, :],
+        sector[None, :],
         jnp.broadcast_to(core, (8, LANES)),
         jnp.broadcast_to(first_step, (8, LANES)),
-    )
-    keep, send, tail = kernel_call(
-        sums_kernel, [(rows + 8, HALF), (rows + 8, HALF), (W, width)], [returns, table],
-        scratch=[pltpu.VMEM((2 * rows + 32, width), bf16)],
-        flops=4 * rows * width * SECTORS, moved=8 * rows * width,
     )
     halo = ahead(tail, "tm")
     swapped = swap(send, "series", 1)
@@ -443,7 +466,7 @@
     other_tail = swap(own_tail, "series", 1)
     other = swap(own, "series", 1)
     prior_other = swap(prior_own, "series", 1)
-    wide = 2 * LANES
+    chunk = 4 * LANES
     lhs = 3 * rows - 2 * W
     mean, crr = kernel_call(
         moments_main_kernel, [(main, width)] * 2, [returns],
@@ -453,7 +476,7 @@
         moments_head_kernel, [(W, width)] * 2, [inv, halo, returns],
         flops=40 * W * width, moved=12 * W * width,
     )
-    left = [pltpu.VMEM((lhs, HALF), bf16)] * 2
+    left = [pltpu.VMEM((lhs, SECTORS), bf16)]
     (spread,) = kernel_call(
         own_kernel, [(lhs, width)], [own, own_tail, table], scratch=left,
         flops=2 * lhs * width * SECTORS, moved=4 * lhs * width,
@@ -461,15 +484,15 @@
     var, factor, colsum = kernel_call(
         main_kernel, [(main, width), (W, width), (8, width)],
         [other, other_tail, spread, returns, mean, crr, table],
-        scratch=left + [pltpu.VMEM((lhs, wide), f32)] * 2,
+        scratch=left + [pltpu.VMEM((lhs, chunk), f32)] * 2,
         flops=4 * lhs * width * SECTORS, moved=12 * rows * width,
     )
     var_head, totals = kernel_call(
         head_kernel, [(W, width), (n_time * n_series, SECTORS)],
         [inv, flip, own, other, own_tail, other_tail, prior_own, prior_other, halo, returns, factor,
          mean_head, crr_head, colsum, table],
-        scratch=[pltpu.VMEM((3 * W, SECTORS), bf16)] * 2
-        + [pltpu.VMEM((3 * W, wide), f32)] * 2
+        scratch=[pltpu.VMEM((3 * W, 2 * SECTORS), bf16)]
+        + [pltpu.VMEM((3 * W, chunk), f32)] * 2
         + [pltpu.VMEM((32, SECTORS), f32)],
         flops=16 * W * width * SECTORS, moved=12 * W * width,
     )

time: 49.5 us -> 46 us (0.929)
  Pallas kernels: 17.2 us -> 13.8 us
  other arithmetic: 0.78 us -> 0.08 us
  local copies, waits for them, and re-layouts: 0.08 us -> 0.77 us
    pallas_call x6 -> x5, Pallas kernels: 14.1 us -> 9.54 us  [kernel_of(): pl.pallas_call(body, out_shape=tuple((o if hasattr(o, 'dtype') else jax.S...]
    pallas_call x1, Pallas kernels: 1.6 us -> 2.71 us  [step(): pl.pallas_call(load_kernel, out_shape=(jax.ShapeDtypeStruct((rows + 8, HA...]
    xor x1 -> x0, other arithmetic: 0.7 us -> none  [step(): sector ^ core * HALF]
    unnamed x1 -> x3, local copies, waits for them, and re-layouts: 0.01 us -> 0.7 us
  transfers between devices with their start and end apart: 8 -> 8, of which waited for: 1 -> 1; matrix products, arithmetic and copies ran while one was open for 0% -> 0% of each run, Pallas kernels for 20% -> 16%
where the time goes in v5:
time: 46 us; the launch traced here: 45.7 us
  Pallas kernels  13.8 us (30%)
  blocking collectives  13.1 us (28%)
  starting transfers between devices  11.3 us (25%)
  waiting for transfers between devices  6.5 us (14%)
  local copies, waits for them, and re-layouts  0.77 us (2%)
    all_to_all x1, blocking collectives, step(): parts = lax.all_to_all(totals, ('tm', 'series'), 0, 0)  13.1 us
    pallas_call x5, Pallas kernels, kernel_of(): pl.pallas_call(body, out_shape=tuple((o if hasattr(o, 'dtype') else jax.S...  9.54 us
    ppermute x2, starting transfers between devices, ahead(): lax.ppermute(value, axis, [(i, i + 1) for i in range(lax.axis_size(axis)...  7.84 us
    ppermute x6, waiting for transfers between devices, swap(): lax.ppermute(value, axis, [(i, i ^ bit) for i in range(lax.axis_size(axis...  6.5 us
    ppermute x6, starting transfers between devices, swap(): lax.ppermute(value, axis, [(i, i ^ bit) for i in range(lax.axis_size(axis...  3.44 us
    pallas_call x1, Pallas kernels, step(): pl.pallas_call(load_kernel, out_shape=(jax.ShapeDtypeStruct((rows + 8, HA...  2.71 us
    pallas_call x1, Pallas kernels, shrink(): pl.pallas_call(functools.partial(shrink_kernel, float(all_steps)), out_sh...  1.59 us
  transfers between devices with their start and end apart: 8, of which 1 were waited for; matrix products, arithmetic and copies ran while one was open for 0% of the time, Pallas kernels for 16%

profile of v5, /device:TPU:0, one launch (start us, length us, event | category | flops | bytes accessed | tf_op | source)
XLA Modules:
  0.0 45.7 jit_solution(10422808054652461272)
XLA Ops:
  0.0 0.0 copy-start
  0.0 0.7 %copy-done = s32[2048]{0:T(1024)S(1)} copy-done((s32[2048]{0:T(1024)S(1)}, s32[2048]{0:T(1024)}, u32[]{:S(2)}) %copy-start) | copy-done | bytes 8216
  0.7 2.7 %load.1 = (f32[264,256]{1,0:T(8,128)S(1)}, f32[264,256]{1,0:T(8,128)S(1)}, bf16[512,2048]{1,0:T(8,128)(2,1)S(1)}, f32[256,2048]{1,0:T(8,128)S(1)}, f32[64,2048]{...) custom-call(f32[256,2048]{1,0:T(8,128)} %ret_hbm.1, s32[1,2048]{1,0:T(1,128)S(1)} %bitcast.7, ...), custom_call_target="tpu_custom_call" | custom-call | tf_op jit(solution)/shard_map/load/pallas_call | solution.py:432
  3.4 0.6 %collective-permute-start = (f32[264,256]{1,0:T(8,128)S(1)}, f32[264,256]{1,0:T(8,128)S(1)}, u32[]{:S(2)}, u32[]{:S(2)}) collective-permute-start(f32[264,256]{1,0:T(8,128)S(1)} %get-tuple-element.24), channel_id=1, source_target_pairs={{0,1},{1,0},{2,3},{3,2},{4,5},{5,4},{6,7},{7,6},{8,9},{9,8},{10,11... | collective-permute-start | bytes 811016 | tf_op jit(solution)/shard_map/ppermute | solution.py:409
  4.0 4.4 %collective-permute-start.7 = (f32[64,2048]{1,0:T(8,128)S(1)}, f32[64,2048]{1,0:T(8,128)S(1)}, u32[]{:S(2)}, u32[]{:S(2)}) collective-permute-start(f32[64,2048]{1,0:T(8,128)S(1)} %get-tuple-element.25), channel_id=1, source_target_pairs={{0,4},{4,8},{8,12},{12,16},{16,20},{20,24},{24,28},{1,5},{5,9},{9,... | collective-permute-start | bytes 1572872 | tf_op jit(solution)/shard_map/ppermute | solution.py:413
  8.4 0.0 collective-permute-done
  8.5 1.6 %collective-permute-start.1 = (f32[192,256]{1,0:T(8,128)S(1)}, f32[192,256]{1,0:T(8,128)S(1)}, u32[]{:S(2)}, u32[]{:S(2)}) collective-permute-start(f32[192,256]{1,0:T(8,128)S(1)} %slice_add_fusion), channel_id=1, source_target_pairs={{0,2},{1,3},{2,0},{3,1},{4,6},{5,7},{6,4},{7,5},{8,10},{9,11},{10,... | collective-permute-start | bytes 589832 | tf_op jit(solution)/shard_map/ppermute | solution.py:409
  10.1 0.6 %collective-permute-start.3 = (f32[72,256]{1,0:T(8,128)S(1)}, f32[72,256]{1,0:T(8,128)S(1)}, u32[]{:S(2)}, u32[]{:S(2)}) collective-permute-start(f32[72,256]{1,0:T(8,128)S(1)} %slice_add_fusion.1), channel_id=1, source_target_pairs={{0,2},{1,3},{2,0},{3,1},{4,6},{5,7},{6,4},{7,5},{8,10},{9,11},{10,... | collective-permute-start | bytes 221192 | tf_op jit(solution)/shard_map/ppermute | solution.py:409
  10.7 6.5 %collective-permute-done.3 = f32[72,256]{1,0:T(8,128)S(1)} collective-permute-done((f32[72,256]{1,0:T(8,128)S(1)}, f32[72,256]{1,0:T(8,128)S(1)}, u32[]{:S(2)}, u32[]{:S(2)}) %collective-permute-start.3) | collective-permute-done | bytes 73760 | tf_op jit(solution)/shard_map/ppermute | solution.py:409
  17.2 3.4 %collective-permute-start.5 = (f32[72,256]{1,0:T(8,128)S(1)}, f32[72,256]{1,0:T(8,128)S(1)}, u32[]{:S(2)}, u32[]{:S(2)}) collective-permute-start(f32[72,256]{1,0:T(8,128)S(1)} %add.20.own_tail_ref.counts_own_ref.cown_ref), channel_id=1, source_target_pairs={{0,4},{4,8},{8,12},{12,16},{16,20},{20,24},{24,28},{1,5},{5,9},{9,... | collective-permute-start | bytes 221192 | tf_op jit(solution)/shard_map/ppermute | solution.py:413
  20.6 0.0 collective-permute-done.1
  20.6 0.1 collective-permute-start.2
  20.7 2.0 %shard_map.29 = (f32[192,2048]{1,0:T(8,128)S(1)}, f32[192,2048]{1,0:T(8,128)S(1)}) custom-call(f32[256,2048]{1,0:T(8,128)S(1)} %get-tuple-element.26.ret_ref), custom_call_target="tpu_custom_call" | custom-call | flops 15728640 | bytes 4718592 | tf_op jit(solution)/shard_map/pallas_call | solution.py:353
  22.7 0.6 %collective-permute-start.4 = (f32[72,256]{1,0:T(8,128)S(1)}, f32[72,256]{1,0:T(8,128)S(1)}, u32[]{:S(2)}, u32[]{:S(2)}) collective-permute-start(f32[72,256]{1,0:T(8,128)S(1)} %add.20.own_tail_ref.counts_own_ref.cown_ref), channel_id=1, source_target_pairs={{0,1},{1,0},{2,3},{3,2},{4,5},{5,4},{6,7},{7,6},{8,9},{9,8},{10,11... | collective-permute-start | bytes 221192 | tf_op jit(solution)/shard_map/ppermute | solution.py:409
  23.3 0.0 collective-permute-done.5.prior_own_ref
  23.3 0.1 collective-permute-start.6
  23.4 1.7 %shard_map.28.spread_ref = f32[640,2048]{1,0:T(8,128)S(1)} custom-call(f32[192,256]{1,0:T(8,128)S(1)} %add.18.own_ref, f32[72,256]{1,0:T(8,128)S(1)} %add.20.own_tail_ref.counts_own_ref.cown_ref, bf16[512,2048]{1,0:T(8,128)(2,1)S(1)} %get-tuple-element.27.table_ref), custom_call_target="tpu_custom_call" | custom-call | flops 1342177280 | bytes 5242880 | tf_op jit(solution)/shard_map/pallas_call | solution.py:353
  25.1 0.0 collective-permute-done.7.halo_ref
  25.1 1.0 %shard_map.31 = (f32[64,2048]{1,0:T(8,128)S(1)}, f32[64,2048]{1,0:T(8,128)S(1)}) custom-call(f32[64,128]{1,0:T(8,128)S(1)} %get-tuple-element.22.inv_ref, f32[64,2048]{1,0:T(8,128)S(1)} %collective-permute-done.7.halo_ref, f32[256,2048]{1,0:T(8,128)S(1)} %get-tuple-element.26.ret_ref), custom_call_target="tpu_custom_call" | custom-call | flops 5242880 | bytes 1572864 | tf_op jit(solution)/shard_map/pallas_call | solution.py:353
  26.1 0.0 collective-permute-done.4.other_tail_ref.counts_other_ref.cother_ref
  26.1 0.0 collective-permute-done.2.other_ref
  26.1 2.6 %shard_map.30 = (f32[192,2048]{1,0:T(8,128)S(1)}, f32[64,2048]{1,0:T(8,128)S(1)}, f32[8,2048]{1,0:T(8,128)S(1)}) custom-call(f32[192,256]{1,0:T(8,128)S(1)} %collective-permute-done.2.other_ref, f32[72,256]{1,0:T(8,128)S(1)} %collective-permute-done.4.other_tail_ref.counts_other_ref.cother_ref, f32[640,2048]{1,0:T(8,128)S(1)} %shard_map.28.spread_ref, ...), custom_call_target="tpu_custom_call" | custom-call | flops 2684354560 | bytes 6291456 | tf_op jit(solution)/shard_map/pallas_call | solution.py:353
  28.7 0.0 collective-permute-done.6.prior_other_ref
  28.7 2.2 %shard_map.32 = (f32[64,2048]{1,0:T(8,128)S(1)}, f32[32,512]{1,0:T(8,128)S(1)}) custom-call(f32[64,128]{1,0:T(8,128)S(1)} %get-tuple-element.22.inv_ref, s32[8,512]{1,0:T(8,128)S(1)} %get-tuple-element.21.flip_ref, f32[192,256]{1,0:T(8,128)S(1)} %add.18.own_ref, f32[192,256]{1,0:T(8,128)S(1)} %collective-permute-done.2.other_ref, ...), custom_call_target="tpu_custom_call" | custom-call | flops 1073741824 | bytes 1572864 | tf_op jit(solution)/shard_map/pallas_call | solution.py:353
  30.9 0.1 copy.3
  31.0 13.1 %all_to_all.11 = f32[32,1,512]{2,1,0:T(1,128)S(1)} all-to-all(f32[32,1,512]{2,1,0:T(1,128)S(1)} %copy.3), channel_id=1, replica_groups=mesh['tm'=8,'series'=4] {'tm','series'}, dimensions={0} | all-to-all | bytes 131072 | tf_op jit(solution)/shard_map/all_to_all | solution.py:499
  44.2 1.6 %shrink.1 = f32[256,2048]{1,0:T(8,128)} custom-call(s32[8,512]{1,0:T(8,128)S(1)} %get-tuple-element.21.flip_ref, f32[32,512]{1,0:T(8,128)S(1)} %bitcast.5, f32[72,256]{1,0:T(8,128)S(1)} %add.20.own_tail_ref.counts_own_ref.cown_ref, f32[72,256]{1,0:T(8,128)S(1)} %collective-permute-done.4.other_tail_ref.counts_other_ref.cother_ref, ...), custom_call_target="tpu_custom_call" | custom-call | flops 1048576 | bytes 4194304 | tf_op jit(solution)/shard_map/shrink/pallas_call | solution.py:391
  (7 shorter events, 0.1 us)
Async XLA Ops:
  0.0 0.7 %copy-start = (s32[2048]{0:T(1024)S(1)}, s32[2048]{0:T(1024)}, u32[]{:S(2)}) copy-start(s32[2048]{0:T(1024)} %param.3) | copy-start | bytes 24580
  3.4 5.0 %collective-permute-start = (f32[264,256]{1,0:T(8,128)S(1)}, f32[264,256]{1,0:T(8,128)S(1)}, u32[]{:S(2)}, u32[]{:S(2)}) collective-permute-start(f32[264,256]{1,0:T(8,128)S(1)} %get-tuple-element.24), channel_id=1, source_target_pairs={{0,1},{1,0},{2,3},{3,2},{4,5},{5,4},{6,7},{7,6},{8,9},{9,8},{10,11... | collective-permute-start | bytes 811016 | tf_op jit(solution)/shard_map/ppermute | solution.py:409
  4.0 21.1 %collective-permute-start.7 = (f32[64,2048]{1,0:T(8,128)S(1)}, f32[64,2048]{1,0:T(8,128)S(1)}, u32[]{:S(2)}, u32[]{:S(2)}) collective-permute-start(f32[64,2048]{1,0:T(8,128)S(1)} %get-tuple-element.25), channel_id=1, source_target_pairs={{0,4},{4,8},{8,12},{12,16},{16,20},{20,24},{24,28},{1,5},{5,9},{9,... | collective-permute-start | bytes 1572872 | tf_op jit(solution)/shard_map/ppermute | solution.py:413
  8.5 12.1 %collective-permute-start.1 = (f32[192,256]{1,0:T(8,128)S(1)}, f32[192,256]{1,0:T(8,128)S(1)}, u32[]{:S(2)}, u32[]{:S(2)}) collective-permute-start(f32[192,256]{1,0:T(8,128)S(1)} %slice_add_fusion), channel_id=1, source_target_pairs={{0,2},{1,3},{2,0},{3,1},{4,6},{5,7},{6,4},{7,5},{8,10},{9,11},{10,... | collective-permute-start | bytes 589832 | tf_op jit(solution)/shard_map/ppermute | solution.py:409
  10.1 7.1 %collective-permute-start.3 = (f32[72,256]{1,0:T(8,128)S(1)}, f32[72,256]{1,0:T(8,128)S(1)}, u32[]{:S(2)}, u32[]{:S(2)}) collective-permute-start(f32[72,256]{1,0:T(8,128)S(1)} %slice_add_fusion.1), channel_id=1, source_target_pairs={{0,2},{1,3},{2,0},{3,1},{4,6},{5,7},{6,4},{7,5},{8,10},{9,11},{10,... | collective-permute-start | bytes 221192 | tf_op jit(solution)/shard_map/ppermute | solution.py:409
  17.2 6.1 %collective-permute-start.5 = (f32[72,256]{1,0:T(8,128)S(1)}, f32[72,256]{1,0:T(8,128)S(1)}, u32[]{:S(2)}, u32[]{:S(2)}) collective-permute-start(f32[72,256]{1,0:T(8,128)S(1)} %add.20.own_tail_ref.counts_own_ref.cown_ref), channel_id=1, source_target_pairs={{0,4},{4,8},{8,12},{12,16},{16,20},{20,24},{24,28},{1,5},{5,9},{9,... | collective-permute-start | bytes 221192 | tf_op jit(solution)/shard_map/ppermute | solution.py:413
  20.6 5.5 %collective-permute-start.2 = (f32[192,256]{1,0:T(8,128)S(1)}, f32[192,256]{1,0:T(8,128)S(1)}, u32[]{:S(2)}, u32[]{:S(2)}) collective-permute-start(f32[192,256]{1,0:T(8,128)S(1)} %add.18.own_ref), channel_id=1, source_target_pairs={{0,1},{1,0},{2,3},{3,2},{4,5},{5,4},{6,7},{7,6},{8,9},{9,8},{10,11... | collective-permute-start | bytes 589832 | tf_op jit(solution)/shard_map/ppermute | solution.py:409
  22.7 3.4 %collective-permute-start.4 = (f32[72,256]{1,0:T(8,128)S(1)}, f32[72,256]{1,0:T(8,128)S(1)}, u32[]{:S(2)}, u32[]{:S(2)}) collective-permute-start(f32[72,256]{1,0:T(8,128)S(1)} %add.20.own_tail_ref.counts_own_ref.cown_ref), channel_id=1, source_target_pairs={{0,1},{1,0},{2,3},{3,2},{4,5},{5,4},{6,7},{7,6},{8,9},{9,8},{10,11... | collective-permute-start | bytes 221192 | tf_op jit(solution)/shard_map/ppermute | solution.py:409
  23.3 5.5 %collective-permute-start.6 = (f32[72,256]{1,0:T(8,128)S(1)}, f32[72,256]{1,0:T(8,128)S(1)}, u32[]{:S(2)}, u32[]{:S(2)}) collective-permute-start(f32[72,256]{1,0:T(8,128)S(1)} %collective-permute-done.5.prior_own_ref), channel_id=1, source_target_pairs={{0,1},{1,0},{2,3},{3,2},{4,5},{5,4},{6,7},{7,6},{8,9},{9,8},{10,11... | collective-permute-start | bytes 221192 | tf_op jit(solution)/shard_map/ppermute | solution.py:409

commit v6 on v5

--- a/solution.py
+++ b/solution.py
@@ -63,8 +63,9 @@
     tail_copy = pltpu.make_async_copy(ret_hbm.at[pl.ds(rows - W, W)], tail_ref, tail_sem)
     tail_copy.start()
     flip_ref[...] = jnp.concatenate([core_ref[...]] * (SECTORS // LANES), axis=1)
-    position = lax.broadcasted_iota(jnp.int32, inv_ref.shape, 0) + (first_ref[0:1] + 1)
-    inv_ref[...] = 1.0 / jnp.minimum(position, W).astype(f32)
+    position = lax.broadcasted_iota(jnp.int32, (W, LANES), 0) + (first_ref[0:1] + 1)
+    inv_ref[:W] = 1.0 / jnp.minimum(position, W).astype(f32)
+    inv_ref[W:] = jnp.where(first_ref[...] > 0, 1.0, 0.0)
     left_ref[rows:height] = jnp.ones((16, wide), bf16)
     left_ref[height + rows :] = jnp.zeros((16, wide), bf16)
     turn = jnp.concatenate([core_ref[0:1] * HALF] * (wide // LANES), axis=1)
@@ -155,7 +156,7 @@
 def moments_head_kernel(inv_ref, halo_ref, ret_ref, mean_ref, crr_ref):
     blocks = W // 8
     moments_body(
-        lambda group, cols: halo_ref[rows_of(group), cols]
+        lambda group, cols: halo_ref[rows_of(group), cols] * inv_ref[W:]
         if group < blocks
         else ret_ref[rows_of(group - blocks), cols],
         lambda group: inv_ref[rows_of(group)],
@@ -291,7 +292,8 @@
         cols = pl.ds((tile * LANES) % HALF, LANES)
         scale = 1.0 / jnp.maximum(counts[W : W + 8, cols], 1.0)
         means = [
-            (prior[rows_of(g), cols] if g < blocks else here[rows_of(g - blocks), cols]) * scale
+            (prior[rows_of(g), cols] * inv_ref[W:] if g < blocks else here[rows_of(g - blocks), cols])
+            * scale
             for g in range(2 * blocks)
         ]
         sector_rows(
@@ -316,6 +318,7 @@
                 g = group - blocks
                 if g < 0:
                     product = halo_ref[rows_of(group), cols] * spread_ref[rows_of(group), inner]
+                    product = product * inv_ref[W:]
                 else:
                     product = ret_ref[rows_of(g), cols] * factor_ref[rows_of(g), cols]
                 product = cross.push(product, row)
@@ -410,7 +413,8 @@
 
 
 def ahead(value, axis):
-    return lax.ppermute(value, axis, [(i, i + 1) for i in range(lax.axis_size(axis) - 1)])
+    count = lax.axis_size(axis)
+    return lax.ppermute(value, axis, [(i, (i + 1) % count) for i in range(count)])
 
 
 def across(value, axis):
@@ -438,7 +442,7 @@
             jax.ShapeDtypeStruct((rows, width), f32),
             jax.ShapeDtypeStruct((W, width), f32),
             jax.ShapeDtypeStruct((8, SECTORS), jnp.int32),
-            jax.ShapeDtypeStruct((W, LANES), f32),
+            jax.ShapeDtypeStruct((W + 8, LANES), f32),
         ),
         in_specs=[hbm, hbm, VMEM, VMEM],
         out_specs=[VMEM] * 7,
@@ -462,7 +466,7 @@
     swapped = swap(send, "series", 1)
     own_tail = across(keep[main:] + swapped[main:], "series")
     own = across(keep[:main] + swapped[:main], "series")
-    prior_own = ahead(own_tail, "tm")
+    prior_own = ahead(own_tail[:W], "tm")
     other_tail = swap(own_tail, "series", 1)
     other = swap(own, "series", 1)
     prior_other = swap(prior_own, "series", 1)

time: 46 us -> 43.7 us (0.950)
  waiting for transfers between devices: 6.5 us -> 11 us
  starting transfers between devices: 11.3 us -> 6.99 us
  blocking collectives: 13.1 us -> 10.4 us
    ppermute x2, waiting for transfers between devices: 0.01 us -> 4.63 us  [ahead(): lax.ppermute(value, axis, [(i, (i + 1) % count) for i in range(count)])]
    ppermute x2, starting transfers between devices: 7.84 us -> 4.14 us  [ahead(): lax.ppermute(value, axis, [(i, (i + 1) % count) for i in range(count)])]
    all_to_all x1, blocking collectives: 13.1 us -> 10.4 us  [step(): parts = lax.all_to_all(totals, ('tm', 'series'), 0, 0)]
    ppermute x6, starting transfers between devices: 3.44 us -> 2.85 us  [swap(): lax.ppermute(value, axis, [(i, i ^ bit) for i in range(lax.axis_size(axis...]
  transfers between devices with their start and end apart: 8 -> 8, of which waited for: 1 -> 3; matrix products, arithmetic and copies ran while one was open for 0% -> 0% of each run, Pallas kernels for 16% -> 18%
where the time goes in v6:
time: 43.7 us; the launch traced here: 43.5 us
  Pallas kernels  14.2 us (32%)
  waiting for transfers between devices  11 us (25%)
  blocking collectives  10.4 us (24%)
  starting transfers between devices  6.99 us (16%)
  local copies, waits for them, and re-layouts  0.78 us (2%)
    all_to_all x1, blocking collectives, step(): parts = lax.all_to_all(totals, ('tm', 'series'), 0, 0)  10.4 us
    pallas_call x5, Pallas kernels, kernel_of(): pl.pallas_call(body, out_shape=tuple((o if hasattr(o, 'dtype') else jax.S...  9.93 us
    ppermute x6, waiting for transfers between devices, swap(): lax.ppermute(value, axis, [(i, i ^ bit) for i in range(lax.axis_size(axis...  6.35 us
    ppermute x2, waiting for transfers between devices, ahead(): lax.ppermute(value, axis, [(i, (i + 1) % count) for i in range(count)])  4.63 us
    ppermute x2, starting transfers between devices, ahead(): lax.ppermute(value, axis, [(i, (i + 1) % count) for i in range(count)])  4.14 us
    ppermute x6, starting transfers between devices, swap(): lax.ppermute(value, axis, [(i, i ^ bit) for i in range(lax.axis_size(axis...  2.85 us
    pallas_call x1, Pallas kernels, step(): pl.pallas_call(load_kernel, out_shape=(jax.ShapeDtypeStruct((rows + 8, HA...  2.72 us
    pallas_call x1, Pallas kernels, shrink(): pl.pallas_call(functools.partial(shrink_kernel, float(all_steps)), out_sh...  1.59 us
  transfers between devices with their start and end apart: 8, of which 3 were waited for; matrix products, arithmetic and copies ran while one was open for 0% of the time, Pallas kernels for 18%

profile of v6, /device:TPU:0, one launch (start us, length us, event | category | flops | bytes accessed | tf_op | source)
XLA Modules:
  0.0 43.5 jit_solution(1830999302261959361)
XLA Ops:
  0.0 0.0 copy-start
  0.0 0.7 %copy-done = s32[2048]{0:T(1024)S(1)} copy-done((s32[2048]{0:T(1024)S(1)}, s32[2048]{0:T(1024)}, u32[]{:S(2)}) %copy-start) | copy-done | bytes 8216
  0.7 2.7 %load.1 = (f32[264,256]{1,0:T(8,128)S(1)}, f32[264,256]{1,0:T(8,128)S(1)}, bf16[512,2048]{1,0:T(8,128)(2,1)S(1)}, f32[256,2048]{1,0:T(8,128)S(1)}, f32[64,2048]{...) custom-call(f32[256,2048]{1,0:T(8,128)} %ret_hbm.1, s32[1,2048]{1,0:T(1,128)S(1)} %bitcast.7, ...), custom_call_target="tpu_custom_call" | custom-call | tf_op jit(solution)/shard_map/load/pallas_call | solution.py:436
  3.4 0.6 %collective-permute-start = (f32[264,256]{1,0:T(8,128)S(1)}, f32[264,256]{1,0:T(8,128)S(1)}, u32[]{:S(2)}, u32[]{:S(2)}) collective-permute-start(f32[264,256]{1,0:T(8,128)S(1)} %get-tuple-element.24), channel_id=1, source_target_pairs={{0,1},{1,0},{2,3},{3,2},{4,5},{5,4},{6,7},{7,6},{8,9},{9,8},{10,11... | collective-permute-start | bytes 811016 | tf_op jit(solution)/shard_map/ppermute | solution.py:412
  4.0 2.6 %collective-permute-start.7 = (f32[64,2048]{1,0:T(8,128)S(1)}, f32[64,2048]{1,0:T(8,128)S(1)}, u32[]{:S(2)}, u32[]{:S(2)}) collective-permute-start(f32[64,2048]{1,0:T(8,128)S(1)} %get-tuple-element.25), channel_id=1, source_target_pairs={{0,4},{4,8},{8,12},{12,16},{16,20},{20,24},{24,28},{28,0},{1,5},{5... | collective-permute-start | bytes 1572872 | tf_op jit(solution)/shard_map/ppermute | solution.py:417
  6.5 0.0 collective-permute-done
  6.6 1.6 %collective-permute-start.1 = (f32[192,256]{1,0:T(8,128)S(1)}, f32[192,256]{1,0:T(8,128)S(1)}, u32[]{:S(2)}, u32[]{:S(2)}) collective-permute-start(f32[192,256]{1,0:T(8,128)S(1)} %slice_add_fusion), channel_id=1, source_target_pairs={{0,2},{1,3},{2,0},{3,1},{4,6},{5,7},{6,4},{7,5},{8,10},{9,11},{10,... | collective-permute-start | bytes 589832 | tf_op jit(solution)/shard_map/ppermute | solution.py:412
  8.2 0.6 %collective-permute-start.3 = (f32[72,256]{1,0:T(8,128)S(1)}, f32[72,256]{1,0:T(8,128)S(1)}, u32[]{:S(2)}, u32[]{:S(2)}) collective-permute-start(f32[72,256]{1,0:T(8,128)S(1)} %slice_add_fusion.1), channel_id=1, source_target_pairs={{0,2},{1,3},{2,0},{3,1},{4,6},{5,7},{6,4},{7,5},{8,10},{9,11},{10,... | collective-permute-start | bytes 221192 | tf_op jit(solution)/shard_map/ppermute | solution.py:412
  8.7 5.7 %collective-permute-done.1 = f32[192,256]{1,0:T(8,128)S(1)} collective-permute-done((f32[192,256]{1,0:T(8,128)S(1)}, f32[192,256]{1,0:T(8,128)S(1)}, u32[]{:S(2)}, u32[]{:S(2)}) %collective-permute-start.1) | collective-permute-done | bytes 196640 | tf_op jit(solution)/shard_map/ppermute | solution.py:412
  14.4 0.1 collective-permute-start.2
  14.5 0.7 %collective-permute-done.3 = f32[72,256]{1,0:T(8,128)S(1)} collective-permute-done((f32[72,256]{1,0:T(8,128)S(1)}, f32[72,256]{1,0:T(8,128)S(1)}, u32[]{:S(2)}, u32[]{:S(2)}) %collective-permute-start.3) | collective-permute-done | bytes 73760 | tf_op jit(solution)/shard_map/ppermute | solution.py:412
  15.2 1.6 %collective-permute-start.5 = (f32[64,256]{1,0:T(8,128)S(1)}, f32[64,256]{1,0:T(8,128)S(1)}, u32[]{:S(2)}, u32[]{:S(2)}) collective-permute-start(f32[64,256]{1,0:T(8,128)S(1)} %slice.22), channel_id=1, source_target_pairs={{0,4},{4,8},{8,12},{12,16},{16,20},{20,24},{24,28},{28,0},{1,5},{5... | collective-permute-start | bytes 196616 | tf_op jit(solution)/shard_map/ppermute | solution.py:417
  16.8 2.0 %shard_map.29 = (f32[192,2048]{1,0:T(8,128)S(1)}, f32[192,2048]{1,0:T(8,128)S(1)}) custom-call(f32[256,2048]{1,0:T(8,128)S(1)} %get-tuple-element.26.ret_ref), custom_call_target="tpu_custom_call" | custom-call | flops 15728640 | bytes 4718592 | tf_op jit(solution)/shard_map/pallas_call | solution.py:356
  18.8 0.1 collective-permute-start.4
  18.9 4.6 %collective-permute-done.5.prior_own_ref = f32[64,256]{1,0:T(8,128)S(1)} collective-permute-done((f32[64,256]{1,0:T(8,128)S(1)}, f32[64,256]{1,0:T(8,128)S(1)}, u32[]{:S(2)}, u32[]{:S(2)}) %collective-permute-start.5) | collective-permute-done | bytes 65568 | tf_op jit(solution)/shard_map/ppermute | solution.py:417
  23.5 0.0 collective-permute-start.6
  23.5 1.7 %shard_map.28.spread_ref = f32[640,2048]{1,0:T(8,128)S(1)} custom-call(f32[192,256]{1,0:T(8,128)S(1)} %add.18.own_ref, f32[72,256]{1,0:T(8,128)S(1)} %add.20.own_tail_ref.counts_own_ref.cown_ref, bf16[512,2048]{1,0:T(8,128)(2,1)S(1)} %get-tuple-element.27.table_ref), custom_call_target="tpu_custom_call" | custom-call | flops 1342177280 | bytes 5242880 | tf_op jit(solution)/shard_map/pallas_call | solution.py:356
  25.3 0.0 collective-permute-done.7.halo_ref
  25.3 1.1 %shard_map.31 = (f32[64,2048]{1,0:T(8,128)S(1)}, f32[64,2048]{1,0:T(8,128)S(1)}) custom-call(f32[72,128]{1,0:T(8,128)S(1)} %get-tuple-element.22.inv_ref, f32[64,2048]{1,0:T(8,128)S(1)} %collective-permute-done.7.halo_ref, f32[256,2048]{1,0:T(8,128)S(1)} %get-tuple-element.26.ret_ref), custom_call_target="tpu_custom_call" | custom-call | flops 5242880 | bytes 1572864 | tf_op jit(solution)/shard_map/pallas_call | solution.py:356
  26.3 0.0 collective-permute-done.4.other_tail_ref.counts_other_ref.cother_ref
  26.3 0.0 collective-permute-done.2.other_ref
  26.4 2.9 %shard_map.30 = (f32[192,2048]{1,0:T(8,128)S(1)}, f32[64,2048]{1,0:T(8,128)S(1)}, f32[8,2048]{1,0:T(8,128)S(1)}) custom-call(f32[192,256]{1,0:T(8,128)S(1)} %collective-permute-done.2.other_ref, f32[72,256]{1,0:T(8,128)S(1)} %collective-permute-done.4.other_tail_ref.counts_other_ref.cother_ref, f32[640,2048]{1,0:T(8,128)S(1)} %shard_map.28.spread_ref, ...), custom_call_target="tpu_custom_call" | custom-call | flops 2684354560 | bytes 6291456 | tf_op jit(solution)/shard_map/pallas_call | solution.py:356
  29.2 0.0 collective-permute-done.6.prior_other_ref
  29.3 2.2 %shard_map.32 = (f32[64,2048]{1,0:T(8,128)S(1)}, f32[32,512]{1,0:T(8,128)S(1)}) custom-call(f32[72,128]{1,0:T(8,128)S(1)} %get-tuple-element.22.inv_ref, s32[8,512]{1,0:T(8,128)S(1)} %get-tuple-element.21.flip_ref, f32[192,256]{1,0:T(8,128)S(1)} %add.18.own_ref, f32[192,256]{1,0:T(8,128)S(1)} %collective-permute-done.2.other_ref, ...), custom_call_target="tpu_custom_call" | custom-call | flops 1073741824 | bytes 1572864 | tf_op jit(solution)/shard_map/pallas_call | solution.py:356
  31.5 0.1 copy.3
  31.6 10.4 %all_to_all.11 = f32[32,1,512]{2,1,0:T(1,128)S(1)} all-to-all(f32[32,1,512]{2,1,0:T(1,128)S(1)} %copy.3), channel_id=1, replica_groups=mesh['tm'=8,'series'=4] {'tm','series'}, dimensions={0} | all-to-all | bytes 131072 | tf_op jit(solution)/shard_map/all_to_all | solution.py:503
  41.9 1.6 %shrink.1 = f32[256,2048]{1,0:T(8,128)} custom-call(s32[8,512]{1,0:T(8,128)S(1)} %get-tuple-element.21.flip_ref, f32[32,512]{1,0:T(8,128)S(1)} %bitcast.5, f32[72,256]{1,0:T(8,128)S(1)} %add.20.own_tail_ref.counts_own_ref.cown_ref, f32[72,256]{1,0:T(8,128)S(1)} %collective-permute-done.4.other_tail_ref.counts_other_ref.cother_ref, ...), custom_call_target="tpu_custom_call" | custom-call | flops 1048576 | bytes 4194304 | tf_op jit(solution)/shard_map/shrink/pallas_call | solution.py:394
  (8 shorter events, 0.1 us)
Async XLA Ops:
  0.0 0.7 %copy-start = (s32[2048]{0:T(1024)S(1)}, s32[2048]{0:T(1024)}, u32[]{:S(2)}) copy-start(s32[2048]{0:T(1024)} %param.3) | copy-start | bytes 24580
  3.4 3.1 %collective-permute-start = (f32[264,256]{1,0:T(8,128)S(1)}, f32[264,256]{1,0:T(8,128)S(1)}, u32[]{:S(2)}, u32[]{:S(2)}) collective-permute-start(f32[264,256]{1,0:T(8,128)S(1)} %get-tuple-element.24), channel_id=1, source_target_pairs={{0,1},{1,0},{2,3},{3,2},{4,5},{5,4},{6,7},{7,6},{8,9},{9,8},{10,11... | collective-permute-start | bytes 811016 | tf_op jit(solution)/shard_map/ppermute | solution.py:412
  4.0 21.3 %collective-permute-start.7 = (f32[64,2048]{1,0:T(8,128)S(1)}, f32[64,2048]{1,0:T(8,128)S(1)}, u32[]{:S(2)}, u32[]{:S(2)}) collective-permute-start(f32[64,2048]{1,0:T(8,128)S(1)} %get-tuple-element.25), channel_id=1, source_target_pairs={{0,4},{4,8},{8,12},{12,16},{16,20},{20,24},{24,28},{28,0},{1,5},{5... | collective-permute-start | bytes 1572872 | tf_op jit(solution)/shard_map/ppermute | solution.py:417
  6.6 7.8 %collective-permute-start.1 = (f32[192,256]{1,0:T(8,128)S(1)}, f32[192,256]{1,0:T(8,128)S(1)}, u32[]{:S(2)}, u32[]{:S(2)}) collective-permute-start(f32[192,256]{1,0:T(8,128)S(1)} %slice_add_fusion), channel_id=1, source_target_pairs={{0,2},{1,3},{2,0},{3,1},{4,6},{5,7},{6,4},{7,5},{8,10},{9,11},{10,... | collective-permute-start | bytes 589832 | tf_op jit(solution)/shard_map/ppermute | solution.py:412
  8.2 7.0 %collective-permute-start.3 = (f32[72,256]{1,0:T(8,128)S(1)}, f32[72,256]{1,0:T(8,128)S(1)}, u32[]{:S(2)}, u32[]{:S(2)}) collective-permute-start(f32[72,256]{1,0:T(8,128)S(1)} %slice_add_fusion.1), channel_id=1, source_target_pairs={{0,2},{1,3},{2,0},{3,1},{4,6},{5,7},{6,4},{7,5},{8,10},{9,11},{10,... | collective-permute-start | bytes 221192 | tf_op jit(solution)/shard_map/ppermute | solution.py:412
  14.4 11.9 %collective-permute-start.2 = (f32[192,256]{1,0:T(8,128)S(1)}, f32[192,256]{1,0:T(8,128)S(1)}, u32[]{:S(2)}, u32[]{:S(2)}) collective-permute-start(f32[192,256]{1,0:T(8,128)S(1)} %add.18.own_ref), channel_id=1, source_target_pairs={{0,1},{1,0},{2,3},{3,2},{4,5},{5,4},{6,7},{7,6},{8,9},{9,8},{10,11... | collective-permute-start | bytes 589832 | tf_op jit(solution)/shard_map/ppermute | solution.py:412
  15.2 8.3 %collective-permute-start.5 = (f32[64,256]{1,0:T(8,128)S(1)}, f32[64,256]{1,0:T(8,128)S(1)}, u32[]{:S(2)}, u32[]{:S(2)}) collective-permute-start(f32[64,256]{1,0:T(8,128)S(1)} %slice.22), channel_id=1, source_target_pairs={{0,4},{4,8},{8,12},{12,16},{16,20},{20,24},{24,28},{28,0},{1,5},{5... | collective-permute-start | bytes 196616 | tf_op jit(solution)/shard_map/ppermute | solution.py:417
  18.8 7.5 %collective-permute-start.4 = (f32[72,256]{1,0:T(8,128)S(1)}, f32[72,256]{1,0:T(8,128)S(1)}, u32[]{:S(2)}, u32[]{:S(2)}) collective-permute-start(f32[72,256]{1,0:T(8,128)S(1)} %add.20.own_tail_ref.counts_own_ref.cown_ref), channel_id=1, source_target_pairs={{0,1},{1,0},{2,3},{3,2},{4,5},{5,4},{6,7},{7,6},{8,9},{9,8},{10,11... | collective-permute-start | bytes 221192 | tf_op jit(solution)/shard_map/ppermute | solution.py:412
  23.5 5.7 %collective-permute-start.6 = (f32[64,256]{1,0:T(8,128)S(1)}, f32[64,256]{1,0:T(8,128)S(1)}, u32[]{:S(2)}, u32[]{:S(2)}) collective-permute-start(f32[64,256]{1,0:T(8,128)S(1)} %collective-permute-done.5.prior_own_ref), channel_id=1, source_target_pairs={{0,1},{1,0},{2,3},{3,2},{4,5},{5,4},{6,7},{7,6},{8,9},{9,8},{10,11... | collective-permute-start | bytes 196616 | tf_op jit(solution)/shard_map/ppermute | solution.py:412

commit v7 on v6

--- a/solution.py
+++ b/solution.py
@@ -166,7 +166,7 @@
     )
 
 
-def sector_rows(means, inv, groups, starts, left_ref, out, low, kept=None):
+def sector_rows(means, inv, groups, starts, left_ref, out, low, kept=slice(None)):
     row = lax.broadcasted_iota(jnp.int32, (8, LANES), 0)
     first, second = Window(), Window()
     mean_parts, gain_parts = [], []
@@ -179,7 +179,7 @@
             spread = squares * scale - mean_f * mean_f + ridge_rate
             mean_parts.append(mean_f)
             gain_parts.append((1.0 - shrink_weight) * scale * scale / spread)
-    for start, parts in zip(starts, (means[:kept], mean_parts, gain_parts)):
+    for start, parts in zip(starts, (means[kept], mean_parts, gain_parts)):
         for pair in range(0, len(parts), 2):
             hi, lo = split2(jnp.concatenate(parts[pair : pair + 2], axis=0))
             here = slice(start + pair * 8, start + pair * 8 + 16)
@@ -208,19 +208,29 @@
     return pl.ds(pl.multiple_of(index * wide, wide), wide)
 
 
-def main_rows(sums_ref, tail_ref, left_ref):
-    main = sums_ref.shape[0]
-    rows = main + W
+def early_rows(early_ref, tail_ref, left_ref):
+    rows = early_ref.shape[0]
     for tile in range(HALF // LANES):
         cols = slice(tile * LANES, (tile + 1) * LANES)
         scale = 1.0 / jnp.maximum(tail_ref[W : W + 8, cols], 1.0)
-        means = [
-            (sums_ref[rows_of(g), cols] if g < main // 8 else tail_ref[rows_of(g - main // 8), cols])
-            * scale
-            for g in range(rows // 8)
-        ]
+        means = [early_ref[rows_of(g), cols] * scale for g in range(rows // 8)]
+        starts = (0, rows, 2 * rows - W)
+        sector_rows(means, lambda g: 1.0 / W, rows // 8, starts, left_ref, tile * LANES, HALF)
+
+
+def late_rows(early_ref, late_ref, tail_ref, left_ref, base):
+    before, middle = early_ref.shape[0], late_ref.shape[0]
+    rows = middle + W
+    for tile in range(HALF // LANES):
+        cols = slice(tile * LANES, (tile + 1) * LANES)
+        scale = 1.0 / jnp.maximum(tail_ref[W : W + 8, cols], 1.0)
+        sums = [early_ref[rows_of(g), cols] for g in range((before - W) // 8, before // 8)]
+        sums += [late_ref[rows_of(g), cols] for g in range(middle // 8)]
+        sums += [tail_ref[rows_of(g), cols] for g in range(W // 8)]
+        starts = (base, base + rows, base + 2 * rows)
         sector_rows(
-            means, lambda g: 1.0 / W, rows // 8, (0, rows, rows + main), left_ref, tile * LANES, HALF
+            [part * scale for part in sums], lambda g: 1.0 / W, len(sums), starts, left_ref,
+            tile * LANES, HALF, slice(W // 8, None),
         )
 
 
@@ -228,28 +238,53 @@
     return jnp.concatenate([table, table], axis=0)
 
 
-def own_kernel(own_ref, own_tail_ref, table_ref, spread_ref, left_ref):
-    main_rows(own_ref, own_tail_ref, left_ref)
+def spread_half(left_ref, table_ref, spread_ref):
     wide = 4 * LANES
     for index in range(table_ref.shape[1] // wide):
         cols = slice(index * wide, (index + 1) * wide)
         spread_ref[:, cols] = dot_nn(left_ref[...], twice(table_ref[:HALF, cols]))
 
 
+def own_early_kernel(early_ref, tail_ref, table_ref, spread_ref, left_ref):
+    early_rows(early_ref, tail_ref, left_ref)
+    spread_half(left_ref, table_ref, spread_ref)
+
+
+def own_late_kernel(early_ref, late_ref, tail_ref, table_ref, spread_ref, left_ref):
+    late_rows(early_ref, late_ref, tail_ref, left_ref, 0)
+    spread_half(left_ref, table_ref, spread_ref)
+
+
 def main_kernel(
-    other_ref, other_tail_ref, spread_ref, ret_ref, total_ref, crr_ref, table_ref,
+    early_ref, late_ref, tail_ref, spread_early_ref, spread_late_ref, ret_ref, total_ref, crr_ref, table_ref,
     var_ref, factor_ref, colsum_ref, left_ref, even_ref, odd_ref,
 ):
     rows = ret_ref.shape[0]
-    main = rows - W
     blocks = W // 8
-    main_rows(other_ref, other_tail_ref, left_ref)
+    base = spread_early_ref.shape[0]
+    early = early_ref.shape[0] // 8
+    late = rows // 8 - early
+    opening = early - blocks
+
+    def factor_at(group):
+        return rows_of(group if group < early else base // 8 + group - early)
+
+    def mean_at(g):
+        return rows_of(early + g if g < opening else base // 8 + late + g - opening)
+
+    def gain_at(g):
+        return rows_of(early + opening + g if g < opening else base // 8 + 2 * late + g - opening)
+
+    early_rows(early_ref, tail_ref, left_ref)
+    late_rows(early_ref, late_ref, tail_ref, left_ref, base)
     row = lax.broadcasted_iota(jnp.int32, (8, LANES), 0)
     wide = even_ref.shape[1]
 
     def fill(buffer, index):
         cols = chunk_at(index, wide)
-        buffer[...] = spread_ref[:, cols] + dot_nn(left_ref[...], twice(table_ref[HALF:, cols]))
+        other = dot_nn(left_ref[...], twice(table_ref[HALF:, cols]))
+        buffer[:base] = spread_early_ref[:, cols] + other[:base]
+        buffer[base:] = spread_late_ref[:, cols] + other[base:]
 
     def work(spread_ref, index):
         for tile in range(wide // LANES):
@@ -258,14 +293,14 @@
             cross = Window()
             total = jnp.zeros((8, LANES), f32)
             for group in range(rows // 8):
-                factor = spread_ref[rows_of(group), inner]
+                factor = spread_ref[factor_at(group), inner]
                 if group < blocks:
                     factor_ref[rows_of(group), cols] = factor
                 product = cross.push(ret_ref[rows_of(group), cols] * factor, row)
                 if group >= blocks:
                     g = group - blocks
-                    mean_f = spread_ref[rows_of(rows // 8 + g), inner]
-                    gain = spread_ref[rows_of((rows + main) // 8 + g), inner]
+                    mean_f = spread_ref[mean_at(g), inner]
+                    gain = spread_ref[gain_at(g), inner]
                     crf = product - total_ref[rows_of(g), cols] * mean_f
                     variance = crr_ref[rows_of(g), cols] - crf * crf * gain
                     var_ref[rows_of(g), cols] = variance
@@ -298,7 +333,7 @@
         ]
         sector_rows(
             means, lambda g: inv_ref[rows_of(g)], 2 * blocks, (0, W, 2 * W), left_ref,
-            tile * LANES, SECTORS, blocks,
+            tile * LANES, SECTORS, slice(blocks),
         )
     row = lax.broadcasted_iota(jnp.int32, (8, LANES), 0)
     wide = even_ref.shape[1]
@@ -465,13 +500,16 @@
     halo = ahead(tail, "tm")
     swapped = swap(send, "series", 1)
     own_tail = across(keep[main:] + swapped[main:], "series")
-    own = across(keep[:main] + swapped[:main], "series")
+    half = rows // 2
+    early = across(keep[:half] + swapped[:half], "series")
+    late = across(keep[half:main] + swapped[half:main], "series")
     prior_own = ahead(own_tail[:W], "tm")
     other_tail = swap(own_tail, "series", 1)
-    other = swap(own, "series", 1)
+    other_early = swap(early, "series", 1)
+    other_late = swap(late, "series", 1)
     prior_other = swap(prior_own, "series", 1)
     chunk = 4 * LANES
-    lhs = 3 * rows - 2 * W
+    lhs_early, lhs_late = 3 * half - 2 * W, 3 * half
     mean, crr = kernel_call(
         moments_main_kernel, [(main, width)] * 2, [returns],
         flops=40 * main * width, moved=12 * main * width,
@@ -480,20 +518,26 @@
         moments_head_kernel, [(W, width)] * 2, [inv, halo, returns],
         flops=40 * W * width, moved=12 * W * width,
     )
-    left = [pltpu.VMEM((lhs, SECTORS), bf16)]
-    (spread,) = kernel_call(
-        own_kernel, [(lhs, width)], [own, own_tail, table], scratch=left,
-        flops=2 * lhs * width * SECTORS, moved=4 * lhs * width,
-    )
+    (spread_early,) = kernel_call(
+        own_early_kernel, [(lhs_early, width)], [early, own_tail, table],
+        scratch=[pltpu.VMEM((lhs_early, SECTORS), bf16)],
+        flops=2 * lhs_early * width * SECTORS, moved=4 * lhs_early * width,
+    )
+    (spread_late,) = kernel_call(
+        own_late_kernel, [(lhs_late, width)], [early, late, own_tail, table],
+        scratch=[pltpu.VMEM((lhs_late, SECTORS), bf16)],
+        flops=2 * lhs_late * width * SECTORS, moved=4 * lhs_late * width,
+    )
+    lhs = lhs_early + lhs_late
     var, factor, colsum = kernel_call(
         main_kernel, [(main, width), (W, width), (8, width)],
-        [other, other_tail, spread, returns, mean, crr, table],
-        scratch=left + [pltpu.VMEM((lhs, chunk), f32)] * 2,
+        [other_early, other_late, other_tail, spread_early, spread_late, returns, mean, crr, table],
+        scratch=[pltpu.VMEM((lhs, SECTORS), bf16)] + [pltpu.VMEM((lhs, chunk), f32)] * 2,
         flops=4 * lhs * width * SECTORS, moved=12 * rows * width,
     )
     var_head, totals = kernel_call(
         head_kernel, [(W, width), (n_time * n_series, SECTORS)],
-        [inv, flip, own, other, own_tail, other_tail, prior_own, prior_other, halo, returns, factor,
+        [inv, flip, early, other_early, own_tail, other_tail, prior_own, prior_other, halo, returns, factor,
          mean_head, crr_head, colsum, table],
         scratch=[pltpu.VMEM((3 * W, 2 * SECTORS), bf16)]
         + [pltpu.VMEM((3 * W, chunk), f32)] * 2

time: 43.7 us -> 42.8 us (0.979)
  waiting for transfers between devices: 11 us -> 7.92 us
  starting transfers between devices: 6.99 us -> 9.13 us
    ppermute x6 -> x8, waiting for transfers between devices: 6.35 us -> 4.2 us  [swap(): lax.ppermute(value, axis, [(i, i ^ bit) for i in range(lax.axis_size(axis...]
    ppermute x6 -> x8, starting transfers between devices: 2.85 us -> 4.99 us  [swap(): lax.ppermute(value, axis, [(i, i ^ bit) for i in range(lax.axis_size(axis...]
    ppermute x2, waiting for transfers between devices: 4.63 us -> 3.73 us  [ahead(): lax.ppermute(value, axis, [(i, (i + 1) % count) for i in range(count)])]
    pallas_call x5 -> x6, Pallas kernels: 9.93 us -> 9.91 us  [kernel_of(): pl.pallas_call(body, out_shape=tuple((o if hasattr(o, 'dtype') else jax.S...]
  transfers between devices with their start and end apart: 8 -> 10, of which waited for: 3 -> 2; matrix products, arithmetic and copies ran while one was open for 0% -> 0% of each run, Pallas kernels for 18% -> 18%
where the time goes in v7:
time: 42.8 us; the launch traced here: 42.6 us
  Pallas kernels  14.2 us (33%)
  blocking collectives  10.3 us (24%)
  starting transfers between devices  9.13 us (21%)
  waiting for transfers between devices  7.92 us (19%)
  local copies, waits for them, and re-layouts  0.78 us (2%)
    all_to_all x1, blocking collectives, step(): parts = lax.all_to_all(totals, ('tm', 'series'), 0, 0)  10.3 us
    pallas_call x6, Pallas kernels, kernel_of(): pl.pallas_call(body, out_shape=tuple((o if hasattr(o, 'dtype') else jax.S...  9.91 us
    ppermute x8, starting transfers between devices, swap(): lax.ppermute(value, axis, [(i, i ^ bit) for i in range(lax.axis_size(axis...  4.99 us
    ppermute x8, waiting for transfers between devices, swap(): lax.ppermute(value, axis, [(i, i ^ bit) for i in range(lax.axis_size(axis...  4.2 us
    ppermute x2, starting transfers between devices, ahead(): lax.ppermute(value, axis, [(i, (i + 1) % count) for i in range(count)])  4.14 us
    ppermute x2, waiting for transfers between devices, ahead(): lax.ppermute(value, axis, [(i, (i + 1) % count) for i in range(count)])  3.73 us
    pallas_call x1, Pallas kernels, step(): pl.pallas_call(load_kernel, out_shape=(jax.ShapeDtypeStruct((rows + 8, HA...  2.72 us
    pallas_call x1, Pallas kernels, shrink(): pl.pallas_call(functools.partial(shrink_kernel, float(all_steps)), out_sh...  1.59 us
  transfers between devices with their start and end apart: 10, of which 2 were waited for; matrix products, arithmetic and copies ran while one was open for 0% of the time, Pallas kernels for 18%

profile of v7, /device:TPU:0, one launch (start us, length us, event | category | flops | bytes accessed | tf_op | source)
XLA Modules:
  0.0 42.6 jit_solution(13968834778232495159)
XLA Ops:
  0.0 0.0 copy-start
  0.0 0.7 %copy-done = s32[2048]{0:T(1024)S(1)} copy-done((s32[2048]{0:T(1024)S(1)}, s32[2048]{0:T(1024)}, u32[]{:S(2)}) %copy-start) | copy-done | bytes 8216
  0.7 2.7 %load.1 = (f32[264,256]{1,0:T(8,128)S(1)}, f32[264,256]{1,0:T(8,128)S(1)}, bf16[512,2048]{1,0:T(8,128)(2,1)S(1)}, f32[256,2048]{1,0:T(8,128)S(1)}, f32[64,2048]{...) custom-call(f32[256,2048]{1,0:T(8,128)} %ret_hbm.1, s32[1,2048]{1,0:T(1,128)S(1)} %bitcast.7, ...), custom_call_target="tpu_custom_call" | custom-call | tf_op jit(solution)/shard_map/load/pallas_call | solution.py:471
  3.4 0.6 %collective-permute-start = (f32[264,256]{1,0:T(8,128)S(1)}, f32[264,256]{1,0:T(8,128)S(1)}, u32[]{:S(2)}, u32[]{:S(2)}) collective-permute-start(f32[264,256]{1,0:T(8,128)S(1)} %get-tuple-element.24), channel_id=1, source_target_pairs={{0,1},{1,0},{2,3},{3,2},{4,5},{5,4},{6,7},{7,6},{8,9},{9,8},{10,11... | collective-permute-start | bytes 811016 | tf_op jit(solution)/shard_map/ppermute | solution.py:447
  4.0 2.6 %collective-permute-start.7 = (f32[64,2048]{1,0:T(8,128)S(1)}, f32[64,2048]{1,0:T(8,128)S(1)}, u32[]{:S(2)}, u32[]{:S(2)}) collective-permute-start(f32[64,2048]{1,0:T(8,128)S(1)} %get-tuple-element.25), channel_id=1, source_target_pairs={{0,4},{4,8},{8,12},{12,16},{16,20},{20,24},{24,28},{28,0},{1,5},{5... | collective-permute-start | bytes 1572872 | tf_op jit(solution)/shard_map/ppermute | solution.py:452
  6.5 0.0 collective-permute-done
  6.6 1.6 %collective-permute-start.3 = (f32[72,256]{1,0:T(8,128)S(1)}, f32[72,256]{1,0:T(8,128)S(1)}, u32[]{:S(2)}, u32[]{:S(2)}) collective-permute-start(f32[72,256]{1,0:T(8,128)S(1)} %slice_add_fusion.1), channel_id=1, source_target_pairs={{0,2},{1,3},{2,0},{3,1},{4,6},{5,7},{6,4},{7,5},{8,10},{9,11},{10,... | collective-permute-start | bytes 221192 | tf_op jit(solution)/shard_map/ppermute | solution.py:447
  8.1 0.6 %collective-permute-start.1 = (f32[128,256]{1,0:T(8,128)S(1)}, f32[128,256]{1,0:T(8,128)S(1)}, u32[]{:S(2)}, u32[]{:S(2)}) collective-permute-start(f32[128,256]{1,0:T(8,128)S(1)} %slice_add_fusion), channel_id=1, source_target_pairs={{0,2},{1,3},{2,0},{3,1},{4,6},{5,7},{6,4},{7,5},{8,10},{9,11},{10,... | collective-permute-start | bytes 393224 | tf_op jit(solution)/shard_map/ppermute | solution.py:447
  8.8 1.6 %collective-permute-start.8 = (f32[64,256]{1,0:T(8,128)S(1)}, f32[64,256]{1,0:T(8,128)S(1)}, u32[]{:S(2)}, u32[]{:S(2)}) collective-permute-start(f32[64,256]{1,0:T(8,128)S(1)} %slice_add_fusion.2), channel_id=1, source_target_pairs={{0,2},{1,3},{2,0},{3,1},{4,6},{5,7},{6,4},{7,5},{8,10},{9,11},{10,... | collective-permute-start | bytes 196616 | tf_op jit(solution)/shard_map/ppermute | solution.py:447
  10.3 4.2 %collective-permute-done.1 = f32[128,256]{1,0:T(8,128)S(1)} collective-permute-done((f32[128,256]{1,0:T(8,128)S(1)}, f32[128,256]{1,0:T(8,128)S(1)}, u32[]{:S(2)}, u32[]{:S(2)}) %collective-permute-start.1) | collective-permute-done | bytes 131104 | tf_op jit(solution)/shard_map/ppermute | solution.py:447
  14.5 0.1 collective-permute-start.2
  14.6 2.0 %shard_map.30 = (f32[192,2048]{1,0:T(8,128)S(1)}, f32[192,2048]{1,0:T(8,128)S(1)}) custom-call(f32[256,2048]{1,0:T(8,128)S(1)} %get-tuple-element.26.ret_ref), custom_call_target="tpu_custom_call" | custom-call | flops 15728640 | bytes 4718592 | tf_op jit(solution)/shard_map/pallas_call | solution.py:391
  16.6 0.0 collective-permute-done.8
  16.6 0.6 %collective-permute-start.9 = (f32[64,256]{1,0:T(8,128)S(1)}, f32[64,256]{1,0:T(8,128)S(1)}, u32[]{:S(2)}, u32[]{:S(2)}) collective-permute-start(f32[64,256]{1,0:T(8,128)S(1)} %add.28.late_ref), channel_id=1, source_target_pairs={{0,1},{1,0},{2,3},{3,2},{4,5},{5,4},{6,7},{7,6},{8,9},{9,8},{10,11... | collective-permute-start | bytes 196616 | tf_op jit(solution)/shard_map/ppermute | solution.py:447
  17.2 0.0 collective-permute-done.3
  17.2 0.1 collective-permute-start.4
  17.3 1.6 %collective-permute-start.5 = (f32[64,256]{1,0:T(8,128)S(1)}, f32[64,256]{1,0:T(8,128)S(1)}, u32[]{:S(2)}, u32[]{:S(2)}) collective-permute-start(f32[64,256]{1,0:T(8,128)S(1)} %slice.30), channel_id=1, source_target_pairs={{0,4},{4,8},{8,12},{12,16},{16,20},{20,24},{24,28},{28,0},{1,5},{5... | collective-permute-start | bytes 196616 | tf_op jit(solution)/shard_map/ppermute | solution.py:452
  18.9 0.8 %shard_map.28.spread_early_ref = f32[256,2048]{1,0:T(8,128)S(1)} custom-call(f32[128,256]{1,0:T(8,128)S(1)} %add.24.early_ref.own_ref, f32[72,256]{1,0:T(8,128)S(1)} %add.26.tail_ref.counts_own_ref.cown_ref, bf16[512,2048]{1,0:T(8,128)(2,1)S(1)} %get-tuple-element.27.table_ref), custom_call_target="tpu_custom_call" | custom-call | flops 536870912 | bytes 2097152 | tf_op jit(solution)/shard_map/pallas_call | solution.py:391
  19.7 1.1 %shard_map.29.spread_late_ref = f32[384,2048]{1,0:T(8,128)S(1)} custom-call(f32[128,256]{1,0:T(8,128)S(1)} %add.24.early_ref.own_ref, f32[64,256]{1,0:T(8,128)S(1)} %add.28.late_ref, f32[72,256]{1,0:T(8,128)S(1)} %add.26.tail_ref.counts_own_ref.cown_ref, bf16[512,2048]{1,0:T(8,128)(2,1)S(1)} %get-tuple-element.27.table_ref), custom_call_target="tpu_custom_call" | custom-call | flops 805306368 | bytes 3145728 | tf_op jit(solution)/shard_map/pallas_call | solution.py:391
  20.9 3.7 %collective-permute-done.5.prior_own_ref = f32[64,256]{1,0:T(8,128)S(1)} collective-permute-done((f32[64,256]{1,0:T(8,128)S(1)}, f32[64,256]{1,0:T(8,128)S(1)}, u32[]{:S(2)}, u32[]{:S(2)}) %collective-permute-start.5) | collective-permute-done | bytes 65568 | tf_op jit(solution)/shard_map/ppermute | solution.py:452
  24.6 0.0 collective-permute-start.6
  24.6 0.0 collective-permute-done.7.halo_ref
  24.6 1.1 %shard_map.32 = (f32[64,2048]{1,0:T(8,128)S(1)}, f32[64,2048]{1,0:T(8,128)S(1)}) custom-call(f32[72,128]{1,0:T(8,128)S(1)} %get-tuple-element.22.inv_ref, f32[64,2048]{1,0:T(8,128)S(1)} %collective-permute-done.7.halo_ref, f32[256,2048]{1,0:T(8,128)S(1)} %get-tuple-element.26.ret_ref), custom_call_target="tpu_custom_call" | custom-call | flops 5242880 | bytes 1572864 | tf_op jit(solution)/shard_map/pallas_call | solution.py:391
  25.7 0.0 collective-permute-done.9.late_ref
  25.7 0.0 collective-permute-done.4.tail_ref.counts_other_ref.cother_ref
  25.7 0.0 collective-permute-done.2.early_ref.other_ref
  25.7 2.7 %shard_map.31 = (f32[192,2048]{1,0:T(8,128)S(1)}, f32[64,2048]{1,0:T(8,128)S(1)}, f32[8,2048]{1,0:T(8,128)S(1)}) custom-call(f32[128,256]{1,0:T(8,128)S(1)} %collective-permute-done.2.early_ref.other_ref, f32[64,256]{1,0:T(8,128)S(1)} %collective-permute-done.9.late_ref, f32[72,256]{1,0:T(8,128)S(1)} %collective-permute-done.4.tail_ref.counts_other_ref.cother_ref, ...), custom_call_target="tpu_custom_call" | custom-call | flops 2684354560 | bytes 6291456 | tf_op jit(solution)/shard_map/pallas_call | solution.py:391
  28.4 0.0 collective-permute-done.6.prior_other_ref
  28.4 2.2 %shard_map.33 = (f32[64,2048]{1,0:T(8,128)S(1)}, f32[32,512]{1,0:T(8,128)S(1)}) custom-call(f32[72,128]{1,0:T(8,128)S(1)} %get-tuple-element.22.inv_ref, s32[8,512]{1,0:T(8,128)S(1)} %get-tuple-element.21.flip_ref, f32[128,256]{1,0:T(8,128)S(1)} %add.24.early_ref.own_ref, f32[128,256]{1,0:T(8,128)S(1)} %collective-permute-done.2.early_ref.other_ref, ...), custom_call_target="tpu_custom_call" | custom-call | flops 1073741824 | bytes 1572864 | tf_op jit(solution)/shard_map/pallas_call | solution.py:391
  30.6 0.1 copy.3
  30.7 10.3 %all_to_all.11 = f32[32,1,512]{2,1,0:T(1,128)S(1)} all-to-all(f32[32,1,512]{2,1,0:T(1,128)S(1)} %copy.3), channel_id=1, replica_groups=mesh['tm'=8,'series'=4] {'tm','series'}, dimensions={0} | all-to-all | bytes 131072 | tf_op jit(solution)/shard_map/all_to_all | solution.py:547
  41.0 1.6 %shrink.1 = f32[256,2048]{1,0:T(8,128)} custom-call(s32[8,512]{1,0:T(8,128)S(1)} %get-tuple-element.21.flip_ref, f32[32,512]{1,0:T(8,128)S(1)} %bitcast.5, f32[72,256]{1,0:T(8,128)S(1)} %add.26.tail_ref.counts_own_ref.cown_ref, f32[72,256]{1,0:T(8,128)S(1)} %collective-permute-done.4.tail_ref.counts_other_ref.cother_ref, ...), custom_call_target="tpu_custom_call" | custom-call | flops 1048576 | bytes 4194304 | tf_op jit(solution)/shard_map/shrink/pallas_call | solution.py:429
  (10 shorter events, 0.1 us)
Async XLA Ops:
  0.0 0.7 %copy-start = (s32[2048]{0:T(1024)S(1)}, s32[2048]{0:T(1024)}, u32[]{:S(2)}) copy-start(s32[2048]{0:T(1024)} %param.3) | copy-start | bytes 24580
  3.4 3.1 %collective-permute-start = (f32[264,256]{1,0:T(8,128)S(1)}, f32[264,256]{1,0:T(8,128)S(1)}, u32[]{:S(2)}, u32[]{:S(2)}) collective-permute-start(f32[264,256]{1,0:T(8,128)S(1)} %get-tuple-element.24), channel_id=1, source_target_pairs={{0,1},{1,0},{2,3},{3,2},{4,5},{5,4},{6,7},{7,6},{8,9},{9,8},{10,11... | collective-permute-start | bytes 811016 | tf_op jit(solution)/shard_map/ppermute | solution.py:447
  4.0 20.6 %collective-permute-start.7 = (f32[64,2048]{1,0:T(8,128)S(1)}, f32[64,2048]{1,0:T(8,128)S(1)}, u32[]{:S(2)}, u32[]{:S(2)}) collective-permute-start(f32[64,2048]{1,0:T(8,128)S(1)} %get-tuple-element.25), channel_id=1, source_target_pairs={{0,4},{4,8},{8,12},{12,16},{16,20},{20,24},{24,28},{28,0},{1,5},{5... | collective-permute-start | bytes 1572872 | tf_op jit(solution)/shard_map/ppermute | solution.py:452
  6.6 10.6 %collective-permute-start.3 = (f32[72,256]{1,0:T(8,128)S(1)}, f32[72,256]{1,0:T(8,128)S(1)}, u32[]{:S(2)}, u32[]{:S(2)}) collective-permute-start(f32[72,256]{1,0:T(8,128)S(1)} %slice_add_fusion.1), channel_id=1, source_target_pairs={{0,2},{1,3},{2,0},{3,1},{4,6},{5,7},{6,4},{7,5},{8,10},{9,11},{10,... | collective-permute-start | bytes 221192 | tf_op jit(solution)/shard_map/ppermute | solution.py:447
  8.1 6.3 %collective-permute-start.1 = (f32[128,256]{1,0:T(8,128)S(1)}, f32[128,256]{1,0:T(8,128)S(1)}, u32[]{:S(2)}, u32[]{:S(2)}) collective-permute-start(f32[128,256]{1,0:T(8,128)S(1)} %slice_add_fusion), channel_id=1, source_target_pairs={{0,2},{1,3},{2,0},{3,1},{4,6},{5,7},{6,4},{7,5},{8,10},{9,11},{10,... | collective-permute-start | bytes 393224 | tf_op jit(solution)/shard_map/ppermute | solution.py:447
  8.8 7.9 %collective-permute-start.8 = (f32[64,256]{1,0:T(8,128)S(1)}, f32[64,256]{1,0:T(8,128)S(1)}, u32[]{:S(2)}, u32[]{:S(2)}) collective-permute-start(f32[64,256]{1,0:T(8,128)S(1)} %slice_add_fusion.2), channel_id=1, source_target_pairs={{0,2},{1,3},{2,0},{3,1},{4,6},{5,7},{6,4},{7,5},{8,10},{9,11},{10,... | collective-permute-start | bytes 196616 | tf_op jit(solution)/shard_map/ppermute | solution.py:447
  14.5 11.2 %collective-permute-start.2 = (f32[128,256]{1,0:T(8,128)S(1)}, f32[128,256]{1,0:T(8,128)S(1)}, u32[]{:S(2)}, u32[]{:S(2)}) collective-permute-start(f32[128,256]{1,0:T(8,128)S(1)} %add.24.early_ref.own_ref), channel_id=1, source_target_pairs={{0,1},{1,0},{2,3},{3,2},{4,5},{5,4},{6,7},{7,6},{8,9},{9,8},{10,11... | collective-permute-start | bytes 393224 | tf_op jit(solution)/shard_map/ppermute | solution.py:447
  16.6 9.0 %collective-permute-start.9 = (f32[64,256]{1,0:T(8,128)S(1)}, f32[64,256]{1,0:T(8,128)S(1)}, u32[]{:S(2)}, u32[]{:S(2)}) collective-permute-start(f32[64,256]{1,0:T(8,128)S(1)} %add.28.late_ref), channel_id=1, source_target_pairs={{0,1},{1,0},{2,3},{3,2},{4,5},{5,4},{6,7},{7,6},{8,9},{9,8},{10,11... | collective-permute-start | bytes 196616 | tf_op jit(solution)/shard_map/ppermute | solution.py:447
  17.2 8.4 %collective-permute-start.4 = (f32[72,256]{1,0:T(8,128)S(1)}, f32[72,256]{1,0:T(8,128)S(1)}, u32[]{:S(2)}, u32[]{:S(2)}) collective-permute-start(f32[72,256]{1,0:T(8,128)S(1)} %add.26.tail_ref.counts_own_ref.cown_ref), channel_id=1, source_target_pairs={{0,1},{1,0},{2,3},{3,2},{4,5},{5,4},{6,7},{7,6},{8,9},{9,8},{10,11... | collective-permute-start | bytes 221192 | tf_op jit(solution)/shard_map/ppermute | solution.py:447
  17.3 7.3 %collective-permute-start.5 = (f32[64,256]{1,0:T(8,128)S(1)}, f32[64,256]{1,0:T(8,128)S(1)}, u32[]{:S(2)}, u32[]{:S(2)}) collective-permute-start(f32[64,256]{1,0:T(8,128)S(1)} %slice.30), channel_id=1, source_target_pairs={{0,4},{4,8},{8,12},{12,16},{16,20},{20,24},{24,28},{28,0},{1,5},{5... | collective-permute-start | bytes 196616 | tf_op jit(solution)/shard_map/ppermute | solution.py:452
  24.6 3.8 %collective-permute-start.6 = (f32[64,256]{1,0:T(8,128)S(1)}, f32[64,256]{1,0:T(8,128)S(1)}, u32[]{:S(2)}, u32[]{:S(2)}) collective-permute-start(f32[64,256]{1,0:T(8,128)S(1)} %collective-permute-done.5.prior_own_ref), channel_id=1, source_target_pairs={{0,1},{1,0},{2,3},{3,2},{4,5},{5,4},{6,7},{7,6},{8,9},{9,8},{10,11... | collective-permute-start | bytes 196616 | tf_op jit(solution)/shard_map/ppermute | solution.py:447

commit v8 on v6

--- a/solution.py
+++ b/solution.py
@@ -91,18 +91,29 @@
     tail_copy.wait()
 
 
+SHIFTED = (1, 2, 4)
+
+
 class Window:
-    def __init__(self):
+    def __init__(self, ref, row):
+        self.ref, self.row, self.groups = ref, row, 0
         self.rolled = {}
         self.sums = {8: [], 16: [], 32: []}
 
-    def push(self, x, row):
+    def push(self, x):
+        here = 8 + 8 * self.groups
+        self.groups += 1
         size = 1
         while size < 8:
-            turned = pltpu.roll(x, size, 0)
-            before = self.rolled.get(size, turned)
-            self.rolled[size] = turned
-            x = x + jnp.where(row < size, before, turned)
+            if size in SHIFTED:
+                slot = SHIFTED.index(size)
+                self.ref[slot, here : here + 8] = x
+                x = x + self.ref[slot, here - size : here - size + 8]
+            else:
+                turned = pltpu.roll(x, size, 0)
+                before = self.rolled.get(size, turned)
+                self.rolled[size] = turned
+                x = x + jnp.where(self.row < size, before, turned)
             size *= 2
         while size < W:
             seen = self.sums[size]
@@ -115,6 +126,10 @@
         return x
 
 
+def stage(count, rows):
+    return pltpu.VMEM((count, len(SHIFTED), rows + 8, LANES), f32)
+
+
 def tile_at(index):
     return pl.ds(pl.multiple_of(index * LANES, LANES), LANES)
 
@@ -123,15 +138,15 @@
     return slice(group * 8, group * 8 + 8)
 
 
-def moments_body(load, inv, groups, total_ref, crr_ref):
+def moments_body(load, inv, groups, total_ref, crr_ref, stage_ref):
     row = lax.broadcasted_iota(jnp.int32, (8, LANES), 0)
 
     def tile(index, _):
         cols = tile_at(index)
-        first, second = Window(), Window()
+        first, second = Window(stage_ref.at[0], row), Window(stage_ref.at[1], row)
         for group in range(groups):
             ret = load(group, cols)
-            total, squares = first.push(ret, row), second.push(ret * ret, row)
+            total, squares = first.push(ret), second.push(ret * ret)
             if group >= W // 8:
                 here = rows_of(group - W // 8)
                 scale = inv(group - W // 8)
@@ -143,17 +158,18 @@
     lax.fori_loop(0, total_ref.shape[1] // LANES, tile, 0)
 
 
-def moments_main_kernel(ret_ref, mean_ref, crr_ref):
+def moments_main_kernel(ret_ref, mean_ref, crr_ref, stage_ref):
     moments_body(
         lambda group, cols: ret_ref[rows_of(group), cols],
         lambda group: 1.0 / W,
         ret_ref.shape[0] // 8,
         mean_ref,
         crr_ref,
-    )
-
-
-def moments_head_kernel(inv_ref, halo_ref, ret_ref, mean_ref, crr_ref):
+        stage_ref,
+    )
+
+
+def moments_head_kernel(inv_ref, halo_ref, ret_ref, mean_ref, crr_ref, stage_ref):
     blocks = W // 8
     moments_body(
         lambda group, cols: halo_ref[rows_of(group), cols] * inv_ref[W:]
@@ -163,16 +179,18 @@
         2 * blocks,
         mean_ref,
         crr_ref,
-    )
-
-
-def sector_rows(means, inv, groups, starts, left_ref, out, low, kept=None):
+        stage_ref,
+    )
+
+
+def sector_rows(means, inv, groups, starts, left_ref, stage_ref, out, low, kept=None):
     row = lax.broadcasted_iota(jnp.int32, (8, LANES), 0)
-    first, second = Window(), Window()
+    spot = 2 * (out // LANES) % stage_ref.shape[0]
+    first, second = Window(stage_ref.at[spot], row), Window(stage_ref.at[spot + 1], row)
     mean_parts, gain_parts = [], []
     for group in range(groups):
         mean = means[group]
-        total, squares = first.push(mean, row), second.push(mean * mean, row)
+        total, squares = first.push(mean), second.push(mean * mean)
         if group >= W // 8:
             scale = inv(group - W // 8)
             mean_f = total * scale
@@ -208,7 +226,7 @@
     return pl.ds(pl.multiple_of(index * wide, wide), wide)
 
 
-def main_rows(sums_ref, tail_ref, left_ref):
+def main_rows(sums_ref, tail_ref, left_ref, stage_ref):
     main = sums_ref.shape[0]
     rows = main + W
     for tile in range(HALF // LANES):
@@ -220,7 +238,8 @@
             for g in range(rows // 8)
         ]
         sector_rows(
-            means, lambda g: 1.0 / W, rows // 8, (0, rows, rows + main), left_ref, tile * LANES, HALF
+            means, lambda g: 1.0 / W, rows // 8, (0, rows, rows + main), left_ref, stage_ref,
+            tile * LANES, HALF
         )
 
 
@@ -228,8 +247,8 @@
     return jnp.concatenate([table, table], axis=0)
 
 
-def own_kernel(own_ref, own_tail_ref, table_ref, spread_ref, left_ref):
-    main_rows(own_ref, own_tail_ref, left_ref)
+def own_kernel(own_ref, own_tail_ref, table_ref, spread_ref, left_ref, stage_ref):
+    main_rows(own_ref, own_tail_ref, left_ref, stage_ref)
     wide = 4 * LANES
     for index in range(table_ref.shape[1] // wide):
         cols = slice(index * wide, (index + 1) * wide)
@@ -238,12 +257,12 @@
 
 def main_kernel(
     other_ref, other_tail_ref, spread_ref, ret_ref, total_ref, crr_ref, table_ref,
-    var_ref, factor_ref, colsum_ref, left_ref, even_ref, odd_ref,
+    var_ref, factor_ref, colsum_ref, left_ref, even_ref, odd_ref, stage_ref,
 ):
     rows = ret_ref.shape[0]
     main = rows - W
     blocks = W // 8
-    main_rows(other_ref, other_tail_ref, left_ref)
+    main_rows(other_ref, other_tail_ref, left_ref, stage_ref)
     row = lax.broadcasted_iota(jnp.int32, (8, LANES), 0)
     wide = even_ref.shape[1]
 
@@ -255,13 +274,13 @@
         for tile in range(wide // LANES):
             inner = slice(tile * LANES, (tile + 1) * LANES)
             cols = pl.ds(pl.multiple_of(index * wide + tile * LANES, LANES), LANES)
-            cross = Window()
+            cross = Window(stage_ref.at[tile], row)
             total = jnp.zeros((8, LANES), f32)
             for group in range(rows // 8):
                 factor = spread_ref[rows_of(group), inner]
                 if group < blocks:
                     factor_ref[rows_of(group), cols] = factor
-                product = cross.push(ret_ref[rows_of(group), cols] * factor, row)
+                product = cross.push(ret_ref[rows_of(group), cols] * factor)
                 if group >= blocks:
                     g = group - blocks
                     mean_f = spread_ref[rows_of(rows // 8 + g), inner]
@@ -278,7 +297,7 @@
 def head_kernel(
     inv_ref, flip_ref, own_ref, other_ref, counts_own_ref, counts_other_ref, prior_own_ref, prior_other_ref,
     halo_ref, ret_ref, factor_ref, total_ref, crr_ref, colsum_ref, table_ref,
-    var_ref, totals_ref, left_ref, even_ref, odd_ref, acc_ref,
+    var_ref, totals_ref, left_ref, even_ref, odd_ref, acc_ref, stage_ref,
 ):
     blocks = W // 8
     acc_ref[...] = jnp.zeros_like(acc_ref)
@@ -298,7 +317,7 @@
         ]
         sector_rows(
             means, lambda g: inv_ref[rows_of(g)], 2 * blocks, (0, W, 2 * W), left_ref,
-            tile * LANES, SECTORS, blocks,
+            stage_ref, tile * LANES, SECTORS, blocks,
         )
     row = lax.broadcasted_iota(jnp.int32, (8, LANES), 0)
     wide = even_ref.shape[1]
@@ -312,7 +331,7 @@
         for tile in range(wide // LANES):
             inner = slice(tile * LANES, (tile + 1) * LANES)
             cols = pl.ds(pl.multiple_of(index * wide + tile * LANES, LANES), LANES)
-            cross = Window()
+            cross = Window(stage_ref.at[tile], row)
             total = colsum_ref[:, cols]
             for group in range(2 * blocks):
                 g = group - blocks
@@ -321,7 +340,7 @@
                     product = product * inv_ref[W:]
                 else:
                     product = ret_ref[rows_of(g), cols] * factor_ref[rows_of(g), cols]
-                product = cross.push(product, row)
+                product = cross.push(product)
                 if g >= 0:
                     mean_f = spread_ref[rows_of(blocks + g), inner]
                     gain = spread_ref[rows_of(2 * blocks + g), inner]
@@ -473,22 +492,22 @@
     chunk = 4 * LANES
     lhs = 3 * rows - 2 * W
     mean, crr = kernel_call(
-        moments_main_kernel, [(main, width)] * 2, [returns],
+        moments_main_kernel, [(main, width)] * 2, [returns], scratch=[stage(2, rows)],
         flops=40 * main * width, moved=12 * main * width,
     )
     mean_head, crr_head = kernel_call(
-        moments_head_kernel, [(W, width)] * 2, [inv, halo, returns],
+        moments_head_kernel, [(W, width)] * 2, [inv, halo, returns], scratch=[stage(2, 2 * W)],
         flops=40 * W * width, moved=12 * W * width,
     )
     left = [pltpu.VMEM((lhs, SECTORS), bf16)]
     (spread,) = kernel_call(
-        own_kernel, [(lhs, width)], [own, own_tail, table], scratch=left,
+        own_kernel, [(lhs, width)], [own, own_tail, table], scratch=left + [stage(4, rows)],
         flops=2 * lhs * width * SECTORS, moved=4 * lhs * width,
     )
     var, factor, colsum = kernel_call(
         main_kernel, [(main, width), (W, width), (8, width)],
         [other, other_tail, spread, returns, mean, crr, table],
-        scratch=left + [pltpu.VMEM((lhs, chunk), f32)] * 2,
+        scratch=left + [pltpu.VMEM((lhs, chunk), f32)] * 2 + [stage(4, rows)],
         flops=4 * lhs * width * SECTORS, moved=12 * rows * width,
     )
     var_head, totals = kernel_call(
@@ -497,7 +516,7 @@
          mean_head, crr_head, colsum, table],
         scratch=[pltpu.VMEM((3 * W, 2 * SECTORS), bf16)]
         + [pltpu.VMEM((3 * W, chunk), f32)] * 2
-        + [pltpu.VMEM((32, SECTORS), f32)],
+        + [pltpu.VMEM((32, SECTORS), f32), stage(8, 2 * W)],
         flops=16 * W * width * SECTORS, moved=12 * W * width,
     )
     parts = lax.all_to_all(totals, ("tm", "series"), 0, 0)

time: 43.7 us -> 43.3 us (level)
  Pallas kernels: 14.2 us -> 13.6 us
    pallas_call x5, Pallas kernels: 9.93 us -> 9.3 us  [kernel_of(): pl.pallas_call(body, out_shape=tuple((o if hasattr(o, 'dtype') else jax.S...]
  transfers between devices with their start and end apart: 8 -> 8, of which waited for: 3 -> 3; matrix products, arithmetic and copies ran while one was open for 0% -> 0% of each run, Pallas kernels for 18% -> 17%
where the time goes in v8:
time: 43.3 us; the launch traced here: 43.1 us
  Pallas kernels  13.6 us (31%)
  waiting for transfers between devices  11.1 us (26%)
  blocking collectives  10.4 us (24%)
  starting transfers between devices  6.99 us (16%)
  local copies, waits for them, and re-layouts  0.78 us (2%)
    all_to_all x1, blocking collectives, step(): parts = lax.all_to_all(totals, ('tm', 'series'), 0, 0)  10.4 us
    pallas_call x5, Pallas kernels, kernel_of(): pl.pallas_call(body, out_shape=tuple((o if hasattr(o, 'dtype') else jax.S...  9.3 us
    ppermute x6, waiting for transfers between devices, swap(): lax.ppermute(value, axis, [(i, i ^ bit) for i in range(lax.axis_size(axis...  6.35 us
    ppermute x2, waiting for transfers between devices, ahead(): lax.ppermute(value, axis, [(i, (i + 1) % count) for i in range(count)])  4.78 us
    ppermute x2, starting transfers between devices, ahead(): lax.ppermute(value, axis, [(i, (i + 1) % count) for i in range(count)])  4.14 us
    ppermute x6, starting transfers between devices, swap(): lax.ppermute(value, axis, [(i, i ^ bit) for i in range(lax.axis_size(axis...  2.85 us
    pallas_call x1, Pallas kernels, step(): pl.pallas_call(load_kernel, out_shape=(jax.ShapeDtypeStruct((rows + 8, HA...  2.72 us
    pallas_call x1, Pallas kernels, shrink(): pl.pallas_call(functools.partial(shrink_kernel, float(all_steps)), out_sh...  1.59 us
  transfers between devices with their start and end apart: 8, of which 3 were waited for; matrix products, arithmetic and copies ran while one was open for 0% of the time, Pallas kernels for 17%

profile of v8, /device:TPU:0, one launch (start us, length us, event | category | flops | bytes accessed | tf_op | source)
XLA Modules:
  0.0 43.1 jit_solution(2230985911155939149)
XLA Ops:
  0.0 0.0 copy-start
  0.0 0.7 %copy-done = s32[2048]{0:T(1024)S(1)} copy-done((s32[2048]{0:T(1024)S(1)}, s32[2048]{0:T(1024)}, u32[]{:S(2)}) %copy-start) | copy-done | bytes 8216
  0.7 2.7 %load.1 = (f32[264,256]{1,0:T(8,128)S(1)}, f32[264,256]{1,0:T(8,128)S(1)}, bf16[512,2048]{1,0:T(8,128)(2,1)S(1)}, f32[256,2048]{1,0:T(8,128)S(1)}, f32[64,2048]{...) custom-call(f32[256,2048]{1,0:T(8,128)} %ret_hbm.1, s32[1,2048]{1,0:T(1,128)S(1)} %bitcast.7, ...), custom_call_target="tpu_custom_call" | custom-call | tf_op jit(solution)/shard_map/load/pallas_call | solution.py:455
  3.4 0.6 %collective-permute-start = (f32[264,256]{1,0:T(8,128)S(1)}, f32[264,256]{1,0:T(8,128)S(1)}, u32[]{:S(2)}, u32[]{:S(2)}) collective-permute-start(f32[264,256]{1,0:T(8,128)S(1)} %get-tuple-element.24), channel_id=1, source_target_pairs={{0,1},{1,0},{2,3},{3,2},{4,5},{5,4},{6,7},{7,6},{8,9},{9,8},{10,11... | collective-permute-start | bytes 811016 | tf_op jit(solution)/shard_map/ppermute | solution.py:431
  4.0 2.6 %collective-permute-start.7 = (f32[64,2048]{1,0:T(8,128)S(1)}, f32[64,2048]{1,0:T(8,128)S(1)}, u32[]{:S(2)}, u32[]{:S(2)}) collective-permute-start(f32[64,2048]{1,0:T(8,128)S(1)} %get-tuple-element.25), channel_id=1, source_target_pairs={{0,4},{4,8},{8,12},{12,16},{16,20},{20,24},{24,28},{28,0},{1,5},{5... | collective-permute-start | bytes 1572872 | tf_op jit(solution)/shard_map/ppermute | solution.py:436
  6.5 0.0 collective-permute-done
  6.6 1.6 %collective-permute-start.1 = (f32[192,256]{1,0:T(8,128)S(1)}, f32[192,256]{1,0:T(8,128)S(1)}, u32[]{:S(2)}, u32[]{:S(2)}) collective-permute-start(f32[192,256]{1,0:T(8,128)S(1)} %slice_add_fusion), channel_id=1, source_target_pairs={{0,2},{1,3},{2,0},{3,1},{4,6},{5,7},{6,4},{7,5},{8,10},{9,11},{10,... | collective-permute-start | bytes 589832 | tf_op jit(solution)/shard_map/ppermute | solution.py:431
  8.2 0.6 %collective-permute-start.3 = (f32[72,256]{1,0:T(8,128)S(1)}, f32[72,256]{1,0:T(8,128)S(1)}, u32[]{:S(2)}, u32[]{:S(2)}) collective-permute-start(f32[72,256]{1,0:T(8,128)S(1)} %slice_add_fusion.1), channel_id=1, source_target_pairs={{0,2},{1,3},{2,0},{3,1},{4,6},{5,7},{6,4},{7,5},{8,10},{9,11},{10,... | collective-permute-start | bytes 221192 | tf_op jit(solution)/shard_map/ppermute | solution.py:431
  8.7 5.7 %collective-permute-done.1 = f32[192,256]{1,0:T(8,128)S(1)} collective-permute-done((f32[192,256]{1,0:T(8,128)S(1)}, f32[192,256]{1,0:T(8,128)S(1)}, u32[]{:S(2)}, u32[]{:S(2)}) %collective-permute-start.1) | collective-permute-done | bytes 196640 | tf_op jit(solution)/shard_map/ppermute | solution.py:431
  14.4 0.1 collective-permute-start.2
  14.5 0.7 %collective-permute-done.3 = f32[72,256]{1,0:T(8,128)S(1)} collective-permute-done((f32[72,256]{1,0:T(8,128)S(1)}, f32[72,256]{1,0:T(8,128)S(1)}, u32[]{:S(2)}, u32[]{:S(2)}) %collective-permute-start.3) | collective-permute-done | bytes 73760 | tf_op jit(solution)/shard_map/ppermute | solution.py:431
  15.2 1.6 %collective-permute-start.5 = (f32[64,256]{1,0:T(8,128)S(1)}, f32[64,256]{1,0:T(8,128)S(1)}, u32[]{:S(2)}, u32[]{:S(2)}) collective-permute-start(f32[64,256]{1,0:T(8,128)S(1)} %slice.22), channel_id=1, source_target_pairs={{0,4},{4,8},{8,12},{12,16},{16,20},{20,24},{24,28},{28,0},{1,5},{5... | collective-permute-start | bytes 196616 | tf_op jit(solution)/shard_map/ppermute | solution.py:436
  16.8 1.9 %shard_map.29 = (f32[192,2048]{1,0:T(8,128)S(1)}, f32[192,2048]{1,0:T(8,128)S(1)}) custom-call(f32[256,2048]{1,0:T(8,128)S(1)} %get-tuple-element.26.ret_ref), custom_call_target="tpu_custom_call" | custom-call | flops 15728640 | bytes 4718592 | tf_op jit(solution)/shard_map/pallas_call | solution.py:375
  18.7 0.1 collective-permute-start.4
  18.7 4.8 %collective-permute-done.5.prior_own_ref = f32[64,256]{1,0:T(8,128)S(1)} collective-permute-done((f32[64,256]{1,0:T(8,128)S(1)}, f32[64,256]{1,0:T(8,128)S(1)}, u32[]{:S(2)}, u32[]{:S(2)}) %collective-permute-start.5) | collective-permute-done | bytes 65568 | tf_op jit(solution)/shard_map/ppermute | solution.py:436
  23.5 0.0 collective-permute-start.6
  23.5 1.6 %shard_map.28.spread_ref = f32[640,2048]{1,0:T(8,128)S(1)} custom-call(f32[192,256]{1,0:T(8,128)S(1)} %add.18.own_ref, f32[72,256]{1,0:T(8,128)S(1)} %add.20.own_tail_ref.counts_own_ref.cown_ref, bf16[512,2048]{1,0:T(8,128)(2,1)S(1)} %get-tuple-element.27.table_ref), custom_call_target="tpu_custom_call" | custom-call | flops 1342177280 | bytes 5242880 | tf_op jit(solution)/shard_map/pallas_call | solution.py:375
  25.2 0.0 collective-permute-done.7.halo_ref
  25.2 1.0 %shard_map.31 = (f32[64,2048]{1,0:T(8,128)S(1)}, f32[64,2048]{1,0:T(8,128)S(1)}) custom-call(f32[72,128]{1,0:T(8,128)S(1)} %get-tuple-element.22.inv_ref, f32[64,2048]{1,0:T(8,128)S(1)} %collective-permute-done.7.halo_ref, f32[256,2048]{1,0:T(8,128)S(1)} %get-tuple-element.26.ret_ref), custom_call_target="tpu_custom_call" | custom-call | flops 5242880 | bytes 1572864 | tf_op jit(solution)/shard_map/pallas_call | solution.py:375
  26.2 0.0 collective-permute-done.4.other_tail_ref.counts_other_ref.cother_ref
  26.2 0.0 collective-permute-done.2.other_ref
  26.2 2.6 %shard_map.30 = (f32[192,2048]{1,0:T(8,128)S(1)}, f32[64,2048]{1,0:T(8,128)S(1)}, f32[8,2048]{1,0:T(8,128)S(1)}) custom-call(f32[192,256]{1,0:T(8,128)S(1)} %collective-permute-done.2.other_ref, f32[72,256]{1,0:T(8,128)S(1)} %collective-permute-done.4.other_tail_ref.counts_other_ref.cother_ref, f32[640,2048]{1,0:T(8,128)S(1)} %shard_map.28.spread_ref, ...), custom_call_target="tpu_custom_call" | custom-call | flops 2684354560 | bytes 6291456 | tf_op jit(solution)/shard_map/pallas_call | solution.py:375
  28.9 0.0 collective-permute-done.6.prior_other_ref
  28.9 2.1 %shard_map.32 = (f32[64,2048]{1,0:T(8,128)S(1)}, f32[32,512]{1,0:T(8,128)S(1)}) custom-call(f32[72,128]{1,0:T(8,128)S(1)} %get-tuple-element.22.inv_ref, s32[8,512]{1,0:T(8,128)S(1)} %get-tuple-element.21.flip_ref, f32[192,256]{1,0:T(8,128)S(1)} %add.18.own_ref, f32[192,256]{1,0:T(8,128)S(1)} %collective-permute-done.2.other_ref, ...), custom_call_target="tpu_custom_call" | custom-call | flops 1073741824 | bytes 1572864 | tf_op jit(solution)/shard_map/pallas_call | solution.py:375
  31.0 0.1 copy.3
  31.1 10.4 %all_to_all.11 = f32[32,1,512]{2,1,0:T(1,128)S(1)} all-to-all(f32[32,1,512]{2,1,0:T(1,128)S(1)} %copy.3), channel_id=1, replica_groups=mesh['tm'=8,'series'=4] {'tm','series'}, dimensions={0} | all-to-all | bytes 131072 | tf_op jit(solution)/shard_map/all_to_all | solution.py:522
  41.5 1.6 %shrink.1 = f32[256,2048]{1,0:T(8,128)} custom-call(s32[8,512]{1,0:T(8,128)S(1)} %get-tuple-element.21.flip_ref, f32[32,512]{1,0:T(8,128)S(1)} %bitcast.5, f32[72,256]{1,0:T(8,128)S(1)} %add.20.own_tail_ref.counts_own_ref.cown_ref, f32[72,256]{1,0:T(8,128)S(1)} %collective-permute-done.4.other_tail_ref.counts_other_ref.cother_ref, ...), custom_call_target="tpu_custom_call" | custom-call | flops 1048576 | bytes 4194304 | tf_op jit(solution)/shard_map/shrink/pallas_call | solution.py:413
  (8 shorter events, 0.1 us)
Async XLA Ops:
  0.0 0.7 %copy-start = (s32[2048]{0:T(1024)S(1)}, s32[2048]{0:T(1024)}, u32[]{:S(2)}) copy-start(s32[2048]{0:T(1024)} %param.3) | copy-start | bytes 24580
  3.4 3.1 %collective-permute-start = (f32[264,256]{1,0:T(8,128)S(1)}, f32[264,256]{1,0:T(8,128)S(1)}, u32[]{:S(2)}, u32[]{:S(2)}) collective-permute-start(f32[264,256]{1,0:T(8,128)S(1)} %get-tuple-element.24), channel_id=1, source_target_pairs={{0,1},{1,0},{2,3},{3,2},{4,5},{5,4},{6,7},{7,6},{8,9},{9,8},{10,11... | collective-permute-start | bytes 811016 | tf_op jit(solution)/shard_map/ppermute | solution.py:431
  4.0 21.2 %collective-permute-start.7 = (f32[64,2048]{1,0:T(8,128)S(1)}, f32[64,2048]{1,0:T(8,128)S(1)}, u32[]{:S(2)}, u32[]{:S(2)}) collective-permute-start(f32[64,2048]{1,0:T(8,128)S(1)} %get-tuple-element.25), channel_id=1, source_target_pairs={{0,4},{4,8},{8,12},{12,16},{16,20},{20,24},{24,28},{28,0},{1,5},{5... | collective-permute-start | bytes 1572872 | tf_op jit(solution)/shard_map/ppermute | solution.py:436
  6.6 7.8 %collective-permute-start.1 = (f32[192,256]{1,0:T(8,128)S(1)}, f32[192,256]{1,0:T(8,128)S(1)}, u32[]{:S(2)}, u32[]{:S(2)}) collective-permute-start(f32[192,256]{1,0:T(8,128)S(1)} %slice_add_fusion), channel_id=1, source_target_pairs={{0,2},{1,3},{2,0},{3,1},{4,6},{5,7},{6,4},{7,5},{8,10},{9,11},{10,... | collective-permute-start | bytes 589832 | tf_op jit(solution)/shard_map/ppermute | solution.py:431
  8.2 7.0 %collective-permute-start.3 = (f32[72,256]{1,0:T(8,128)S(1)}, f32[72,256]{1,0:T(8,128)S(1)}, u32[]{:S(2)}, u32[]{:S(2)}) collective-permute-start(f32[72,256]{1,0:T(8,128)S(1)} %slice_add_fusion.1), channel_id=1, source_target_pairs={{0,2},{1,3},{2,0},{3,1},{4,6},{5,7},{6,4},{7,5},{8,10},{9,11},{10,... | collective-permute-start | bytes 221192 | tf_op jit(solution)/shard_map/ppermute | solution.py:431
  14.4 11.8 %collective-permute-start.2 = (f32[192,256]{1,0:T(8,128)S(1)}, f32[192,256]{1,0:T(8,128)S(1)}, u32[]{:S(2)}, u32[]{:S(2)}) collective-permute-start(f32[192,256]{1,0:T(8,128)S(1)} %add.18.own_ref), channel_id=1, source_target_pairs={{0,1},{1,0},{2,3},{3,2},{4,5},{5,4},{6,7},{7,6},{8,9},{9,8},{10,11... | collective-permute-start | bytes 589832 | tf_op jit(solution)/shard_map/ppermute | solution.py:431
  15.2 8.3 %collective-permute-start.5 = (f32[64,256]{1,0:T(8,128)S(1)}, f32[64,256]{1,0:T(8,128)S(1)}, u32[]{:S(2)}, u32[]{:S(2)}) collective-permute-start(f32[64,256]{1,0:T(8,128)S(1)} %slice.22), channel_id=1, source_target_pairs={{0,4},{4,8},{8,12},{12,16},{16,20},{20,24},{24,28},{28,0},{1,5},{5... | collective-permute-start | bytes 196616 | tf_op jit(solution)/shard_map/ppermute | solution.py:436
  18.7 7.6 %collective-permute-start.4 = (f32[72,256]{1,0:T(8,128)S(1)}, f32[72,256]{1,0:T(8,128)S(1)}, u32[]{:S(2)}, u32[]{:S(2)}) collective-permute-start(f32[72,256]{1,0:T(8,128)S(1)} %add.20.own_tail_ref.counts_own_ref.cown_ref), channel_id=1, source_target_pairs={{0,1},{1,0},{2,3},{3,2},{4,5},{5,4},{6,7},{7,6},{8,9},{9,8},{10,11... | collective-permute-start | bytes 221192 | tf_op jit(solution)/shard_map/ppermute | solution.py:431
  23.5 5.4 %collective-permute-start.6 = (f32[64,256]{1,0:T(8,128)S(1)}, f32[64,256]{1,0:T(8,128)S(1)}, u32[]{:S(2)}, u32[]{:S(2)}) collective-permute-start(f32[64,256]{1,0:T(8,128)S(1)} %collective-permute-done.5.prior_own_ref), channel_id=1, source_target_pairs={{0,1},{1,0},{2,3},{3,2},{4,5},{5,4},{6,7},{7,6},{8,9},{9,8},{10,11... | collective-permute-start | bytes 196616 | tf_op jit(solution)/shard_map/ppermute | solution.py:431

commit v9 on v8

--- a/solution.py
+++ b/solution.py
@@ -294,37 +294,46 @@
     pipelined(fill, work, (even_ref, odd_ref), ret_ref.shape[1] // wide)
 
 
+def head_rows(here_ref, prior_ref, counts_ref, inv_ref, left_ref, stage_ref):
+    blocks = W // 8
+    for tile in range(HALF // LANES):
+        cols = slice(tile * LANES, (tile + 1) * LANES)
+        scale = 1.0 / jnp.maximum(counts_ref[W : W + 8, cols], 1.0)
+        means = [
+            (prior_ref[rows_of(g), cols] * inv_ref[W:] if g < blocks else here_ref[rows_of(g - blocks), cols])
+            * scale
+            for g in range(2 * blocks)
+        ]
+        sector_rows(
+            means, lambda g: inv_ref[rows_of(g)], 2 * blocks, (0, W, 2 * W), left_ref,
+            stage_ref, tile * LANES, HALF, blocks,
+        )
+
+
+def head_own_kernel(
+    inv_ref, here_ref, prior_ref, counts_ref, table_ref, spread_ref, left_ref, stage_ref
+):
+    head_rows(here_ref, prior_ref, counts_ref, inv_ref, left_ref, stage_ref)
+    wide = 4 * LANES
+    for index in range(table_ref.shape[1] // wide):
+        cols = slice(index * wide, (index + 1) * wide)
+        spread_ref[:, cols] = dot_nn(left_ref[...], twice(table_ref[:HALF, cols]))
+
+
 def head_kernel(
-    inv_ref, flip_ref, own_ref, other_ref, counts_own_ref, counts_other_ref, prior_own_ref, prior_other_ref,
+    inv_ref, flip_ref, here_ref, prior_ref, counts_ref, spread_ref,
     halo_ref, ret_ref, factor_ref, total_ref, crr_ref, colsum_ref, table_ref,
     var_ref, totals_ref, left_ref, even_ref, odd_ref, acc_ref, stage_ref,
 ):
     blocks = W // 8
     acc_ref[...] = jnp.zeros_like(acc_ref)
-    for tile in range(SECTORS // LANES):
-        mine = tile < HALF // LANES
-        here, prior, counts = (
-            (own_ref, prior_own_ref, counts_own_ref)
-            if mine
-            else (other_ref, prior_other_ref, counts_other_ref)
-        )
-        cols = pl.ds((tile * LANES) % HALF, LANES)
-        scale = 1.0 / jnp.maximum(counts[W : W + 8, cols], 1.0)
-        means = [
-            (prior[rows_of(g), cols] * inv_ref[W:] if g < blocks else here[rows_of(g - blocks), cols])
-            * scale
-            for g in range(2 * blocks)
-        ]
-        sector_rows(
-            means, lambda g: inv_ref[rows_of(g)], 2 * blocks, (0, W, 2 * W), left_ref,
-            stage_ref, tile * LANES, SECTORS, blocks,
-        )
+    head_rows(here_ref, prior_ref, counts_ref, inv_ref, left_ref, stage_ref)
     row = lax.broadcasted_iota(jnp.int32, (8, LANES), 0)
     wide = even_ref.shape[1]
 
     def fill(buffer, index):
         cols = chunk_at(index, wide)
-        buffer[...] = dot_nn(left_ref[...], twice(table_ref[:, cols]))
+        buffer[...] = spread_ref[:, cols] + dot_nn(left_ref[...], twice(table_ref[HALF:, cols]))
 
     def work(spread_ref, index):
         parts = []
@@ -409,7 +418,7 @@
 def shrink(all_steps, flip, parts, own, other, table, head, main):
     width = head.shape[1]
     rows = head.shape[0] + main.shape[0]
-    chunks = 4
+    chunks = 8
     return pl.pallas_call(
         functools.partial(shrink_kernel, float(all_steps)),
         out_shape=jax.ShapeDtypeStruct((rows, width), f32),
@@ -510,13 +519,18 @@
         scratch=left + [pltpu.VMEM((lhs, chunk), f32)] * 2 + [stage(4, rows)],
         flops=4 * lhs * width * SECTORS, moved=12 * rows * width,
     )
+    left = [pltpu.VMEM((3 * W, SECTORS), bf16)]
+    (spread_head,) = kernel_call(
+        head_own_kernel, [(3 * W, width)], [inv, own, prior_own, own_tail, table],
+        scratch=left + [stage(4, 2 * W)], flops=8 * W * width * SECTORS, moved=12 * W * width,
+    )
     var_head, totals = kernel_call(
         head_kernel, [(W, width), (n_time * n_series, SECTORS)],
-        [inv, flip, own, other, own_tail, other_tail, prior_own, prior_other, halo, returns, factor,
+        [inv, flip, other, prior_other, other_tail, spread_head, halo, returns, factor,
          mean_head, crr_head, colsum, table],
-        scratch=[pltpu.VMEM((3 * W, 2 * SECTORS), bf16)]
+        scratch=left
         + [pltpu.VMEM((3 * W, chunk), f32)] * 2
-        + [pltpu.VMEM((32, SECTORS), f32), stage(8, 2 * W)],
+        + [pltpu.VMEM((32, SECTORS), f32), stage(4, 2 * W)],
         flops=16 * W * width * SECTORS, moved=12 * W * width,
     )
     parts = lax.all_to_all(totals, ("tm", "series"), 0, 0)

time: 43.3 us -> 43.5 us (level)
  starting transfers between devices: 6.99 us -> 7.48 us
    ppermute x2, waiting for transfers between devices: 4.78 us -> 4.2 us  [ahead(): lax.ppermute(value, axis, [(i, (i + 1) % count) for i in range(count)])]
    ppermute x6, starting transfers between devices: 2.85 us -> 3.34 us  [swap(): lax.ppermute(value, axis, [(i, i ^ bit) for i in range(lax.axis_size(axis...]
    pallas_call x5 -> x6, Pallas kernels: 9.3 us -> 9.51 us  [kernel_of(): pl.pallas_call(body, out_shape=tuple((o if hasattr(o, 'dtype') else jax.S...]
  transfers between devices with their start and end apart: 8 -> 8, of which waited for: 3 -> 2; matrix products, arithmetic and copies ran while one was open for 0% -> 0% of each run, Pallas kernels for 17% -> 18%
where the time goes in v9:
time: 43.5 us; the launch traced here: 43.3 us
  Pallas kernels  13.8 us (32%)
  waiting for transfers between devices  10.7 us (25%)
  blocking collectives  10.4 us (24%)
  starting transfers between devices  7.48 us (17%)
  local copies, waits for them, and re-layouts  0.78 us (2%)
    all_to_all x1, blocking collectives, step(): parts = lax.all_to_all(totals, ('tm', 'series'), 0, 0)  10.4 us
    pallas_call x6, Pallas kernels, kernel_of(): pl.pallas_call(body, out_shape=tuple((o if hasattr(o, 'dtype') else jax.S...  9.51 us
    ppermute x6, waiting for transfers between devices, swap(): lax.ppermute(value, axis, [(i, i ^ bit) for i in range(lax.axis_size(axis...  6.46 us
    ppermute x2, waiting for transfers between devices, ahead(): lax.ppermute(value, axis, [(i, (i + 1) % count) for i in range(count)])  4.2 us
    ppermute x2, starting transfers between devices, ahead(): lax.ppermute(value, axis, [(i, (i + 1) % count) for i in range(count)])  4.14 us
    ppermute x6, starting transfers between devices, swap(): lax.ppermute(value, axis, [(i, i ^ bit) for i in range(lax.axis_size(axis...  3.34 us
    pallas_call x1, Pallas kernels, step(): pl.pallas_call(load_kernel, out_shape=(jax.ShapeDtypeStruct((rows + 8, HA...  2.72 us
    pallas_call x1, Pallas kernels, shrink(): pl.pallas_call(functools.partial(shrink_kernel, float(all_steps)), out_sh...  1.6 us
  transfers between devices with their start and end apart: 8, of which 2 were waited for; matrix products, arithmetic and copies ran while one was open for 0% of the time, Pallas kernels for 18%

profile of v9, /device:TPU:0, one launch (start us, length us, event | category | flops | bytes accessed | tf_op | source)
XLA Modules:
  0.0 43.3 jit_solution(13221493919691506089)
XLA Ops:
  0.0 0.0 copy-start
  0.0 0.7 %copy-done = s32[2048]{0:T(1024)S(1)} copy-done((s32[2048]{0:T(1024)S(1)}, s32[2048]{0:T(1024)}, u32[]{:S(2)}) %copy-start) | copy-done | bytes 8216
  0.7 2.7 %load.1 = (f32[264,256]{1,0:T(8,128)S(1)}, f32[264,256]{1,0:T(8,128)S(1)}, bf16[512,2048]{1,0:T(8,128)(2,1)S(1)}, f32[256,2048]{1,0:T(8,128)S(1)}, f32[64,2048]{...) custom-call(f32[256,2048]{1,0:T(8,128)} %ret_hbm.1, s32[1,2048]{1,0:T(1,128)S(1)} %bitcast.7, ...), custom_call_target="tpu_custom_call" | custom-call | tf_op jit(solution)/shard_map/load/pallas_call | solution.py:464
  3.4 0.6 %collective-permute-start = (f32[264,256]{1,0:T(8,128)S(1)}, f32[264,256]{1,0:T(8,128)S(1)}, u32[]{:S(2)}, u32[]{:S(2)}) collective-permute-start(f32[264,256]{1,0:T(8,128)S(1)} %get-tuple-element.24), channel_id=1, source_target_pairs={{0,1},{1,0},{2,3},{3,2},{4,5},{5,4},{6,7},{7,6},{8,9},{9,8},{10,11... | collective-permute-start | bytes 811016 | tf_op jit(solution)/shard_map/ppermute | solution.py:440
  4.0 2.6 %collective-permute-start.7 = (f32[64,2048]{1,0:T(8,128)S(1)}, f32[64,2048]{1,0:T(8,128)S(1)}, u32[]{:S(2)}, u32[]{:S(2)}) collective-permute-start(f32[64,2048]{1,0:T(8,128)S(1)} %get-tuple-element.26), channel_id=1, source_target_pairs={{0,4},{4,8},{8,12},{12,16},{16,20},{20,24},{24,28},{28,0},{1,5},{5... | collective-permute-start | bytes 1572872 | tf_op jit(solution)/shard_map/ppermute | solution.py:445
  6.5 0.0 collective-permute-done
  6.6 1.6 %collective-permute-start.1 = (f32[192,256]{1,0:T(8,128)S(1)}, f32[192,256]{1,0:T(8,128)S(1)}, u32[]{:S(2)}, u32[]{:S(2)}) collective-permute-start(f32[192,256]{1,0:T(8,128)S(1)} %slice_add_fusion), channel_id=1, source_target_pairs={{0,2},{1,3},{2,0},{3,1},{4,6},{5,7},{6,4},{7,5},{8,10},{9,11},{10,... | collective-permute-start | bytes 589832 | tf_op jit(solution)/shard_map/ppermute | solution.py:440
  8.2 0.6 %collective-permute-start.3 = (f32[72,256]{1,0:T(8,128)S(1)}, f32[72,256]{1,0:T(8,128)S(1)}, u32[]{:S(2)}, u32[]{:S(2)}) collective-permute-start(f32[72,256]{1,0:T(8,128)S(1)} %slice_add_fusion.1), channel_id=1, source_target_pairs={{0,2},{1,3},{2,0},{3,1},{4,6},{5,7},{6,4},{7,5},{8,10},{9,11},{10,... | collective-permute-start | bytes 221192 | tf_op jit(solution)/shard_map/ppermute | solution.py:440
  8.7 6.4 %collective-permute-done.3 = f32[72,256]{1,0:T(8,128)S(1)} collective-permute-done((f32[72,256]{1,0:T(8,128)S(1)}, f32[72,256]{1,0:T(8,128)S(1)}, u32[]{:S(2)}, u32[]{:S(2)}) %collective-permute-start.3) | collective-permute-done | bytes 73760 | tf_op jit(solution)/shard_map/ppermute | solution.py:440
  15.2 1.6 %collective-permute-start.4 = (f32[64,256]{1,0:T(8,128)S(1)}, f32[64,256]{1,0:T(8,128)S(1)}, u32[]{:S(2)}, u32[]{:S(2)}) collective-permute-start(f32[64,256]{1,0:T(8,128)S(1)} %slice.22), channel_id=1, source_target_pairs={{0,4},{4,8},{8,12},{12,16},{16,20},{20,24},{24,28},{28,0},{1,5},{5... | collective-permute-start | bytes 196616 | tf_op jit(solution)/shard_map/ppermute | solution.py:445
  16.8 0.0 collective-permute-done.1
  16.8 0.1 collective-permute-start.2
  16.9 1.9 %shard_map.30 = (f32[192,2048]{1,0:T(8,128)S(1)}, f32[192,2048]{1,0:T(8,128)S(1)}) custom-call(f32[256,2048]{1,0:T(8,128)S(1)} %get-tuple-element.27.ret_ref), custom_call_target="tpu_custom_call" | custom-call | flops 15728640 | bytes 4718592 | tf_op jit(solution)/shard_map/pallas_call | solution.py:384
  18.8 0.6 %collective-permute-start.6 = (f32[72,256]{1,0:T(8,128)S(1)}, f32[72,256]{1,0:T(8,128)S(1)}, u32[]{:S(2)}, u32[]{:S(2)}) collective-permute-start(f32[72,256]{1,0:T(8,128)S(1)} %add.20.counts_ref.own_tail_ref.cown_ref), channel_id=1, source_target_pairs={{0,1},{1,0},{2,3},{3,2},{4,5},{5,4},{6,7},{7,6},{8,9},{9,8},{10,11... | collective-permute-start | bytes 221192 | tf_op jit(solution)/shard_map/ppermute | solution.py:440
  19.3 4.2 %collective-permute-done.4.prior_ref = f32[64,256]{1,0:T(8,128)S(1)} collective-permute-done((f32[64,256]{1,0:T(8,128)S(1)}, f32[64,256]{1,0:T(8,128)S(1)}, u32[]{:S(2)}, u32[]{:S(2)}) %collective-permute-start.4) | collective-permute-done | bytes 65568 | tf_op jit(solution)/shard_map/ppermute | solution.py:445
  23.5 0.0 collective-permute-start.5
  23.5 1.6 %shard_map.29.spread_ref = f32[640,2048]{1,0:T(8,128)S(1)} custom-call(f32[192,256]{1,0:T(8,128)S(1)} %add.18.here_ref.own_ref, f32[72,256]{1,0:T(8,128)S(1)} %add.20.counts_ref.own_tail_ref.cown_ref, bf16[512,2048]{1,0:T(8,128)(2,1)S(1)} %get-tuple-element.25.table_ref), custom_call_target="tpu_custom_call" | custom-call | flops 1342177280 | bytes 5242880 | tf_op jit(solution)/shard_map/pallas_call | solution.py:384
  25.2 0.7 %shard_map.28.spread_ref = f32[192,2048]{1,0:T(8,128)S(1)} custom-call(f32[72,128]{1,0:T(8,128)S(1)} %get-tuple-element.22.inv_ref, f32[192,256]{1,0:T(8,128)S(1)} %add.18.here_ref.own_ref, f32[64,256]{1,0:T(8,128)S(1)} %collective-permute-done.4.prior_ref, f32[72,256]{1,0:T(8,128)S(1)} %add.20.counts_ref.own_tail_ref.cown_ref, ...), custom_call_target="tpu_custom_call" | custom-call | flops 536870912 | bytes 1572864 | tf_op jit(solution)/shard_map/pallas_call | solution.py:384
  25.9 0.0 collective-permute-done.7.halo_ref
  25.9 1.0 %shard_map.32 = (f32[64,2048]{1,0:T(8,128)S(1)}, f32[64,2048]{1,0:T(8,128)S(1)}) custom-call(f32[72,128]{1,0:T(8,128)S(1)} %get-tuple-element.22.inv_ref, f32[64,2048]{1,0:T(8,128)S(1)} %collective-permute-done.7.halo_ref, f32[256,2048]{1,0:T(8,128)S(1)} %get-tuple-element.27.ret_ref), custom_call_target="tpu_custom_call" | custom-call | flops 5242880 | bytes 1572864 | tf_op jit(solution)/shard_map/pallas_call | solution.py:384
  26.9 0.0 collective-permute-done.6.other_tail_ref.counts_ref.cother_ref
  26.9 0.0 collective-permute-done.2.other_ref.here_ref
  26.9 2.6 %shard_map.31 = (f32[192,2048]{1,0:T(8,128)S(1)}, f32[64,2048]{1,0:T(8,128)S(1)}, f32[8,2048]{1,0:T(8,128)S(1)}) custom-call(f32[192,256]{1,0:T(8,128)S(1)} %collective-permute-done.2.other_ref.here_ref, f32[72,256]{1,0:T(8,128)S(1)} %collective-permute-done.6.other_tail_ref.counts_ref.cother_ref, f32[640,2048]{1,0:T(8,128)S(1)} %shard_map.29.spread_ref, ...), custom_call_target="tpu_custom_call" | custom-call | flops 2684354560 | bytes 6291456 | tf_op jit(solution)/shard_map/pallas_call | solution.py:384
  29.5 0.0 collective-permute-done.5.prior_ref
  29.6 1.7 %shard_map.33 = (f32[64,2048]{1,0:T(8,128)S(1)}, f32[32,512]{1,0:T(8,128)S(1)}) custom-call(f32[72,128]{1,0:T(8,128)S(1)} %get-tuple-element.22.inv_ref, s32[8,512]{1,0:T(8,128)S(1)} %get-tuple-element.21.flip_ref, f32[192,256]{1,0:T(8,128)S(1)} %collective-permute-done.2.other_ref.here_ref, f32[64,256]{1,0:T(8,128)S(1)} %collective-permute-done.5.prior_ref, ...), custom_call_target="tpu_custom_call" | custom-call | flops 1073741824 | bytes 1572864 | tf_op jit(solution)/shard_map/pallas_call | solution.py:384
  31.3 0.1 copy.3
  31.3 10.4 %all_to_all.11 = f32[32,1,512]{2,1,0:T(1,128)S(1)} all-to-all(f32[32,1,512]{2,1,0:T(1,128)S(1)} %copy.3), channel_id=1, replica_groups=mesh['tm'=8,'series'=4] {'tm','series'}, dimensions={0} | all-to-all | bytes 131072 | tf_op jit(solution)/shard_map/all_to_all | solution.py:536
  41.7 1.6 %shrink.1 = f32[256,2048]{1,0:T(8,128)} custom-call(s32[8,512]{1,0:T(8,128)S(1)} %get-tuple-element.21.flip_ref, f32[32,512]{1,0:T(8,128)S(1)} %bitcast.5, f32[72,256]{1,0:T(8,128)S(1)} %add.20.counts_ref.own_tail_ref.cown_ref, f32[72,256]{1,0:T(8,128)S(1)} %collective-permute-done.6.other_tail_ref.counts_ref.cother_ref, ...), custom_call_target="tpu_custom_call" | custom-call | flops 1048576 | bytes 4194304 | tf_op jit(solution)/shard_map/shrink/pallas_call | solution.py:422
  (8 shorter events, 0.1 us)
Async XLA Ops:
  0.0 0.7 %copy-start = (s32[2048]{0:T(1024)S(1)}, s32[2048]{0:T(1024)}, u32[]{:S(2)}) copy-start(s32[2048]{0:T(1024)} %param.3) | copy-start | bytes 24580
  3.4 3.1 %collective-permute-start = (f32[264,256]{1,0:T(8,128)S(1)}, f32[264,256]{1,0:T(8,128)S(1)}, u32[]{:S(2)}, u32[]{:S(2)}) collective-permute-start(f32[264,256]{1,0:T(8,128)S(1)} %get-tuple-element.24), channel_id=1, source_target_pairs={{0,1},{1,0},{2,3},{3,2},{4,5},{5,4},{6,7},{7,6},{8,9},{9,8},{10,11... | collective-permute-start | bytes 811016 | tf_op jit(solution)/shard_map/ppermute | solution.py:440
  4.0 21.9 %collective-permute-start.7 = (f32[64,2048]{1,0:T(8,128)S(1)}, f32[64,2048]{1,0:T(8,128)S(1)}, u32[]{:S(2)}, u32[]{:S(2)}) collective-permute-start(f32[64,2048]{1,0:T(8,128)S(1)} %get-tuple-element.26), channel_id=1, source_target_pairs={{0,4},{4,8},{8,12},{12,16},{16,20},{20,24},{24,28},{28,0},{1,5},{5... | collective-permute-start | bytes 1572872 | tf_op jit(solution)/shard_map/ppermute | solution.py:445
  6.6 10.2 %collective-permute-start.1 = (f32[192,256]{1,0:T(8,128)S(1)}, f32[192,256]{1,0:T(8,128)S(1)}, u32[]{:S(2)}, u32[]{:S(2)}) collective-permute-start(f32[192,256]{1,0:T(8,128)S(1)} %slice_add_fusion), channel_id=1, source_target_pairs={{0,2},{1,3},{2,0},{3,1},{4,6},{5,7},{6,4},{7,5},{8,10},{9,11},{10,... | collective-permute-start | bytes 589832 | tf_op jit(solution)/shard_map/ppermute | solution.py:440
  8.2 7.0 %collective-permute-start.3 = (f32[72,256]{1,0:T(8,128)S(1)}, f32[72,256]{1,0:T(8,128)S(1)}, u32[]{:S(2)}, u32[]{:S(2)}) collective-permute-start(f32[72,256]{1,0:T(8,128)S(1)} %slice_add_fusion.1), channel_id=1, source_target_pairs={{0,2},{1,3},{2,0},{3,1},{4,6},{5,7},{6,4},{7,5},{8,10},{9,11},{10,... | collective-permute-start | bytes 221192 | tf_op jit(solution)/shard_map/ppermute | solution.py:440
  15.2 8.3 %collective-permute-start.4 = (f32[64,256]{1,0:T(8,128)S(1)}, f32[64,256]{1,0:T(8,128)S(1)}, u32[]{:S(2)}, u32[]{:S(2)}) collective-permute-start(f32[64,256]{1,0:T(8,128)S(1)} %slice.22), channel_id=1, source_target_pairs={{0,4},{4,8},{8,12},{12,16},{16,20},{20,24},{24,28},{28,0},{1,5},{5... | collective-permute-start | bytes 196616 | tf_op jit(solution)/shard_map/ppermute | solution.py:445
  16.8 10.1 %collective-permute-start.2 = (f32[192,256]{1,0:T(8,128)S(1)}, f32[192,256]{1,0:T(8,128)S(1)}, u32[]{:S(2)}, u32[]{:S(2)}) collective-permute-start(f32[192,256]{1,0:T(8,128)S(1)} %add.18.here_ref.own_ref), channel_id=1, source_target_pairs={{0,1},{1,0},{2,3},{3,2},{4,5},{5,4},{6,7},{7,6},{8,9},{9,8},{10,11... | collective-permute-start | bytes 589832 | tf_op jit(solution)/shard_map/ppermute | solution.py:440
  18.8 8.1 %collective-permute-start.6 = (f32[72,256]{1,0:T(8,128)S(1)}, f32[72,256]{1,0:T(8,128)S(1)}, u32[]{:S(2)}, u32[]{:S(2)}) collective-permute-start(f32[72,256]{1,0:T(8,128)S(1)} %add.20.counts_ref.own_tail_ref.cown_ref), channel_id=1, source_target_pairs={{0,1},{1,0},{2,3},{3,2},{4,5},{5,4},{6,7},{7,6},{8,9},{9,8},{10,11... | collective-permute-start | bytes 221192 | tf_op jit(solution)/shard_map/ppermute | solution.py:440
  23.5 6.0 %collective-permute-start.5 = (f32[64,256]{1,0:T(8,128)S(1)}, f32[64,256]{1,0:T(8,128)S(1)}, u32[]{:S(2)}, u32[]{:S(2)}) collective-permute-start(f32[64,256]{1,0:T(8,128)S(1)} %collective-permute-done.4.prior_ref), channel_id=1, source_target_pairs={{0,1},{1,0},{2,3},{3,2},{4,5},{5,4},{6,7},{7,6},{8,9},{9,8},{10,11... | collective-permute-start | bytes 196616 | tf_op jit(solution)/shard_map/ppermute | solution.py:440
